TPU v7x, 256 devices: a 8x8x2 block of a 8x8x16 slice. The times are simulated.
256 devices in a mesh: groups: 2 (over z), ha: 128 (over y, x, core).
Axes of the slice: x: 8, y: 8, z: 2, core: 2. Of those that a mesh axis runs over, the one named last changes fastest.
The devices are a block of a 8x8x16 slice.
Arguments:
- video: bfloat16 [8, 512, 256, 128], P('groups', 'ha'), parts along dimension 0, may hold values from -90 to 90
- cache_video: bfloat16 [4, 512, 256, 128], P('groups', 'ha'), parts along dimension 0, may hold values from -90 to 90
- cache_hidden: bfloat16 [4, 256, 128, 256], P('groups', 'ha'), parts along dimension 0, may hold values from -0.25 to 2
- kernel_down: bfloat16 [3, 3, 3, 128, 256], replicated, may hold values from -0.05103104 to 0.05103104
- gain_down: float32 [256], replicated, may hold values from 0.1 to 1.9
- shift_down: float32 [256], replicated, may hold values from -3 to 3
- kernel_mix: bfloat16 [3, 3, 3, 256, 256], replicated, may hold values from -0.03608439 to 0.03608439
- gain_mix: float32 [256], replicated, may hold values from 0.1 to 1.9
- shift_mix: float32 [256], replicated, may hold values from -3 to 3
Outputs:
- encoded: bfloat16 [8, 256, 128, 256], P('groups', 'ha'), parts along dimension 0
- next_cache: bfloat16 [4, 256, 128, 256], P('groups', 'ha'), parts along dimension 0
There are 2 independent parts, one for each index of `groups`. A program takes and returns all parts, laid end to end along the dimension named above; an argument that names none is the same for every part. Nothing has to cross between parts.
All inputs are finite; a program needn't handle non-finite values.
Results may differ from a plain program's by a relative error of at most 0.0032.
Values may be sent and summed in bfloat16 or wider, within the bound.
No kernel may reach another device: no remote copies, remote signals or barrier semaphores. Data moves between devices by JAX's collectives and lax.ppermute only.
A program may use at most 64 MiB of HBM per device.

v0:
```python
import jax
import jax.numpy as jnp
from jax import lax
from jax.sharding import Mesh
from jax.sharding import PartitionSpec as P

GROUPS = 32
HA = ("ha_0", "ha_1", "ha_2")


def by_axis(shard, axes):
    for axis in axes:
        shard = lax.psum(shard, axis)
    return shard


def shifted(shard, axis, by):
    length = lax.axis_size(axis)
    pairs = [(i, i + by) for i in range(length) if 0 <= i + by < length]
    return lax.ppermute(shard, axis, pairs)


def extended_2(cells, sides, width):
    for axis, dim in sides:
        count = lax.axis_size(axis)
        ends = count - 1
        head = lax.slice_in_dim(cells, 0, width, axis=dim)
        tail = lax.slice_in_dim(cells, cells.shape[dim] - width, cells.shape[dim], axis=dim)
        cells = jnp.concatenate(
            [
                lax.ppermute(tail, axis, [(i, (i + 1) % count) for i in range(ends)]),
                cells,
                lax.ppermute(head, axis, [((i + 1) % count, i) for i in range(ends)]),
            ],
            axis=dim,
        )
    return cells


def convolve(stack, kernel, strides):
    result = lax.conv_general_dilated(
        stack[None],
        kernel,
        strides,
        "VALID",
        dimension_numbers=("NDHWC", "DHWIO", "NDHWC"),
        preferred_element_type=jnp.float32,
    )
    return result[0]


def group_totals(values, per_group):
    return jnp.sum(values, axis=(0, 1, 2)).reshape(-1, per_group).sum(1)


def normalize(values, scales, offsets):
    per_group = values.shape[-1] // GROUPS
    members = values.shape[0] * values.shape[1] * lax.axis_size(HA) * values.shape[2] * per_group
    totals, squares = (
        by_axis(group_totals(values, per_group), HA),
        by_axis(group_totals(values * values, per_group), HA),
    )
    center_group = totals / members
    spread_group = squares / members - center_group * center_group
    deviate = values - jnp.repeat(center_group, per_group)
    normed = deviate * jnp.repeat(lax.rsqrt(spread_group + 1e-06), per_group) * scales + offsets
    return jax.nn.silu(normed).astype(jnp.bfloat16)


def local(
    video,
    cache_video,
    cache_hidden,
    kernel_down,
    gain_down,
    shift_down,
    kernel_mix,
    gain_mix,
    shift_mix,
):
    stacked = jnp.concatenate([cache_video, video], axis=0)
    lower_rim = shifted(stacked[:, :1], HA, -1)
    extended = jnp.concatenate([stacked, lower_rim], axis=1)
    extended = jnp.pad(extended, ((0, 0), (0, 0), (0, 1), (0, 0)))
    first = convolve(extended, kernel_down, (1, 2, 2))
    hidden = normalize(first, gain_down, shift_down)
    padded = extended_2(jnp.concatenate([cache_hidden, hidden], axis=0), ((HA, 1),), 1)
    padded = jnp.pad(padded, ((0, 0), (0, 0), (1, 1), (0, 0)))
    second = convolve(padded, kernel_mix, (1, 1, 1))
    encoded = normalize(second, gain_mix, shift_mix)
    return (encoded, hidden[hidden.shape[0] - 2 :])


def solution(mesh):
    split = Mesh(
        mesh.devices.reshape(mesh.shape["groups"], 8, 8, 2), ("groups", "ha_0", "ha_1", "ha_2")
    )
    in_specs = (
        P("groups", HA, None, None),
        P("groups", HA, None, None),
        P("groups", HA, None, None),
        P(),
        P(),
        P(),
        P(),
        P(),
        P(),
    )
    out_specs = (P("groups", HA, None, None), P("groups", HA, None, None))
    return jax.shard_map(local, mesh=split, in_specs=in_specs, out_specs=out_specs, check_vma=False)
```

profile of v0, /device:TPU:513, one launch (start us, length us, event | category | flops | bytes accessed | tf_op | source)
XLA Modules:
  0.0 149.8 jit_solution(11974664359289612967)
XLA Ops:
  0.6 1.2 constant_dynamic-update-slice_fusion.1
  1.9 1.4 constant_dynamic-update-slice_fusion
  3.3 22.4 %collective-permute-start = (bf16[6,1,256,128]{3,2,1,0:T(8,128)(2,1)S(1)}, bf16[6,1,256,128]{3,2,1,0:T(8,128)(2,1)S(1)}, u32[]{:S(2)}, u32[]{:S(2)}) collective-permute-start(bf16[6,1,256,128]{3,2,1,0:T(8,128)(2,1)S(1)} %slice.20), channel_id=1, source_target_pairs={{1,0},{2,1},{3,2},{4,3},{5,4},{6,5},{7,6},{8,7},{9,8},{10,9},{11,1... | collective-permute-start | bytes 1179656 | tf_op jit(solution)/shard_map/ppermute | solution.py:20
  25.7 1.3 collective-permute-done
  27.2 1.5 pad.10
  28.6 4.5 %reshape.30 = bf16[6,5,1,8,34,128]{5,4,3,1,0,2:T(8,128)(2,1)} reshape(bf16[6,5,1,272,128]{4,3,1,0,2:T(8,128)(2,1)} %pad.10) | data formatting | bytes 4177920 | tf_op jit(solution)/shard_map/conv_general_dilated | solution.py:41
  33.1 2.1 %copy.34 = bf16[6,5,1,8,34,128]{5,3,4,1,0,2:T(8,128)(2,1)S(1)} copy(bf16[6,5,1,8,34,128]{5,4,3,1,0,2:T(8,128)(2,1)} %reshape.30) | data formatting | bytes 4177920 | tf_op jit(solution)/shard_map/conv_general_dilated | solution.py:41
  35.4 3.8 %select_reduce_fusion.1 = (f32[256]{0:T(256)}, f32[4,2,8,17,256]{4,2,3,1,0:T(8,128)}) fusion(pred[8,17]{0,1:T(8,128)(4,1)S(1)} %copy-done.5, bf16[3,3,3,128,256]{4,3,2,1,0:T(8,128)(2,1)S(1)} %copy-done.4, bf16[6,5,1,7,2,128]{5,3,4,1,0,2:T(8,128)(2,1)S(1)} %slice.21, bf16[6,5,1,8,34,128]{5,3,4,1,0,2:T(8,128)(2,1)S(1)} %copy.34), kind=kOutput, calls=%fused_computation.33 | convolution fusion | flops 1932656384 | bytes 5081224 | tf_op jit(solution)/shard_map/conv_general_dilated | solution.py:41
  39.1 0.8 reshape.24
  39.9 1.8 %copy.35 = f32[4,2,8,17,256]{4,1,3,2,0:T(2,128)S(1)} copy(f32[4,2,8,17,256]{4,2,3,1,0:T(8,128)} %get-tuple-element.25) | data formatting | bytes 2228224 | tf_op jit(solution)/shard_map/conv_general_dilated | solution.py:41
  42.1 1.0 copy-done.1
  43.8 1.4 reshape.25
  45.8 0.8 reduce_sum.75
  46.6 10.9 %all-reduce.5 = (f32[32]{0:T(128)S(1)}, f32[32]{0:T(128)S(1)}) all-reduce(f32[32]{0:T(128)S(1)} %reduce_sum.75, f32[32]{0:T(128)} %reduce_sum.73), channel_id=1, replica_groups=mesh['groups'=2,'ha_0'=8,'ha_1'=8,'ha_2'=2] {'ha_0'}, use_global_device_ids=true, to_apply=%region_7.8 | all-reduce | flops 64 | bytes 512 | tf_op jit(solution)/shard_map/psum | solution.py:13
  57.5 12.1 %all-reduce.3 = (f32[32]{0:T(128)S(1)}, f32[32]{0:T(128)}) all-reduce(f32[32]{0:T(128)S(1)} %get-tuple-element.12, f32[32]{0:T(128)S(1)} %get-tuple-element.13), channel_id=1, replica_groups=mesh['groups'=2,'ha_0'=8,'ha_1'=8,'ha_2'=2] {'ha_1'}, use_global_device_ids=true, to_apply=%region_8.9 | all-reduce | flops 64 | bytes 512 | tf_op jit(solution)/shard_map/psum | solution.py:13
  69.6 9.6 %all-reduce.7 = (f32[32]{0:T(128)S(1)}, f32[32]{0:T(128)S(1)}) all-reduce(f32[32]{0:T(128)S(1)} %get-tuple-element.8, f32[32]{0:T(128)} %get-tuple-element.9), channel_id=1, replica_groups=mesh['groups'=2,'ha_0'=8,'ha_1'=8,'ha_2'=2] {'ha_2'}, use_global_device_ids=true, to_apply=%region_9.10 | all-reduce | flops 64 | bytes 512 | tf_op jit(solution)/shard_map/psum | solution.py:13
  81.8 1.6 %multiply_convert_fusion.1 = bf16[4,2,128,256]{3,2,1,0:T(8,128)(2,1)S(1)} fusion(f32[4,2,1,128,256]{4,1,3,0,2:T(2,128)} %copy-done.1, f32[256]{0:T(256)} %param.14, f32[256]{0:T(256)} %param.13, f32[256]{0:T(256)} %mul.57, f32[256]{0:T(256)} %sub.26), kind=kLoop, calls=%fused_computation.39 | loop fusion | flops 2359296 | bytes 1576960 | tf_op jit(solution)/shard_map/convert_element_type | solution.py:67
  83.5 1.0 fusion.33
  84.5 2.9 %collective-permute-start.1 = (bf16[6,1,128,256]{3,2,1,0:T(8,128)(2,1)S(1)}, bf16[6,1,128,256]{3,2,1,0:T(8,128)(2,1)S(1)}, u32[]{:S(2)}, u32[]{:S(2)}) collective-permute-start(bf16[6,1,128,256]{3,2,1,0:T(8,128)(2,1)S(1)} %get-tuple-element.18), channel_id=1, source_target_pairs={{0,1},{1,2},{2,3},{3,4},{4,5},{5,6},{6,7},{7,8},{8,9},{9,10},{10,1... | collective-permute-start | bytes 1179656 | tf_op jit(solution)/shard_map/ppermute | solution.py:31
  87.4 2.1 %collective-permute-start.2 = (bf16[6,1,128,256]{3,2,1,0:T(8,128)(2,1)S(1)}, bf16[6,1,128,256]{3,2,1,0:T(8,128)(2,1)S(1)}, u32[]{:S(2)}, u32[]{:S(2)}) collective-permute-start(bf16[6,1,128,256]{3,2,1,0:T(8,128)(2,1)S(1)} %get-tuple-element.19), channel_id=1, source_target_pairs={{1,0},{2,1},{3,2},{4,3},{5,4},{6,5},{7,6},{8,7},{9,8},{10,9},{11,1... | collective-permute-start | bytes 1179656 | tf_op jit(solution)/shard_map/ppermute | solution.py:33
  90.3 1.8 %collective-permute-done.1 = bf16[6,1,128,256]{3,2,1,0:T(8,128)(2,1)S(1)} collective-permute-done((bf16[6,1,128,256]{3,2,1,0:T(8,128)(2,1)S(1)}, bf16[6,1,128,256]{3,2,1,0:T(8,128)(2,1)S(1)}, u32[]{:S(2)}, u32[]{:S(2)}) %collective-permute-start.1) | collective-permute-done | bytes 393248 | tf_op jit(solution)/shard_map/ppermute | solution.py:31
  92.1 4.4 %collective-permute-done.2 = bf16[6,1,128,256]{3,2,1,0:T(8,128)(2,1)S(1)} collective-permute-done((bf16[6,1,128,256]{3,2,1,0:T(8,128)(2,1)S(1)}, bf16[6,1,128,256]{3,2,1,0:T(8,128)(2,1)S(1)}, u32[]{:S(2)}, u32[]{:S(2)}) %collective-permute-start.2) | collective-permute-done | bytes 393248 | tf_op jit(solution)/shard_map/ppermute | solution.py:33
  96.6 0.9 fusion.21
  99.4 5.6 %select_reduce_fusion = (f32[256]{0:T(256)}, f32[4,2,8,17,256]{4,2,3,1,0:T(8,128)}) fusion(pred[8,17]{0,1:T(8,128)(4,1)S(1)} %copy-done.6, bf16[3,3,3,256,256]{4,3,2,1,0:T(8,128)(2,1)S(1)} %copy-done, bf16[6,4,1,7,2,256]{5,3,4,1,0,2:T(8,128)(2,1)S(1)} %slice.25, bf16[6,4,1,8,17,256]{5,3,4,1,0,2:T(8,128)(2,1)S(1)} %copy.39), kind=kOutput, calls=%fused_computation.32 | convolution fusion | flops 3856809728 | bytes 6497416 | tf_op jit(solution)/shard_map/conv_general_dilated | solution.py:41
  105.0 0.8 reshape.26
  106.4 1.8 %copy.40 = f32[4,2,8,17,256]{4,1,3,2,0:T(2,128)S(1)} copy(f32[4,2,8,17,256]{4,2,3,1,0:T(8,128)} %get-tuple-element.27) | data formatting | bytes 2228224 | tf_op jit(solution)/shard_map/conv_general_dilated | solution.py:41
  108.6 1.0 copy-done.2
  110.3 0.8 reshape.27
  111.7 12.5 %all-reduce.4 = (f32[32]{0:T(128)S(1)}, f32[32]{0:T(128)S(1)}) all-reduce(f32[32]{0:T(128)} %reduce_sum.79, f32[32]{0:T(128)} %reduce_sum.77), channel_id=1, replica_groups=mesh['groups'=2,'ha_0'=8,'ha_1'=8,'ha_2'=2] {'ha_0'}, use_global_device_ids=true, to_apply=%region_17.18 | all-reduce | flops 64 | bytes 512 | tf_op jit(solution)/shard_map/psum | solution.py:13
  124.2 13.5 %all-reduce.2 = (f32[32]{0:T(128)S(1)}, f32[32]{0:T(128)S(1)}) all-reduce(f32[32]{0:T(128)S(1)} %get-tuple-element.10, f32[32]{0:T(128)S(1)} %get-tuple-element.11), channel_id=1, replica_groups=mesh['groups'=2,'ha_0'=8,'ha_1'=8,'ha_2'=2] {'ha_1'}, use_global_device_ids=true, to_apply=%region_18.19 | all-reduce | flops 64 | bytes 512 | tf_op jit(solution)/shard_map/psum | solution.py:13
  137.7 7.0 %all-reduce.6 = (f32[32]{0:T(128)S(1)}, f32[32]{0:T(128)S(1)}) all-reduce(f32[32]{0:T(128)S(1)} %get-tuple-element.6, f32[32]{0:T(128)S(1)} %get-tuple-element.7), channel_id=1, replica_groups=mesh['groups'=2,'ha_0'=8,'ha_1'=8,'ha_2'=2] {'ha_2'}, use_global_device_ids=true, to_apply=%region_19.20 | all-reduce | flops 64 | bytes 512 | tf_op jit(solution)/shard_map/psum | solution.py:13
  147.4 2.4 %multiply_convert_fusion = bf16[4,2,128,256]{3,2,1,0:T(8,128)(2,1)} fusion(f32[4,2,1,128,256]{4,1,3,0,2:T(2,128)} %copy-done.2, f32[256]{0:T(256)} %param.17, f32[256]{0:T(256)} %param.16, f32[256]{0:T(256)} %mul.65, f32[256]{0:T(256)} %sub.30), kind=kLoop, calls=%fused_computation.37 | loop fusion | flops 2359296 | bytes 1576960 | tf_op jit(solution)/shard_map/convert_element_type | solution.py:67
  (37 shorter events, 12.3 us)
Async XLA Ops:
  0.6 98.4 %copy-start = (bf16[3,3,3,256,256]{4,3,2,1,0:T(8,128)(2,1)S(1)}, bf16[3,3,3,256,256]{4,3,2,1,0:T(8,128)(2,1)}, u32[]{:S(2)}) copy-start(bf16[3,3,3,256,256]{4,3,2,1,0:T(8,128)(2,1)} %param.15) | copy-start | bytes 10616836
  3.3 23.7 %collective-permute-start = (bf16[6,1,256,128]{3,2,1,0:T(8,128)(2,1)S(1)}, bf16[6,1,256,128]{3,2,1,0:T(8,128)(2,1)S(1)}, u32[]{:S(2)}, u32[]{:S(2)}) collective-permute-start(bf16[6,1,256,128]{3,2,1,0:T(8,128)(2,1)S(1)} %slice.20), channel_id=1, source_target_pairs={{1,0},{2,1},{3,2},{4,3},{5,4},{6,5},{7,6},{8,7},{9,8},{10,9},{11,1... | collective-permute-start | bytes 1179656 | tf_op jit(solution)/shard_map/ppermute | solution.py:20
  33.1 2.2 %copy-start.4 = (bf16[3,3,3,128,256]{4,3,2,1,0:T(8,128)(2,1)S(1)}, bf16[3,3,3,128,256]{4,3,2,1,0:T(8,128)(2,1)}, u32[]{:S(2)}) copy-start(bf16[3,3,3,128,256]{4,3,2,1,0:T(8,128)(2,1)} %param.12) | copy-start | bytes 5308420
  33.1 2.2 %copy-start.5 = (pred[8,17]{0,1:T(8,128)(4,1)S(1)}, pred[8,17]{0,1:T(8,128)(4,1)}, u32[]{:S(2)}) copy-start(pred[8,17]{0,1:T(8,128)(4,1)} %constant.34) | copy-start | bytes 412
  42.1 1.0 copy-start.1
  81.8 14.7 %copy-start.3 = (bf16[2,2,128,256]{3,2,1,0:T(8,128)(2,1)S(1)}, bf16[2,2,128,256]{3,2,1,0:T(8,128)(2,1)}, u32[]{:S(2)}) copy-start(bf16[2,2,128,256]{3,2,1,0:T(8,128)(2,1)} %param.11) | copy-start | bytes 786436
  84.5 7.6 %collective-permute-start.1 = (bf16[6,1,128,256]{3,2,1,0:T(8,128)(2,1)S(1)}, bf16[6,1,128,256]{3,2,1,0:T(8,128)(2,1)S(1)}, u32[]{:S(2)}, u32[]{:S(2)}) collective-permute-start(bf16[6,1,128,256]{3,2,1,0:T(8,128)(2,1)S(1)} %get-tuple-element.18), channel_id=1, source_target_pairs={{0,1},{1,2},{2,3},{3,4},{4,5},{5,6},{6,7},{7,8},{8,9},{9,10},{10,1... | collective-permute-start | bytes 1179656 | tf_op jit(solution)/shard_map/ppermute | solution.py:31
  87.4 9.1 %collective-permute-start.2 = (bf16[6,1,128,256]{3,2,1,0:T(8,128)(2,1)S(1)}, bf16[6,1,128,256]{3,2,1,0:T(8,128)(2,1)S(1)}, u32[]{:S(2)}, u32[]{:S(2)}) collective-permute-start(bf16[6,1,128,256]{3,2,1,0:T(8,128)(2,1)S(1)} %get-tuple-element.19), channel_id=1, source_target_pairs={{1,0},{2,1},{3,2},{4,3},{5,4},{6,5},{7,6},{8,7},{9,8},{10,9},{11,1... | collective-permute-start | bytes 1179656 | tf_op jit(solution)/shard_map/ppermute | solution.py:33
  98.7 0.7 copy-start.6
  108.6 1.0 copy-start.2
where the time goes:
time: 150 us
  blocking collectives  65.6 us (44%)
  local copies, waits for them, and re-layouts  27.7 us (18%)
  starting transfers between devices  27.4 us (18%)
  other arithmetic  11.3 us (8%)
  matrix products  9.38 us (6%)
  waiting for transfers between devices  7.59 us (5%)
    psum x6, blocking collectives, by_axis(): shard = lax.psum(shard, axis)  65.6 us
    ppermute x1, starting transfers between devices, shifted(): return lax.ppermute(shard, axis, pairs)  22.4 us
    conv_general_dilated x9, local copies, waits for them, and re-layouts, convolve(): lax.conv_general_dilated(stack[None], kernel, strides, 'VALID', dimension...  11.3 us
    conv_general_dilated x2, matrix products, convolve(): lax.conv_general_dilated(stack[None], kernel, strides, 'VALID', dimension...  9.38 us
    ppermute x1, waiting for transfers between devices, extended_2(): lax.ppermute(head, axis, [((i + 1) % count, i) for i in range(ends)])  4.43 us
    unnamed x16, local copies, waits for them, and re-layouts  4.29 us
    reduce_sum x6, other arithmetic, group_totals(): return jnp.sum(values, axis=(0, 1, 2)).reshape(-1, per_group).sum(1)  4.14 us
    convert_element_type x2, other arithmetic, normalize(): return jax.nn.silu(normed).astype(jnp.bfloat16)  4.01 us
  transfers between devices with their start and end apart: 3, of which 3 were waited for; matrix products, arithmetic and copies ran while one was open for 0% of the time, Pallas kernels for 0%

commit v1 on v0

v1 whole, which is shorter than its diff:
```python
import jax
import jax.numpy as jnp
from jax import lax
from jax.experimental import pallas as pl
from jax.experimental.pallas import tpu as pltpu
from jax.sharding import Mesh
from jax.sharding import PartitionSpec as P

GROUPS = 32
LANES = 128
EPS = 1e-6
HA = ("ha_0", "ha_1", "ha_2")
F32 = jnp.float32
BF16 = jnp.bfloat16
VMEM = pl.BlockSpec(memory_space=pltpu.VMEM)


def whole(shape, dtype):
    return jax.ShapeDtypeStruct(shape, dtype)


def group_onehot(channels, transpose):
    per_group = channels // GROUPS
    shape = (LANES, channels) if transpose else (channels, LANES)
    channel = lax.broadcasted_iota(jnp.int32, shape, 1 if transpose else 0)
    group = lax.broadcasted_iota(jnp.int32, shape, 0 if transpose else 1)
    return jnp.where(channel // per_group == group, 1.0, 0.0).astype(F32)


def exact_dot(a, b):
    return jnp.dot(a, b, precision=lax.Precision.HIGHEST, preferred_element_type=F32)


def local_moments(blocks, members):
    channels = blocks[0].shape[-1]
    onehot = group_onehot(channels, False)
    spread = group_onehot(channels, True)
    total = sum(jnp.sum(b, axis=0, keepdims=True) for b in blocks)
    sums = exact_dot(total, onehot)
    center = exact_dot(sums * (1.0 / members), spread)
    squares = sum(jnp.sum((b - center) * (b - center), axis=0, keepdims=True) for b in blocks)
    squares = exact_dot(squares, onehot)
    return sums + pltpu.roll(squares, GROUPS, 1)


def affine(stats, members, scales, offsets):
    count = stats.shape[0]
    sums = jnp.sum(stats, axis=0, keepdims=True)
    center = sums * (1.0 / (members * count))
    off = stats - members * center
    between = jnp.sum(off * off, axis=0, keepdims=True) * (1.0 / members)
    squares = pltpu.roll(sums, LANES - GROUPS, 1) + between
    spread = squares * (1.0 / (members * count))
    group = lax.broadcasted_iota(jnp.int32, spread.shape, 1) < GROUPS
    rate = jnp.where(group, lax.rsqrt(spread + EPS), 0.0)
    center = jnp.where(group, center, 0.0)
    expand = group_onehot(scales.shape[-1], True)
    return exact_dot(center, expand), exact_dot(rate, expand) * scales, offsets


def silu_norm(values, center, factor, offset):
    normed = (values - center) * factor + offset
    return normed / (1.0 + jnp.exp(-normed))


def down_kernel(cache_ref, video_ref, rim_ref, kernel_ref, first_ref, stats_ref, pairs_ref):
    frames, rows, width, c_in = video_ref.shape
    cached = cache_ref.shape[0]
    half = width // 2
    for f in range(cached + frames):
        for r in range(rows + 1):
            if r == rows:
                source = rim_ref.at[f, 0]
            elif f < cached:
                source = cache_ref.at[f, r]
            else:
                source = video_ref.at[f - cached, r]
            pairs_ref[f, r, :, :c_in] = source[pl.ds(0, half, stride=2), :]
            pairs_ref[f, r, :, c_in:] = source[pl.ds(1, half, stride=2), :]
    c_out = kernel_ref.shape[-1]
    last = lax.broadcasted_iota(jnp.int32, (half, c_out), 0) == half - 1
    both = jnp.concatenate([kernel_ref[a, b, c] for a in range(3) for b in range(3) for c in range(2)], axis=0)
    ahead = jnp.concatenate([kernel_ref[a, b, 2] for a in range(3) for b in range(3)], axis=0)
    blocks = []
    for i in range(rows // 2):
        taps = [
            pairs_ref[a : a + frames, 2 * i + b].reshape(frames * half, 2 * c_in)
            for a in range(3)
            for b in range(3)
        ]
        here = jnp.dot(jnp.concatenate(taps, axis=1), both, preferred_element_type=F32)
        next_ = jnp.dot(
            jnp.concatenate([t[:, :c_in] for t in taps], axis=1), ahead, preferred_element_type=F32
        )
        for t in range(frames):
            rolled = pltpu.roll(next_[t * half : (t + 1) * half], half - 1, 0)
            block = here[t * half : (t + 1) * half] + jnp.where(last, 0.0, rolled)
            first_ref[t, i] = block
    blocks = [first_ref[t, i] for t in range(frames) for i in range(rows // 2)]
    members = len(blocks) * half * (c_out // GROUPS)
    stats_ref[...] = local_moments(blocks, members)


def mix_kernel(
    first_ref, above_ref, below_ref, hidden_in_ref, cached_above_ref, cached_below_ref,
    stats_in_ref, gain_ref, shift_ref, edge_ref, kernel_ref,
    second_ref, next_ref, stats_ref, rows_ref,
):
    frames, rows, width, channels = first_ref.shape
    cached = hidden_in_ref.shape[0]
    members = frames * rows * width * (channels // GROUPS)
    center, factor, offset = affine(stats_in_ref[...], members, gain_ref[...], shift_ref[...])
    top = edge_ref[0, 0] > 0
    bottom = edge_ref[0, 1] > 0
    for f in range(cached):
        rows_ref[f, 0] = cached_above_ref[f, 0]
        rows_ref[f, rows + 1] = cached_below_ref[f, 0]
        for i in range(rows):
            rows_ref[f, 1 + i] = hidden_in_ref[f, i]
    for t in range(frames):
        for i in range(rows):
            hidden = silu_norm(first_ref[t, i], center, factor, offset).astype(BF16)
            rows_ref[cached + t, 1 + i] = hidden
            if t >= frames - 2:
                next_ref[t - (frames - 2), i] = hidden
        above = silu_norm(above_ref[t, 0], center, factor, offset)
        rows_ref[cached + t, 0] = jnp.where(top, 0.0, above).astype(BF16)
        below = silu_norm(below_ref[t, 0], center, factor, offset)
        rows_ref[cached + t, rows + 1] = jnp.where(bottom, 0.0, below).astype(BF16)
    weights = [
        jnp.concatenate([kernel_ref[a, b, c] for a in range(3) for b in range(3)], axis=0)
        for c in range(3)
    ]
    place = lax.broadcasted_iota(jnp.int32, (width, channels), 0)
    for i in range(rows):
        taps = jnp.concatenate(
            [
                rows_ref[a : a + frames, i + b].reshape(frames * width, channels)
                for a in range(3)
                for b in range(3)
            ],
            axis=1,
        )
        left, here, right = (jnp.dot(taps, w, preferred_element_type=F32) for w in weights)
        for t in range(frames):
            span = slice(t * width, (t + 1) * width)
            block = here[span] + jnp.where(place == 0, 0.0, pltpu.roll(left[span], 1, 0))
            block = block + jnp.where(place == width - 1, 0.0, pltpu.roll(right[span], width - 1, 0))
            second_ref[t, i] = block
    blocks = [second_ref[t, i] for t in range(frames) for i in range(rows)]
    stats_ref[...] = local_moments(blocks, members)


def final_kernel(second_ref, stats_ref, gain_ref, shift_ref, out_ref):
    frames, rows, width, channels = second_ref.shape
    members = frames * rows * width * (channels // GROUPS)
    center, factor, offset = affine(stats_ref[...], members, gain_ref[...], shift_ref[...])
    for t in range(frames):
        for i in range(rows):
            out_ref[t, i] = silu_norm(second_ref[t, i], center, factor, offset).astype(BF16)


def chain_pairs(by):
    count = lax.axis_size(HA)
    return [(i, i + by) for i in range(count) if 0 <= i + by < count]


def everyone(stats):
    count = lax.axis_size(HA)
    spread = jnp.broadcast_to(stats[None], (count, *stats.shape))
    return lax.all_to_all(spread, HA, 0, 0).reshape(count, stats.shape[-1])


def local(video, cache_video, cache_hidden, kernel_down, gain_down, shift_down, kernel_mix, gain_mix, shift_mix):
    frames, rows, width, _ = video.shape
    c_out = kernel_down.shape[-1]
    half = width // 2
    down = chain_pairs(1)
    up = chain_pairs(-1)
    rim = lax.ppermute(jnp.concatenate([cache_video[:, :1], video[:, :1]], axis=0), HA, up)
    cached_above = lax.ppermute(cache_hidden[:, -1:], HA, down)
    cached_below = lax.ppermute(cache_hidden[:, :1], HA, up)
    first, stats = pl.pallas_call(
        down_kernel,
        name="down",
        out_shape=(whole((frames, rows // 2, half, c_out), F32), whole((1, LANES), F32)),
        in_specs=[VMEM] * 4,
        out_specs=(VMEM, VMEM),
        scratch_shapes=[pltpu.VMEM((frames + 2, rows + 1, half, 2 * video.shape[-1]), BF16)],
    )(cache_video, video, rim, kernel_down)
    above = lax.ppermute(first[:, -1:], HA, down)
    below = lax.ppermute(first[:, :1], HA, up)
    stats = everyone(stats)
    place = lax.axis_index(HA)
    edge = jnp.stack([place == 0, place == lax.axis_size(HA) - 1]).astype(jnp.int32)[None]
    second, next_cache, stats = pl.pallas_call(
        mix_kernel,
        name="mix",
        out_shape=(
            whole(first.shape, F32),
            whole((2, *first.shape[1:]), BF16),
            whole((1, LANES), F32),
        ),
        in_specs=[VMEM] * 9 + [pl.BlockSpec(memory_space=pltpu.SMEM), VMEM],
        out_specs=(VMEM, VMEM, VMEM),
        scratch_shapes=[pltpu.VMEM((frames + 2, rows // 2 + 2, half, c_out), BF16)],
    )(
        first, above, below, cache_hidden, cached_above, cached_below,
        stats, gain_down[None], shift_down[None], edge, kernel_mix,
    )
    stats = everyone(stats)
    encoded = pl.pallas_call(
        final_kernel,
        name="final",
        out_shape=whole(first.shape, BF16),
        in_specs=[VMEM] * 4,
        out_specs=VMEM,
    )(second, stats, gain_mix[None], shift_mix[None])
    return (encoded, next_cache)


def solution(mesh):
    split = Mesh(
        mesh.devices.reshape(mesh.shape["groups"], 8, 8, 2), ("groups", "ha_0", "ha_1", "ha_2")
    )
    strips = P("groups", HA, None, None)
    return jax.shard_map(
        local,
        mesh=split,
        in_specs=(strips, strips, strips, P(), P(), P(), P(), P(), P()),
        out_specs=(strips, strips),
        check_vma=False,
    )
```

time: 150 us -> 103 us (0.69)
  blocking collectives: 65.6 us -> 20.1 us
  local copies, waits for them, and re-layouts: 27.7 us -> 6.93 us
  starting transfers between devices: 27.4 us -> 45.5 us
  Pallas kernels: 0 us -> 16.5 us
  other arithmetic: 11.3 us -> 0.69 us
  matrix products: 9.38 us -> 0 us
  waiting for transfers between devices: 7.59 us -> 12.6 us
    psum x6 -> x0, blocking collectives: 65.6 us -> none  [by_axis(): shard = lax.psum(shard, axis)]
    all_to_all x0 -> x1, blocking collectives: none -> 20.1 us  [everyone(): return lax.all_to_all(spread, HA, 0, 0).reshape(count, stats.shape[-1])]
    pallas_call x0 -> x3, Pallas kernels: none -> 16.5 us  [the longest x1 8.25 us: local(): pl.pallas_call(mix_kernel, name='mix', out_shape=(whole(first.shape, F32)...]
    all_to_all x0 -> x1, starting transfers between devices: none -> 11.9 us  [everyone(): return lax.all_to_all(spread, HA, 0, 0).reshape(count, stats.shape[-1])]
    conv_general_dilated x9 -> x0, local copies, waits for them, and re-layouts: 11.3 us -> none  [convolve(): lax.conv_general_dilated(stack[None], kernel, strides, 'VALID', dimension...]
    all_to_all x0 -> x1, waiting for transfers between devices: none -> 11.2 us  [everyone(): return lax.all_to_all(spread, HA, 0, 0).reshape(count, stats.shape[-1])]
    conv_general_dilated x2 -> x0, matrix products: 9.38 us -> none  [convolve(): lax.conv_general_dilated(stack[None], kernel, strides, 'VALID', dimension...]
    ppermute x3 -> x5, waiting for transfers between devices: 7.59 us -> 1.34 us  [the longest x1 1.33 us: local(): lax.ppermute(jnp.concatenate([cache_video[:, :1], video[:, :1]], axis=0),...]
  transfers between devices with their start and end apart: 3 -> 6, of which waited for: 3 -> 2; matrix products, arithmetic and copies ran while one was open for 0% -> 2% of each run, Pallas kernels for 0% -> 0%
where the time goes in v1:
time: 103 us
  starting transfers between devices  45.5 us (44%)
  blocking collectives  20.1 us (20%)
  Pallas kernels  16.5 us (16%)
  waiting for transfers between devices  12.6 us (12%)
  local copies, waits for them, and re-layouts  6.93 us (7%)
    ppermute x1, starting transfers between devices, local(): lax.ppermute(jnp.concatenate([cache_video[:, :1], video[:, :1]], axis=0),...  22.4 us
    all_to_all x1, blocking collectives, everyone(): return lax.all_to_all(spread, HA, 0, 0).reshape(count, stats.shape[-1])  20.1 us
    all_to_all x1, starting transfers between devices, everyone(): return lax.all_to_all(spread, HA, 0, 0).reshape(count, stats.shape[-1])  11.9 us
    all_to_all x1, waiting for transfers between devices, everyone(): return lax.all_to_all(spread, HA, 0, 0).reshape(count, stats.shape[-1])  11.2 us
    pallas_call x1, Pallas kernels, local(): pl.pallas_call(mix_kernel, name='mix', out_shape=(whole(first.shape, F32)...  8.25 us
    pallas_call x1, Pallas kernels, local(): pl.pallas_call(down_kernel, name='down', out_shape=(whole((frames, rows /...  5.53 us
    ppermute x1, starting transfers between devices, local(): cached_above = lax.ppermute(cache_hidden[:, -1:], HA, down)  3.67 us
    ppermute x1, starting transfers between devices, local(): above = lax.ppermute(first[:, -1:], HA, down)  3.31 us
  transfers between devices with their start and end apart: 6, of which 2 were waited for; matrix products, arithmetic and copies ran while one was open for 2% of the time, Pallas kernels for 0%

profile of v1, /device:TPU:513, one launch (start us, length us, event | category | flops | bytes accessed | tf_op | source)
XLA Modules:
  0.0 103.0 jit_solution(16061488258398026394)
XLA Ops:
  0.6 0.9 slice.18
  1.6 0.0 copy-start
  1.6 1.0 slice.19
  2.6 22.4 %collective-permute-start = (bf16[6,1,256,128]{3,2,1,0:T(8,128)(2,1)S(1)}, bf16[6,1,256,128]{3,2,1,0:T(8,128)(2,1)S(1)}, u32[]{:S(2)}, u32[]{:S(2)}) collective-permute-start(bf16[6,1,256,128]{3,2,1,0:T(8,128)(2,1)S(1)} %pad_maximum_fusion), channel_id=1, source_target_pairs={{1,0},{2,1},{3,2},{4,3},{5,4},{6,5},{7,6},{8,7},{9,8},{10,9},{11,1... | collective-permute-start | bytes 1179656 | tf_op jit(solution)/shard_map/ppermute | solution.py:180
  25.0 1.3 %collective-permute-done.rim_ref = bf16[6,1,256,128]{3,2,1,0:T(8,128)(2,1)S(1)} collective-permute-done((bf16[6,1,256,128]{3,2,1,0:T(8,128)(2,1)S(1)}, bf16[6,1,256,128]{3,2,1,0:T(8,128)(2,1)S(1)}, u32[]{:S(2)}, u32[]{:S(2)}) %collective-permute-start) | collective-permute-done | bytes 393248 | tf_op jit(solution)/shard_map/ppermute | solution.py:180
  26.3 0.7 copy-done.3
  27.1 5.5 %down.1 = (f32[4,2,128,256]{3,2,1,0:T(8,128)}, f32[1,128]{1,0:T(1,128)}) custom-call(bf16[2,4,256,128]{3,2,1,0:T(8,128)(2,1)} %cache_ref.1, bf16[4,4,256,128]{3,2,1,0:T(8,128)(2,1)} %video_ref.1, bf16[6,1,256,128]{3,2,1,0:T(8,128)(2,1)} %copy-done.3, bf16[3,3,3,128,256]{4,3,2,1,0:T(8,128)(2,1)} %kernel_ref.2), custom_call_target="tpu_custom_call" | custom-call | tf_op jit(solution)/shard_map/down/pallas_call | solution.py:183
  32.6 1.3 %fusion = (f32[4,1,128,256]{3,2,1,0:T(8,128)S(1)}, f32[4,1,128,256]{3,2,1,0:T(8,128)S(1)}) fusion(f32[4,2,128,256]{3,2,1,0:T(8,128)} %get-tuple-element.7.first_ref), kind=kLoop, calls=%fused_computation.2 | loop fusion | bytes 2097152 | tf_op jit(solution)/shard_map/slice | solution.py:192
  33.9 2.3 %collective-permute-start.2 = (f32[4,1,128,256]{3,2,1,0:T(8,128)S(1)}, f32[4,1,128,256]{3,2,1,0:T(8,128)S(1)}, u32[]{:S(2)}, u32[]{:S(2)}) collective-permute-start(f32[4,1,128,256]{3,2,1,0:T(8,128)S(1)} %get-tuple-element.12), channel_id=1, source_target_pairs={{1,0},{2,1},{3,2},{4,3},{5,4},{6,5},{7,6},{8,7},{9,8},{10,9},{11,1... | collective-permute-start | bytes 1572872 | tf_op jit(solution)/shard_map/ppermute | solution.py:192
  36.2 3.3 %collective-permute-start.1 = (f32[4,1,128,256]{3,2,1,0:T(8,128)S(1)}, f32[4,1,128,256]{3,2,1,0:T(8,128)S(1)}, u32[]{:S(2)}, u32[]{:S(2)}) collective-permute-start(f32[4,1,128,256]{3,2,1,0:T(8,128)S(1)} %get-tuple-element.13), channel_id=1, source_target_pairs={{0,1},{1,2},{2,3},{3,4},{4,5},{5,6},{6,7},{7,8},{8,9},{9,10},{10,1... | collective-permute-start | bytes 1572872 | tf_op jit(solution)/shard_map/ppermute | solution.py:191
  39.5 0.0 copy-done
  39.6 2.0 %collective-permute-start.4 = (bf16[2,1,128,256]{3,2,1,0:T(8,128)(2,1)S(1)}, bf16[2,1,128,256]{3,2,1,0:T(8,128)(2,1)S(1)}, u32[]{:S(2)}, u32[]{:S(2)}) collective-permute-start(bf16[2,1,128,256]{3,2,1,0:T(8,128)(2,1)S(1)} %get-tuple-element.14), channel_id=1, source_target_pairs={{1,0},{2,1},{3,2},{4,3},{5,4},{6,5},{7,6},{8,7},{9,8},{10,9},{11,1... | collective-permute-start | bytes 393224 | tf_op jit(solution)/shard_map/ppermute | solution.py:182
  41.5 3.7 %collective-permute-start.3 = (bf16[2,1,128,256]{3,2,1,0:T(8,128)(2,1)S(1)}, bf16[2,1,128,256]{3,2,1,0:T(8,128)(2,1)S(1)}, u32[]{:S(2)}, u32[]{:S(2)}) collective-permute-start(bf16[2,1,128,256]{3,2,1,0:T(8,128)(2,1)S(1)} %get-tuple-element.15), channel_id=1, source_target_pairs={{0,1},{1,2},{2,3},{3,4},{4,5},{5,6},{6,7},{7,8},{8,9},{9,10},{10,1... | collective-permute-start | bytes 393224 | tf_op jit(solution)/shard_map/ppermute | solution.py:181
  45.2 1.3 %broadcast_in_dim.30 = f32[128,1,128]{2,1,0:T(1,128)} broadcast(f32[128]{0:T(128)} %bitcast.16), dimensions={2} | broadcast | bytes 66048 | tf_op jit(solution)/shard_map/broadcast_in_dim | solution.py:170
  46.5 11.9 %all-to-all-start = ((f32[128,1,128]{2,1,0:T(1,128)}), f32[128,1,128]{2,1,0:T(1,128)S(1)}, u32[]{:S(2)}, u32[]{:S(2)}) async-start(f32[128,1,128]{2,1,0:T(1,128)} %broadcast_in_dim.30), calls=%async_computation | async-start | bytes 131072 | tf_op jit(solution)/shard_map/all_to_all | solution.py:171
  58.5 0.7 add_convert_fusion.edge_ref
  59.1 0.0 collective-permute-done.4.cached_below_ref
  59.1 0.0 collective-permute-done.3.cached_above_ref
  59.1 0.0 copy-start.6
  59.1 11.2 %all-to-all-done = f32[128,1,128]{2,1,0:T(1,128)S(1)} async-done(((f32[128,1,128]{2,1,0:T(1,128)}), f32[128,1,128]{2,1,0:T(1,128)S(1)}, u32[]{:S(2)}, u32[]{:S(2)}) %all-to-all-start) | async-done | bytes 65568 | tf_op jit(solution)/shard_map/all_to_all | solution.py:171
  70.4 0.0 collective-permute-done.2.below_ref
  70.4 0.0 collective-permute-done.1.above_ref
  70.4 0.0 copy-start.2
  70.4 0.0 copy-done.5
  70.4 0.0 copy-done.6
  70.4 0.6 copy-done.4
  71.0 0.2 copy-done.1
  71.2 0.1 copy-done.2
  71.3 8.2 %mix.1 = (f32[4,2,128,256]{3,2,1,0:T(8,128)}, bf16[2,2,128,256]{3,2,1,0:T(8,128)(2,1)}, f32[1,128]{1,0:T(1,128)}) custom-call(f32[4,2,128,256]{3,2,1,0:T(8,128)} %get-tuple-element.7.first_ref, f32[4,1,128,256]{3,2,1,0:T(8,128)} %copy-done.2, f32[4,1,128,256]{3,2,1,0:T(8,128)} %copy-done.1, bf16[2,2,128,256]{3,2,1,0:T(8,128)(2,1)} %hidden_in_ref.1, ...), custom_call_target="tpu_custom_call" | custom-call | tf_op jit(solution)/shard_map/mix/pallas_call | solution.py:196
  79.6 0.6 broadcast_in_dim.34
  80.2 20.1 %all_to_all.10 = f32[128,1,128]{2,1,0:T(1,128)} all-to-all(f32[128,1,128]{2,1,0:T(1,128)S(1)} %broadcast_in_dim.34), channel_id=1, replica_groups=mesh['groups'=2,'ha_0'=8,'ha_1'=8,'ha_2'=2] {'ha_0','ha_1','ha_2'}, dimensions={0} | all-to-all | bytes 131072 | tf_op jit(solution)/shard_map/all_to_all | solution.py:171
  100.3 2.7 %final.1 = bf16[4,2,128,256]{3,2,1,0:T(8,128)(2,1)} custom-call(f32[4,2,128,256]{3,2,1,0:T(8,128)} %get-tuple-element.9.second_ref, f32[128,128]{1,0:T(8,128)} %bitcast.11, f32[1,256]{1,0:T(1,128)} %bitcast.14, f32[1,256]{1,0:T(1,128)} %bitcast.15), custom_call_target="tpu_custom_call" | custom-call | tf_op jit(solution)/shard_map/final/pallas_call | solution.py:212
  (6 shorter events, 0.1 us)
Async XLA Ops:
  1.6 38.0 %copy-start = (bf16[2,2,128,256]{3,2,1,0:T(8,128)(2,1)S(1)}, bf16[2,2,128,256]{3,2,1,0:T(8,128)(2,1)}, u32[]{:S(2)}) copy-start(bf16[2,2,128,256]{3,2,1,0:T(8,128)(2,1)} %hidden_in_ref.1) | copy-start | bytes 786436
  2.6 23.7 %collective-permute-start = (bf16[6,1,256,128]{3,2,1,0:T(8,128)(2,1)S(1)}, bf16[6,1,256,128]{3,2,1,0:T(8,128)(2,1)S(1)}, u32[]{:S(2)}, u32[]{:S(2)}) collective-permute-start(bf16[6,1,256,128]{3,2,1,0:T(8,128)(2,1)S(1)} %pad_maximum_fusion), channel_id=1, source_target_pairs={{1,0},{2,1},{3,2},{4,3},{5,4},{6,5},{7,6},{8,7},{9,8},{10,9},{11,1... | collective-permute-start | bytes 1179656 | tf_op jit(solution)/shard_map/ppermute | solution.py:180
  26.3 0.7 copy-start.3
  33.9 36.5 %collective-permute-start.2 = (f32[4,1,128,256]{3,2,1,0:T(8,128)S(1)}, f32[4,1,128,256]{3,2,1,0:T(8,128)S(1)}, u32[]{:S(2)}, u32[]{:S(2)}) collective-permute-start(f32[4,1,128,256]{3,2,1,0:T(8,128)S(1)} %get-tuple-element.12), channel_id=1, source_target_pairs={{1,0},{2,1},{3,2},{4,3},{5,4},{6,5},{7,6},{8,7},{9,8},{10,9},{11,1... | collective-permute-start | bytes 1572872 | tf_op jit(solution)/shard_map/ppermute | solution.py:192
  36.2 34.1 %collective-permute-start.1 = (f32[4,1,128,256]{3,2,1,0:T(8,128)S(1)}, f32[4,1,128,256]{3,2,1,0:T(8,128)S(1)}, u32[]{:S(2)}, u32[]{:S(2)}) collective-permute-start(f32[4,1,128,256]{3,2,1,0:T(8,128)S(1)} %get-tuple-element.13), channel_id=1, source_target_pairs={{0,1},{1,2},{2,3},{3,4},{4,5},{5,6},{6,7},{7,8},{8,9},{9,10},{10,1... | collective-permute-start | bytes 1572872 | tf_op jit(solution)/shard_map/ppermute | solution.py:191
  39.6 19.5 %collective-permute-start.4 = (bf16[2,1,128,256]{3,2,1,0:T(8,128)(2,1)S(1)}, bf16[2,1,128,256]{3,2,1,0:T(8,128)(2,1)S(1)}, u32[]{:S(2)}, u32[]{:S(2)}) collective-permute-start(bf16[2,1,128,256]{3,2,1,0:T(8,128)(2,1)S(1)} %get-tuple-element.14), channel_id=1, source_target_pairs={{1,0},{2,1},{3,2},{4,3},{5,4},{6,5},{7,6},{8,7},{9,8},{10,9},{11,1... | collective-permute-start | bytes 393224 | tf_op jit(solution)/shard_map/ppermute | solution.py:182
  41.5 17.6 %collective-permute-start.3 = (bf16[2,1,128,256]{3,2,1,0:T(8,128)(2,1)S(1)}, bf16[2,1,128,256]{3,2,1,0:T(8,128)(2,1)S(1)}, u32[]{:S(2)}, u32[]{:S(2)}) collective-permute-start(bf16[2,1,128,256]{3,2,1,0:T(8,128)(2,1)S(1)} %get-tuple-element.15), channel_id=1, source_target_pairs={{0,1},{1,2},{2,3},{3,4},{4,5},{5,6},{6,7},{7,8},{8,9},{9,10},{10,1... | collective-permute-start | bytes 393224 | tf_op jit(solution)/shard_map/ppermute | solution.py:181
  46.5 23.8 %all-to-all-start = ((f32[128,1,128]{2,1,0:T(1,128)}), f32[128,1,128]{2,1,0:T(1,128)S(1)}, u32[]{:S(2)}, u32[]{:S(2)}) async-start(f32[128,1,128]{2,1,0:T(1,128)} %broadcast_in_dim.30), calls=%async_computation | async-start | bytes 131072 | tf_op jit(solution)/shard_map/all_to_all | solution.py:171
  59.1 11.3 %copy-start.5 = (bf16[2,1,128,256]{3,2,1,0:T(8,128)(2,1)}, bf16[2,1,128,256]{3,2,1,0:T(8,128)(2,1)S(1)}, u32[]{:S(2)}) copy-start(bf16[2,1,128,256]{3,2,1,0:T(8,128)(2,1)S(1)} %collective-permute-done.4.cached_below_ref) | copy-start | bytes 393220
  59.1 11.3 %copy-start.6 = (bf16[2,1,128,256]{3,2,1,0:T(8,128)(2,1)}, bf16[2,1,128,256]{3,2,1,0:T(8,128)(2,1)S(1)}, u32[]{:S(2)}) copy-start(bf16[2,1,128,256]{3,2,1,0:T(8,128)(2,1)S(1)} %collective-permute-done.3.cached_above_ref) | copy-start | bytes 393220
  70.4 0.6 copy-start.4
  70.4 0.8 copy-start.1
  70.4 1.0 copy-start.2

commit v2 on v0

v2 whole, which is shorter than its diff:
```python
import jax
import jax.numpy as jnp
from jax import lax
from jax.experimental import pallas as pl
from jax.experimental.pallas import tpu as pltpu
from jax.sharding import Mesh
from jax.sharding import PartitionSpec as P

GROUPS = 32
LANES = 128
EPS = 1e-6
HA = ("ha_0", "ha_1", "ha_2")
F32 = jnp.float32
BF16 = jnp.bfloat16
AUTO = pl.BlockSpec()
ANY = pl.BlockSpec(memory_space=pl.ANY)
HBM = pl.BlockSpec(memory_space=pltpu.HBM)
SMEM = pl.BlockSpec(memory_space=pltpu.SMEM)
DMA = pltpu.SemaphoreType.DMA


def limit(mib):
    return pltpu.CompilerParams(vmem_limit_bytes=mib * 2**20)


def lanes_of(x):
    return lax.broadcasted_iota(jnp.int32, x.shape, x.ndim - 1)


def turn(x, by):
    return pltpu.roll(x, by % x.shape[-1], x.ndim - 1)


def group_sum(x):
    lane = lanes_of(x)
    step = 1
    while step < x.shape[-1] // GROUPS:
        x = x + jnp.where((lane & step) != 0, turn(x, step), turn(x, -step))
        step *= 2
    return x


def column_sum(block):
    return jnp.sum(block, axis=0, keepdims=True)


def moments_row(center, sums, squares, count):
    members = count * (center.shape[-1] // GROUPS)
    shift = group_sum(sums) * (1.0 / members)
    squares = group_sum(squares) - shift * shift * members
    mean = center + shift
    kind = lanes_of(mean[:, :LANES]) % 4
    low = jnp.where(kind == 0, mean[:, :LANES], squares[:, :LANES])
    high = jnp.where(kind == 2, mean[:, LANES:], squares[:, LANES:])
    return jnp.where(kind < 2, low, high)


def affine(rows, members, gain):
    devices = rows.shape[0]
    total = column_sum(rows)
    center = total * (1.0 / devices)
    off = rows - center
    between = column_sum(off * off) * members
    spread = (total + turn(between, 1)) * (1.0 / (members * devices))
    rate = lax.rsqrt(jnp.maximum(spread, 0.0) + EPS)
    kind = lanes_of(total) % 4

    def fill(value, at):
        value = jnp.where(kind == at, value, 0.0)
        value = value + turn(value, 1 if at % 2 == 0 else -1)
        return value + turn(value, 2 if at < 2 else -2)

    centers = jnp.concatenate([fill(center, 0), fill(center, 2)], axis=1)
    rates = jnp.concatenate([fill(rate, 1), fill(rate, 3)], axis=1)
    return centers, rates * gain


def silu_norm(values, center, factor, offset):
    normed = (values - center) * factor + offset
    return normed / (1.0 + jnp.exp(-normed))


def shift_back(x):
    rows = x.shape[0]
    place = lax.broadcasted_iota(jnp.int32, x.shape, 0)
    return jnp.where(place == rows - 1, 0.0, pltpu.roll(x, rows - 1, 0))


def shift_on(x):
    place = lax.broadcasted_iota(jnp.int32, x.shape, 0)
    return jnp.where(place == 0, 0.0, pltpu.roll(x, 1, 0))


def rim_kernel(cache_ref, video_ref, out_ref, sems):
    cached = cache_ref.shape[0]
    copies = [
        pltpu.make_async_copy(cache_ref.at[:, 0], out_ref.at[:cached], sems.at[0]),
        pltpu.make_async_copy(video_ref.at[:, 0], out_ref.at[cached:], sems.at[1]),
    ]
    for c in copies:
        c.start()
    for c in copies:
        c.wait()


def pair_up(source, target, c_in):
    half = target.shape[0]
    target[:, :c_in] = source[pl.ds(0, half, stride=2), :]
    target[:, c_in:] = source[pl.ds(1, half, stride=2), :]


def down_kernel(
    cache_ref, video_ref, kernel_ref,
    row_ref, part_ref, third_ref, center_ref, sums_ref,
    cache_buf, video_buf, kernel_buf, pairs_ref, sems,
):
    frames, rows, width, c_in = video_ref.shape
    cached = cache_ref.shape[0]
    half = width // 2
    c_out = kernel_ref.shape[-1]
    loads = [
        pltpu.make_async_copy(cache_ref, cache_buf, sems.at[0]),
        pltpu.make_async_copy(video_ref, video_buf, sems.at[1]),
        pltpu.make_async_copy(kernel_ref.at[:, :2], kernel_buf, sems.at[2]),
        pltpu.make_async_copy(kernel_ref.at[:, 2], third_ref, sems.at[3]),
    ]
    for c in loads:
        c.start()
    for f in range(cached + frames):
        if f == 0:
            loads[0].wait()
        if f == cached:
            loads[1].wait()
        for r in range(rows):
            source = cache_buf.at[f, r] if f < cached else video_buf.at[f - cached, r]
            pair_up(source, pairs_ref.at[f, r], c_in)
    loads[2].wait()
    loads[3].wait()

    def tap(a, b, c):
        return third_ref[a, c] if b == 2 else kernel_buf[a, b, c]

    for i, depth in ((0, 3), (1, 2)):
        where = [(a, b) for b in range(depth) for a in range(3)]
        taps = [pairs_ref[a : a + frames, 2 * i + b].reshape(frames * half, 2 * c_in) for a, b in where]
        both = jnp.concatenate([tap(a, b, c) for a, b in where for c in range(2)], axis=0)
        ahead = jnp.concatenate([tap(a, b, 2) for a, b in where], axis=0)
        here = jnp.dot(jnp.concatenate(taps, axis=1), both, preferred_element_type=F32)
        evens = jnp.concatenate([t[:, :c_in] for t in taps], axis=1)
        after = jnp.dot(evens, ahead, preferred_element_type=F32)
        for t in range(frames):
            span = slice(t * half, (t + 1) * half)
            block = here[span] + shift_back(after[span])
            if i == 0:
                row_ref[t] = block
            else:
                part_ref[t] = block
    total = sum(column_sum(row_ref[t]) for t in range(frames))
    center = group_sum(total) * (1.0 / (frames * half * (c_out // GROUPS)))
    center_ref[...] = center
    sums_ref[0:1] = total - center * (frames * half)
    sums_ref[1:2] = sum(column_sum((row_ref[t] - center) ** 2) for t in range(frames))


def rim_down_kernel(
    core_ref, rim_ref, third_ref, row_ref, part_ref, center_ref, sums_ref, hidden_ref,
    last_ref, edge_a_ref, edge_b_ref, message_ref,
    pairs_ref, sems,
):
    frames, half, c_out = row_ref.shape
    c_in = rim_ref.shape[-1]
    cached = hidden_ref.shape[0]
    core = core_ref[0]
    loads = [
        pltpu.make_async_copy(hidden_ref.at[:, 1 - core], edge_a_ref.at[:cached], sems.at[0]),
        pltpu.make_async_copy(hidden_ref.at[:, core], edge_b_ref.at[:cached], sems.at[1]),
    ]
    for c in loads:
        c.start()
    for f in range(rim_ref.shape[0]):
        pair_up(rim_ref.at[f], pairs_ref.at[f], c_in)
    taps = [pairs_ref[a : a + frames].reshape(frames * half, 2 * c_in) for a in range(3)]
    both = jnp.concatenate([third_ref[a, c] for a in range(3) for c in range(2)], axis=0)
    ahead = jnp.concatenate([third_ref[a, 2] for a in range(3)], axis=0)
    here = jnp.dot(jnp.concatenate(taps, axis=1), both, preferred_element_type=F32)
    evens = jnp.concatenate([t[:, :c_in] for t in taps], axis=1)
    after = jnp.dot(evens, ahead, preferred_element_type=F32)
    center = center_ref[...]
    sums, squares = sums_ref[0:1], sums_ref[1:2]
    upper = core == 0
    for t in range(frames):
        span = slice(t * half, (t + 1) * half)
        block = part_ref[t] + here[span] + shift_back(after[span])
        last_ref[t] = block
        off = block - center
        sums = sums + column_sum(off)
        squares = squares + column_sum(off * off)
        other = row_ref[t]
        for edge_ref, value in (
            (edge_a_ref, jnp.where(upper, block, other)),
            (edge_b_ref, jnp.where(upper, other, block)),
        ):
            coarse = value.astype(BF16)
            edge_ref[cached + t] = coarse
            edge_ref[cached + frames + t] = (value - coarse.astype(F32)).astype(BF16)
    message = moments_row(center, sums, squares, 2 * frames * half)
    message_ref[...] = jnp.broadcast_to(message[None], message_ref.shape)
    for c in loads:
        c.wait()


def mix_kernel(
    core_ref, row_ref, last_ref, edge_a_ref, edge_b_ref, stats_ref, gain_ref, shift_ref, hidden_ref, kernel_ref,
    second_ref, next_ref, message_ref,
    rows_ref, sem,
):
    frames, width, channels = row_ref.shape
    cached = hidden_ref.shape[0]
    rows = 2
    core, top, bottom = core_ref[0], core_ref[1], core_ref[2]
    for f in range(cached):
        for i in range(rows):
            rows_ref[f, 1 + i] = hidden_ref[f, i]
    count = rows * frames * width
    center, factor = affine(stats_ref[...][:, 0], count * (channels // GROUPS), gain_ref[...])
    offset = shift_ref[...]
    for edge_ref, at, missing in (
        (edge_a_ref, jnp.where(core == 0, rows + 1, 0), jnp.where(core == 0, bottom, top)),
        (edge_b_ref, jnp.where(core == 0, 0, rows + 1), jnp.where(core == 0, top, bottom)),
    ):
        for f in range(cached):
            rows_ref[f, at] = jnp.where(missing != 0, jnp.zeros_like(edge_ref[f]), edge_ref[f])
        for t in range(frames):
            value = edge_ref[cached + t].astype(F32) + edge_ref[cached + frames + t].astype(F32)
            hidden = silu_norm(value, center, factor, offset)
            rows_ref[cached + t, at] = jnp.where(missing != 0, 0.0, hidden).astype(BF16)
    for t in range(frames):
        rows_ref[cached + t, 1] = silu_norm(row_ref[t], center, factor, offset).astype(BF16)
        rows_ref[cached + t, 2] = silu_norm(last_ref[t], center, factor, offset).astype(BF16)
    store = pltpu.make_async_copy(
        rows_ref.at[cached + frames - 2 : cached + frames, 1 : 1 + rows], next_ref, sem
    )
    store.start()
    for c in (1, 0, 2):
        weights = jnp.concatenate([kernel_ref[a, b, c] for a in range(3) for b in range(3)], axis=0)
        for i in range(rows):
            taps = jnp.concatenate(
                [
                    rows_ref[a : a + frames, i + b].reshape(frames * width, channels)
                    for a in range(3)
                    for b in range(3)
                ],
                axis=1,
            )
            result = jnp.dot(taps, weights, preferred_element_type=F32)
            for t in range(frames):
                block = result[t * width : (t + 1) * width]
                if c != 1:
                    block = shift_on(block) if c == 0 else shift_back(block)
                    block = block + second_ref[t, i]
                second_ref[t, i] = block
    total = sum(column_sum(second_ref[t, 0]) for t in range(frames))
    center = group_sum(total) * (1.0 / (frames * width * (channels // GROUPS)))
    offs = [second_ref[t, i] - center for t in range(frames) for i in range(rows)]
    sums = sum(column_sum(off) for off in offs)
    squares = sum(column_sum(off * off) for off in offs)
    message = moments_row(center, sums, squares, count)
    message_ref[...] = jnp.broadcast_to(message[None], message_ref.shape)
    store.wait()


def final_kernel(second_ref, stats_ref, gain_ref, shift_ref, out_ref, buf, sems):
    frames, rows, width, channels = second_ref.shape
    members = frames * rows * width * (channels // GROUPS)
    center, factor = affine(stats_ref[...][:, 0], members, gain_ref[...])
    offset = shift_ref[...]
    stores = []
    for t in range(frames):
        for i in range(rows):
            buf[t, i] = silu_norm(second_ref[t, i], center, factor, offset).astype(BF16)
        stores.append(pltpu.make_async_copy(buf.at[t], out_ref.at[t], sems.at[t]))
        stores[-1].start()
    for c in stores:
        c.wait()


def everyone(message):
    return lax.all_to_all(message, HA, 0, 0)


def local(video, cache_video, cache_hidden, kernel_down, gain_down, shift_down, kernel_mix, gain_mix, shift_mix):
    frames, rows, width, c_in = video.shape
    cached = cache_video.shape[0]
    c_out = kernel_down.shape[-1]
    half = width // 2
    video, cache_video, kernel_down = (
        pltpu.with_memory_space_constraint(x, pltpu.HBM) for x in (video, cache_video, kernel_down)
    )
    devices = lax.axis_size(HA)
    place, core = lax.axis_index(HA), lax.axis_index(HA[-1])
    whole = jax.ShapeDtypeStruct
    spot = jnp.stack([core, place == 0, place == devices - 1]).astype(jnp.int32)
    rim = pl.pallas_call(
        rim_kernel,
        name="rim",
        out_shape=whole((cached + frames, width, c_in), BF16),
        in_specs=[HBM] * 2,
        out_specs=AUTO,
        scratch_shapes=[DMA((2,))],
        compiler_params=limit(4),
    )(cache_video, video)
    rim = lax.ppermute(rim, HA, [(i + 1, i) for i in range(devices - 1)])
    line = whole((frames, half, c_out), F32)
    row, part, third, center, sums = pl.pallas_call(
        down_kernel,
        name="down",
        out_shape=(
            line,
            line,
            whole((3, 3, c_in, c_out), BF16),
            whole((1, c_out), F32),
            whole((2, c_out), F32),
        ),
        in_specs=[HBM] * 3,
        out_specs=(AUTO,) * 5,
        scratch_shapes=[
            pltpu.VMEM(cache_video.shape, BF16),
            pltpu.VMEM(video.shape, BF16),
            pltpu.VMEM((3, 2, 3, c_in, c_out), BF16),
            pltpu.VMEM((cached + frames, rows, half, 2 * c_in), BF16),
            DMA((4,)),
        ],
        compiler_params=limit(24),
        cost_estimate=pl.CostEstimate(flops=2 * 10**9, bytes_accessed=4 * 10**6, transcendentals=0),
    )(cache_video, video, kernel_down)
    edge = whole((cached + 2 * frames, half, c_out), BF16)
    message = whole((devices, 1, LANES), F32)
    last, edge_a, edge_b, stats = pl.pallas_call(
        rim_down_kernel,
        name="rim_down",
        out_shape=(line, edge, edge, message),
        in_specs=[SMEM] + [AUTO] * 6 + [ANY],
        out_specs=(AUTO,) * 4,
        scratch_shapes=[pltpu.VMEM((cached + frames, half, 2 * c_in), BF16), DMA((2,))],
        compiler_params=limit(16),
    )(spot, rim, third, row, part, center, sums, cache_hidden)
    within = [(i, i ^ 1) for i in range(devices)]
    across = [(i, j) for i in range(1, devices - 1) for j in [i + 1 if i % 2 else i - 1]]
    edge_a = lax.ppermute(edge_a, HA, within)
    edge_b = lax.ppermute(edge_b, HA, across)
    stats = everyone(stats)
    second, next_cache, stats = pl.pallas_call(
        mix_kernel,
        name="mix",
        out_shape=(whole((frames, 2, half, c_out), F32), whole((2, 2, half, c_out), BF16), message),
        in_specs=[SMEM] + [AUTO] * 9,
        out_specs=(AUTO, ANY, AUTO),
        scratch_shapes=[
            pltpu.VMEM((cached + frames, 4, half, c_out), BF16),
            DMA(()),
        ],
        compiler_params=limit(28),
    )(spot, row, last, edge_a, edge_b, stats, gain_down[None], shift_down[None], cache_hidden, kernel_mix)
    stats = everyone(stats)
    encoded = pl.pallas_call(
        final_kernel,
        name="final",
        out_shape=whole((frames, 2, half, c_out), BF16),
        in_specs=[AUTO] * 4,
        out_specs=ANY,
        scratch_shapes=[pltpu.VMEM((frames, 2, half, c_out), BF16), DMA((frames,))],
        compiler_params=limit(8),
    )(second, stats, gain_mix[None], shift_mix[None])
    return (encoded, next_cache)


def solution(mesh):
    split = Mesh(
        mesh.devices.reshape(mesh.shape["groups"], 8, 8, 2), ("groups", "ha_0", "ha_1", "ha_2")
    )
    strips = P("groups", HA, None, None)
    return jax.shard_map(
        local,
        mesh=split,
        in_specs=(strips, strips, strips, P(), P(), P(), P(), P(), P()),
        out_specs=(strips, strips),
        check_vma=False,
    )
```

time: 150 us -> 78.4 us (0.52)
  local copies, waits for them, and re-layouts: 27.7 us -> 0.03 us
  blocking collectives: 65.6 us -> 38.5 us
  Pallas kernels: 0 us -> 14.1 us
  other arithmetic: 11.3 us -> 0.08 us
  matrix products: 9.38 us -> 0 us
  waiting for transfers between devices: 7.59 us -> 0.01 us
  starting transfers between devices: 27.4 us -> 24.4 us
    psum x6 -> x0, blocking collectives: 65.6 us -> none  [by_axis(): shard = lax.psum(shard, axis)]
    all_to_all x0 -> x2, blocking collectives: none -> 38.5 us  [everyone(): return lax.all_to_all(message, HA, 0, 0)]
    pallas_call x0 -> x5, Pallas kernels: none -> 14.1 us  [the longest x1 6.17 us: local(): pl.pallas_call(mix_kernel, name='mix', out_shape=(whole((frames, 2, half,...]
    conv_general_dilated x9 -> x0, local copies, waits for them, and re-layouts: 11.3 us -> none  [convolve(): lax.conv_general_dilated(stack[None], kernel, strides, 'VALID', dimension...]
    conv_general_dilated x2 -> x0, matrix products: 9.38 us -> none  [convolve(): lax.conv_general_dilated(stack[None], kernel, strides, 'VALID', dimension...]
    ppermute x3, waiting for transfers between devices: 7.59 us -> 0.01 us  [the longest x1 0.01 us: local(): rim = lax.ppermute(rim, HA, [(i + 1, i) for i in range(devices - 1)])]
    unnamed x16 -> x12, local copies, waits for them, and re-layouts: 4.29 us -> 0.03 us
    reduce_sum x6 -> x0, other arithmetic: 4.14 us -> none  [group_totals(): return jnp.sum(values, axis=(0, 1, 2)).reshape(-1, per_group).sum(1)]
  transfers between devices with their start and end apart: 3 -> 3, of which waited for: 3 -> 0; matrix products, arithmetic and copies ran while one was open for 0% -> 0% of each run, Pallas kernels for 0% -> 5%
where the time goes in v2:
time: 78.4 us; the launch traced here: 78.1 us
  blocking collectives  38.5 us (49%)
  starting transfers between devices  24.4 us (31%)
  Pallas kernels  14.1 us (18%)
  between operations  0.92 us (1%)
    all_to_all x2, blocking collectives, everyone(): return lax.all_to_all(message, HA, 0, 0)  38.5 us
    ppermute x1, starting transfers between devices, local(): rim = lax.ppermute(rim, HA, [(i + 1, i) for i in range(devices - 1)])  22.4 us
    pallas_call x1, Pallas kernels, local(): pl.pallas_call(mix_kernel, name='mix', out_shape=(whole((frames, 2, half,...  6.17 us
    pallas_call x1, Pallas kernels, local(): pl.pallas_call(down_kernel, name='down', out_shape=(line, line, whole((3,...  3.83 us
    ppermute x1, starting transfers between devices, local(): edge_b = lax.ppermute(edge_b, HA, across)  1.95 us
    pallas_call x1, Pallas kernels, local(): pl.pallas_call(rim_down_kernel, name='rim_down', out_shape=(line, edge, e...  1.73 us
  transfers between devices with their start and end apart: 3, of which 0 were waited for; matrix products, arithmetic and copies ran while one was open for 0% of the time, Pallas kernels for 5%

profile of v2, /device:TPU:513, one launch (start us, length us, event | category | flops | bytes accessed | tf_op | source)
XLA Modules:
  0.0 78.1 jit_solution(7774621075435099224)
XLA Ops:
  0.6 1.0 %rim.1 = bf16[6,256,128]{2,1,0:T(8,128)(2,1)S(1)} custom-call(bf16[2,4,256,128]{3,2,1,0:T(8,128)(2,1)} %cache_ref.3, bf16[4,4,256,128]{3,2,1,0:T(8,128)(2,1)} %video_ref.3), custom_call_target="tpu_custom_call" | custom-call | tf_op jit(solution)/shard_map/rim/pallas_call | solution.py:303
  1.7 22.4 %collective-permute-start = (bf16[6,256,128]{2,1,0:T(8,128)(2,1)S(1)}, bf16[6,256,128]{2,1,0:T(8,128)(2,1)S(1)}, u32[]{:S(2)}, u32[]{:S(2)}) collective-permute-start(bf16[6,256,128]{2,1,0:T(8,128)(2,1)S(1)} %rim.1), channel_id=1, source_target_pairs={{1,0},{2,1},{3,2},{4,3},{5,4},{6,5},{7,6},{8,7},{9,8},{10,9},{11,1... | collective-permute-start | bytes 1179656 | tf_op jit(solution)/shard_map/ppermute | solution.py:312
  24.0 0.1 pad_add_fusion.core_ref
  24.1 0.0 copy-start.1
  24.1 0.0 copy-start
  24.1 0.0 copy-start.2
  24.1 0.0 copy-start.3
  24.1 3.8 %down.1 = (f32[4,128,256]{2,1,0:T(8,128)S(1)}, f32[4,128,256]{2,1,0:T(8,128)S(1)}, bf16[3,3,128,256]{3,2,1,0:T(8,128)(2,1)S(1)}, f32[1,256]{1,0:T(1,128)S(1)}, f32[2,256]{1,0:T(2,128)S(1)}) custom-call(bf16[2,4,256,128]{3,2,1,0:T(8,128)(2,1)} %cache_ref.3, bf16[4,4,256,128]{3,2,1,0:T(8,128)(2,1)} %video_ref.3, bf16[3,3,3,128,256]{4,3,2,1,0:T(8,128)(2,1)} %kernel_ref.2), custom_call_target="tpu_custom_call" | custom-call | flops 2000000000 | bytes 4000000 | tf_op jit(solution)/shard_map/down/pallas_call | solution.py:314
  28.0 0.0 collective-permute-done.rim_ref
  28.0 0.0 copy-done.1
  28.0 1.7 %rim_down.1 = (f32[4,128,256]{2,1,0:T(8,128)S(1)}, bf16[10,128,256]{2,1,0:T(8,128)(2,1)S(1)}, bf16[10,128,256]{2,1,0:T(8,128)(2,1)S(1)}, f32[128,1,128]{2,1,0:T(1,128)S(1)}) custom-call(s32[3]{0:T(128)S(1)} %pad_add_fusion.core_ref, bf16[6,256,128]{2,1,0:T(8,128)(2,1)S(1)} %collective-permute-done.rim_ref, ...), custom_call_target="tpu_custom_call" | custom-call | tf_op jit(solution)/shard_map/rim_down/pallas_call | solution.py:338
  29.7 0.0 copy-start.4
  29.7 0.0 copy-start.5
  29.8 0.1 collective-permute-start.1
  29.9 2.0 %collective-permute-start.2 = (bf16[10,128,256]{2,1,0:T(8,128)(2,1)S(1)}, bf16[10,128,256]{2,1,0:T(8,128)(2,1)S(1)}, u32[]{:S(2)}, u32[]{:S(2)}) collective-permute-start(bf16[10,128,256]{2,1,0:T(8,128)(2,1)S(1)} %get-tuple-element.21), channel_id=1, source_target_pairs={{1,2},{2,1},{3,4},{4,3},{5,6},{6,5},{7,8},{8,7},{9,10},{10,9},{11,... | collective-permute-start | bytes 1966088 | tf_op jit(solution)/shard_map/ppermute | solution.py:350
  31.9 19.1 %all_to_all.10.stats_ref = f32[128,1,128]{2,1,0:T(1,128)S(1)} all-to-all(f32[128,1,128]{2,1,0:T(1,128)S(1)} %get-tuple-element.22), channel_id=1, replica_groups=mesh['groups'=2,'ha_0'=8,'ha_1'=8,'ha_2'=2] {'ha_0','ha_1','ha_2'}, dimensions={0} | all-to-all | bytes 131072 | tf_op jit(solution)/shard_map/all_to_all | solution.py:288
  51.0 0.0 collective-permute-done.1.edge_a_ref
  51.0 0.0 collective-permute-done.2.edge_b_ref
  51.0 0.0 copy-done
  51.0 0.0 copy-done.2
  51.0 0.0 copy-done.3
  51.0 6.2 %mix.1 = (f32[4,2,128,256]{3,2,1,0:T(8,128)S(1)}, bf16[2,2,128,256]{3,2,1,0:T(8,128)(2,1)}, f32[128,1,128]{2,1,0:T(1,128)S(1)}) custom-call(s32[3]{0:T(128)S(1)} %pad_add_fusion.core_ref, f32[4,128,256]{2,1,0:T(8,128)S(1)} %get-tuple-element.14.row_ref, f32[4,128,256]{2,1,0:T(8,128)S(1)} %get-tuple-element.19.last_ref, ...), custom_call_target="tpu_custom_call" | custom-call | tf_op jit(solution)/shard_map/mix/pallas_call | solution.py:352
  57.2 19.4 %all_to_all.11.stats_ref = f32[128,1,128]{2,1,0:T(1,128)S(1)} all-to-all(f32[128,1,128]{2,1,0:T(1,128)S(1)} %get-tuple-element.24), channel_id=1, replica_groups=mesh['groups'=2,'ha_0'=8,'ha_1'=8,'ha_2'=2] {'ha_0','ha_1','ha_2'}, dimensions={0} | all-to-all | bytes 131072 | tf_op jit(solution)/shard_map/all_to_all | solution.py:288
  76.6 0.0 copy-done.4
  76.6 0.0 copy-done.5
  76.6 1.4 %final.1 = bf16[4,2,128,256]{3,2,1,0:T(8,128)(2,1)} custom-call(f32[4,2,128,256]{3,2,1,0:T(8,128)S(1)} %get-tuple-element.23.second_ref, f32[128,1,128]{2,1,0:T(1,128)S(1)} %all_to_all.11.stats_ref, f32[1,256]{1,0:T(1,128)S(1)} %bitcast.9, f32[1,256]{1,0:T(1,128)S(1)} %bitcast.10), custom_call_target="tpu_custom_call" | custom-call | tf_op jit(solution)/shard_map/final/pallas_call | solution.py:365
Async XLA Ops:
  1.7 26.3 %collective-permute-start = (bf16[6,256,128]{2,1,0:T(8,128)(2,1)S(1)}, bf16[6,256,128]{2,1,0:T(8,128)(2,1)S(1)}, u32[]{:S(2)}, u32[]{:S(2)}) collective-permute-start(bf16[6,256,128]{2,1,0:T(8,128)(2,1)S(1)} %rim.1), channel_id=1, source_target_pairs={{1,0},{2,1},{3,2},{4,3},{5,4},{6,5},{7,6},{8,7},{9,8},{10,9},{11,1... | collective-permute-start | bytes 1179656 | tf_op jit(solution)/shard_map/ppermute | solution.py:312
  24.1 3.9 %copy-start.1 = (bf16[2,2,128,256]{3,2,1,0:T(8,128)(2,1)S(1)}, bf16[2,2,128,256]{3,2,1,0:T(8,128)(2,1)}, u32[]{:S(2)}) copy-start(bf16[2,2,128,256]{3,2,1,0:T(8,128)(2,1)} %hidden_ref.3) | copy-start | bytes 786436
  24.1 26.8 %copy-start = (bf16[3,3,3,256,256]{4,3,2,1,0:T(8,128)(2,1)S(1)}, bf16[3,3,3,256,256]{4,3,2,1,0:T(8,128)(2,1)}, u32[]{:S(2)}) copy-start(bf16[3,3,3,256,256]{4,3,2,1,0:T(8,128)(2,1)} %kernel_ref.3) | copy-start | bytes 10616836
  24.1 26.9 %copy-start.2 = (f32[256]{0:T(256)S(1)}, f32[256]{0:T(256)}, u32[]{:S(2)}) copy-start(f32[256]{0:T(256)} %param.13) | copy-start | bytes 3076
  24.1 26.9 %copy-start.3 = (f32[256]{0:T(256)S(1)}, f32[256]{0:T(256)}, u32[]{:S(2)}) copy-start(f32[256]{0:T(256)} %param.14) | copy-start | bytes 3076
  29.7 46.9 %copy-start.4 = (f32[256]{0:T(256)S(1)}, f32[256]{0:T(256)}, u32[]{:S(2)}) copy-start(f32[256]{0:T(256)} %param.16) | copy-start | bytes 3076
  29.7 46.9 %copy-start.5 = (f32[256]{0:T(256)S(1)}, f32[256]{0:T(256)}, u32[]{:S(2)}) copy-start(f32[256]{0:T(256)} %param.17) | copy-start | bytes 3076
  29.8 21.2 %collective-permute-start.1 = (bf16[10,128,256]{2,1,0:T(8,128)(2,1)S(1)}, bf16[10,128,256]{2,1,0:T(8,128)(2,1)S(1)}, u32[]{:S(2)}, u32[]{:S(2)}) collective-permute-start(bf16[10,128,256]{2,1,0:T(8,128)(2,1)S(1)} %get-tuple-element.20), channel_id=1, source_target_pairs={{0,1},{1,0},{2,3},{3,2},{4,5},{5,4},{6,7},{7,6},{8,9},{9,8},{10,11... | collective-permute-start | bytes 1966088 | tf_op jit(solution)/shard_map/ppermute | solution.py:349
  29.9 21.1 %collective-permute-start.2 = (bf16[10,128,256]{2,1,0:T(8,128)(2,1)S(1)}, bf16[10,128,256]{2,1,0:T(8,128)(2,1)S(1)}, u32[]{:S(2)}, u32[]{:S(2)}) collective-permute-start(bf16[10,128,256]{2,1,0:T(8,128)(2,1)S(1)} %get-tuple-element.21), channel_id=1, source_target_pairs={{1,2},{2,1},{3,4},{4,3},{5,6},{6,5},{7,8},{8,7},{9,10},{10,9},{11,... | collective-permute-start | bytes 1966088 | tf_op jit(solution)/shard_map/ppermute | solution.py:350

commit v3 on v2

--- a/solution.py
+++ b/solution.py
@@ -15,7 +15,6 @@
 AUTO = pl.BlockSpec()
 ANY = pl.BlockSpec(memory_space=pl.ANY)
 HBM = pl.BlockSpec(memory_space=pltpu.HBM)
-SMEM = pl.BlockSpec(memory_space=pltpu.SMEM)
 DMA = pltpu.SemaphoreType.DMA
 
 
@@ -109,9 +108,14 @@
     target[:, c_in:] = source[pl.ds(1, half, stride=2), :]
 
 
+def split_in_two(value):
+    coarse = value.astype(BF16)
+    return coarse, (value - coarse.astype(F32)).astype(BF16)
+
+
 def down_kernel(
-    cache_ref, video_ref, kernel_ref,
-    row_ref, part_ref, third_ref, center_ref, sums_ref,
+    cache_ref, video_ref, kernel_ref, hidden_ref,
+    row_ref, part_ref, third_ref, center_ref, sums_ref, edge_ref,
     cache_buf, video_buf, kernel_buf, pairs_ref, sems,
 ):
     frames, rows, width, c_in = video_ref.shape
@@ -134,6 +138,8 @@
         for r in range(rows):
             source = cache_buf.at[f, r] if f < cached else video_buf.at[f - cached, r]
             pair_up(source, pairs_ref.at[f, r], c_in)
+    for f in range(cached):
+        edge_ref[f] = hidden_ref[f, 0]
     loads[2].wait()
     loads[3].wait()
 
@@ -153,6 +159,7 @@
             block = here[span] + shift_back(after[span])
             if i == 0:
                 row_ref[t] = block
+                edge_ref[cached + t], edge_ref[cached + frames + t] = split_in_two(block)
             else:
                 part_ref[t] = block
     total = sum(column_sum(row_ref[t]) for t in range(frames))
@@ -163,22 +170,17 @@
 
 
 def rim_down_kernel(
-    core_ref, rim_ref, third_ref, row_ref, part_ref, center_ref, sums_ref, hidden_ref,
-    last_ref, edge_a_ref, edge_b_ref, message_ref,
-    pairs_ref, sems,
+    rim_ref, third_ref, part_ref, center_ref, sums_ref, hidden_ref,
+    last_ref, edge_ref, message_ref,
+    pairs_ref,
 ):
-    frames, half, c_out = row_ref.shape
+    frames, half, c_out = part_ref.shape
     c_in = rim_ref.shape[-1]
-    cached = hidden_ref.shape[0]
-    core = core_ref[0]
-    loads = [
-        pltpu.make_async_copy(hidden_ref.at[:, 1 - core], edge_a_ref.at[:cached], sems.at[0]),
-        pltpu.make_async_copy(hidden_ref.at[:, core], edge_b_ref.at[:cached], sems.at[1]),
-    ]
-    for c in loads:
-        c.start()
+    cached, rows = hidden_ref.shape[:2]
     for f in range(rim_ref.shape[0]):
         pair_up(rim_ref.at[f], pairs_ref.at[f], c_in)
+    for f in range(cached):
+        edge_ref[f] = hidden_ref[f, rows - 1]
     taps = [pairs_ref[a : a + frames].reshape(frames * half, 2 * c_in) for a in range(3)]
     both = jnp.concatenate([third_ref[a, c] for a in range(3) for c in range(2)], axis=0)
     ahead = jnp.concatenate([third_ref[a, 2] for a in range(3)], axis=0)
@@ -187,92 +189,88 @@
     after = jnp.dot(evens, ahead, preferred_element_type=F32)
     center = center_ref[...]
     sums, squares = sums_ref[0:1], sums_ref[1:2]
-    upper = core == 0
     for t in range(frames):
         span = slice(t * half, (t + 1) * half)
         block = part_ref[t] + here[span] + shift_back(after[span])
         last_ref[t] = block
+        edge_ref[cached + t], edge_ref[cached + frames + t] = split_in_two(block)
         off = block - center
         sums = sums + column_sum(off)
         squares = squares + column_sum(off * off)
-        other = row_ref[t]
-        for edge_ref, value in (
-            (edge_a_ref, jnp.where(upper, block, other)),
-            (edge_b_ref, jnp.where(upper, other, block)),
-        ):
-            coarse = value.astype(BF16)
-            edge_ref[cached + t] = coarse
-            edge_ref[cached + frames + t] = (value - coarse.astype(F32)).astype(BF16)
-    message = moments_row(center, sums, squares, 2 * frames * half)
-    message_ref[...] = jnp.broadcast_to(message[None], message_ref.shape)
-    for c in loads:
-        c.wait()
+    message_ref[...] = moments_row(center, sums, squares, 2 * frames * half)
+
+
+def unpack(stats_ref):
+    both = stats_ref[...][:, 0]
+    return jnp.concatenate([both[:, :LANES], both[:, LANES:]], axis=0)
 
 
 def mix_kernel(
-    core_ref, row_ref, last_ref, edge_a_ref, edge_b_ref, stats_ref, gain_ref, shift_ref, hidden_ref, kernel_ref,
+    row_ref, last_ref, above_ref, below_ref, ends_ref, stats_ref, gain_ref, shift_ref, hidden_ref, kernel_ref,
     second_ref, next_ref, message_ref,
     rows_ref, sem,
 ):
     frames, width, channels = row_ref.shape
     cached = hidden_ref.shape[0]
     rows = 2
-    core, top, bottom = core_ref[0], core_ref[1], core_ref[2]
+    count = rows * frames * width
     for f in range(cached):
+        rows_ref[f, 0] = above_ref[f]
+        rows_ref[f, rows + 1] = below_ref[f]
         for i in range(rows):
             rows_ref[f, 1 + i] = hidden_ref[f, i]
-    count = rows * frames * width
-    center, factor = affine(stats_ref[...][:, 0], count * (channels // GROUPS), gain_ref[...])
+    center, factor = affine(unpack(stats_ref), count * (channels // GROUPS), gain_ref[...])
     offset = shift_ref[...]
-    for edge_ref, at, missing in (
-        (edge_a_ref, jnp.where(core == 0, rows + 1, 0), jnp.where(core == 0, bottom, top)),
-        (edge_b_ref, jnp.where(core == 0, 0, rows + 1), jnp.where(core == 0, top, bottom)),
-    ):
-        for f in range(cached):
-            rows_ref[f, at] = jnp.where(missing != 0, jnp.zeros_like(edge_ref[f]), edge_ref[f])
-        for t in range(frames):
+    keep_above, keep_below = ends_ref[0:1], ends_ref[1:2]
+
+    def activate(t):
+        for at, edge_ref, keep in ((0, above_ref, keep_above), (rows + 1, below_ref, keep_below)):
             value = edge_ref[cached + t].astype(F32) + edge_ref[cached + frames + t].astype(F32)
             hidden = silu_norm(value, center, factor, offset)
-            rows_ref[cached + t, at] = jnp.where(missing != 0, 0.0, hidden).astype(BF16)
-    for t in range(frames):
+            rows_ref[cached + t, at] = jnp.where(keep > 0, hidden, 0.0).astype(BF16)
         rows_ref[cached + t, 1] = silu_norm(row_ref[t], center, factor, offset).astype(BF16)
         rows_ref[cached + t, 2] = silu_norm(last_ref[t], center, factor, offset).astype(BF16)
+
+    weights = [
+        jnp.concatenate([kernel_ref[a, b, c] for a in range(3) for b in range(3)], axis=0)
+        for c in range(3)
+    ]
+    step = frames // 2
+    for begin in range(0, frames, step):
+        for t in range(begin, begin + step):
+            activate(t)
+        taps = jnp.concatenate(
+            [
+                rows_ref[begin + a : begin + a + step, b : b + rows].reshape(step * rows * width, channels)
+                for a in range(3)
+                for b in range(3)
+            ],
+            axis=1,
+        )
+        left, here, right = (jnp.dot(taps, w, preferred_element_type=F32) for w in weights)
+        for n in range(step * rows):
+            span = slice(n * width, (n + 1) * width)
+            t, i = begin + n // rows, n % rows
+            second_ref[t, i] = here[span] + shift_on(left[span]) + shift_back(right[span])
+        if begin == 0:
+            blocks = [second_ref[t, i] for t in range(step) for i in range(rows)]
+            total = sum(column_sum(b) for b in blocks)
+            middle = group_sum(total) * (2.0 / (count * (channels // GROUPS)))
     store = pltpu.make_async_copy(
         rows_ref.at[cached + frames - 2 : cached + frames, 1 : 1 + rows], next_ref, sem
     )
     store.start()
-    for c in (1, 0, 2):
-        weights = jnp.concatenate([kernel_ref[a, b, c] for a in range(3) for b in range(3)], axis=0)
-        for i in range(rows):
-            taps = jnp.concatenate(
-                [
-                    rows_ref[a : a + frames, i + b].reshape(frames * width, channels)
-                    for a in range(3)
-                    for b in range(3)
-                ],
-                axis=1,
-            )
-            result = jnp.dot(taps, weights, preferred_element_type=F32)
-            for t in range(frames):
-                block = result[t * width : (t + 1) * width]
-                if c != 1:
-                    block = shift_on(block) if c == 0 else shift_back(block)
-                    block = block + second_ref[t, i]
-                second_ref[t, i] = block
-    total = sum(column_sum(second_ref[t, 0]) for t in range(frames))
-    center = group_sum(total) * (1.0 / (frames * width * (channels // GROUPS)))
-    offs = [second_ref[t, i] - center for t in range(frames) for i in range(rows)]
+    offs = [second_ref[t, i] - middle for t in range(frames) for i in range(rows)]
     sums = sum(column_sum(off) for off in offs)
     squares = sum(column_sum(off * off) for off in offs)
-    message = moments_row(center, sums, squares, count)
-    message_ref[...] = jnp.broadcast_to(message[None], message_ref.shape)
+    message_ref[...] = moments_row(middle, sums, squares, count)
     store.wait()
 
 
 def final_kernel(second_ref, stats_ref, gain_ref, shift_ref, out_ref, buf, sems):
     frames, rows, width, channels = second_ref.shape
     members = frames * rows * width * (channels // GROUPS)
-    center, factor = affine(stats_ref[...][:, 0], members, gain_ref[...])
+    center, factor = affine(unpack(stats_ref), members, gain_ref[...])
     offset = shift_ref[...]
     stores = []
     for t in range(frames):
@@ -284,8 +282,23 @@
         c.wait()
 
 
+def both_kernel(mine_ref, other_ref, out_ref):
+    both = jnp.concatenate([mine_ref[...], other_ref[...]], axis=1)
+    out_ref[...] = jnp.broadcast_to(both[None], out_ref.shape)
+
+
 def everyone(message):
-    return lax.all_to_all(message, HA, 0, 0)
+    devices, chips = lax.axis_size(HA), lax.axis_size(HA[:-1])
+    other = lax.ppermute(message, HA, [(i, i ^ 1) for i in range(devices)])
+    copies = pl.pallas_call(
+        both_kernel,
+        name="both",
+        out_shape=jax.ShapeDtypeStruct((chips, 1, 2 * LANES), F32),
+        in_specs=[AUTO] * 2,
+        out_specs=AUTO,
+        compiler_params=limit(1),
+    )(message, other)
+    return lax.all_to_all(copies, HA[:-1], 0, 0)
 
 
 def local(video, cache_video, cache_hidden, kernel_down, gain_down, shift_down, kernel_mix, gain_mix, shift_mix):
@@ -297,9 +310,10 @@
         pltpu.with_memory_space_constraint(x, pltpu.HBM) for x in (video, cache_video, kernel_down)
     )
     devices = lax.axis_size(HA)
-    place, core = lax.axis_index(HA), lax.axis_index(HA[-1])
+    place = lax.axis_index(HA)
+    up = [(i + 1, i) for i in range(devices - 1)]
+    down = [(i, i + 1) for i in range(devices - 1)]
     whole = jax.ShapeDtypeStruct
-    spot = jnp.stack([core, place == 0, place == devices - 1]).astype(jnp.int32)
     rim = pl.pallas_call(
         rim_kernel,
         name="rim",
@@ -309,9 +323,15 @@
         scratch_shapes=[DMA((2,))],
         compiler_params=limit(4),
     )(cache_video, video)
-    rim = lax.ppermute(rim, HA, [(i + 1, i) for i in range(devices - 1)])
+    rim = lax.ppermute(rim, HA, up)
+    ends = jnp.broadcast_to(
+        jnp.stack([place > 0, place < devices - 1]).astype(F32)[:, None], (2, c_out)
+    )
+    cache_hidden, ends = lax.optimization_barrier((cache_hidden, ends))
     line = whole((frames, half, c_out), F32)
-    row, part, third, center, sums = pl.pallas_call(
+    edge = whole((cached + 2 * frames, half, c_out), BF16)
+    message = whole((1, LANES), F32)
+    row, part, third, center, sums, below = pl.pallas_call(
         down_kernel,
         name="down",
         out_shape=(
@@ -320,9 +340,10 @@
             whole((3, 3, c_in, c_out), BF16),
             whole((1, c_out), F32),
             whole((2, c_out), F32),
+            edge,
         ),
-        in_specs=[HBM] * 3,
-        out_specs=(AUTO,) * 5,
+        in_specs=[HBM] * 3 + [AUTO],
+        out_specs=(AUTO,) * 6,
         scratch_shapes=[
             pltpu.VMEM(cache_video.shape, BF16),
             pltpu.VMEM(video.shape, BF16),
@@ -332,35 +353,31 @@
         ],
         compiler_params=limit(24),
         cost_estimate=pl.CostEstimate(flops=2 * 10**9, bytes_accessed=4 * 10**6, transcendentals=0),
-    )(cache_video, video, kernel_down)
-    edge = whole((cached + 2 * frames, half, c_out), BF16)
-    message = whole((devices, 1, LANES), F32)
-    last, edge_a, edge_b, stats = pl.pallas_call(
+    )(cache_video, video, kernel_down, cache_hidden)
+    below = lax.ppermute(below, HA, up)
+    last, above, stats = pl.pallas_call(
         rim_down_kernel,
         name="rim_down",
-        out_shape=(line, edge, edge, message),
-        in_specs=[SMEM] + [AUTO] * 6 + [ANY],
-        out_specs=(AUTO,) * 4,
-        scratch_shapes=[pltpu.VMEM((cached + frames, half, 2 * c_in), BF16), DMA((2,))],
+        out_shape=(line, edge, message),
+        in_specs=[AUTO] * 6,
+        out_specs=(AUTO,) * 3,
+        scratch_shapes=[pltpu.VMEM((cached + frames, half, 2 * c_in), BF16)],
         compiler_params=limit(16),
-    )(spot, rim, third, row, part, center, sums, cache_hidden)
-    within = [(i, i ^ 1) for i in range(devices)]
-    across = [(i, j) for i in range(1, devices - 1) for j in [i + 1 if i % 2 else i - 1]]
-    edge_a = lax.ppermute(edge_a, HA, within)
-    edge_b = lax.ppermute(edge_b, HA, across)
+    )(rim, third, part, center, sums, cache_hidden)
+    above = lax.ppermute(above, HA, down)
     stats = everyone(stats)
     second, next_cache, stats = pl.pallas_call(
         mix_kernel,
         name="mix",
         out_shape=(whole((frames, 2, half, c_out), F32), whole((2, 2, half, c_out), BF16), message),
-        in_specs=[SMEM] + [AUTO] * 9,
+        in_specs=[AUTO] * 10,
         out_specs=(AUTO, ANY, AUTO),
         scratch_shapes=[
             pltpu.VMEM((cached + frames, 4, half, c_out), BF16),
             DMA(()),
         ],
         compiler_params=limit(28),
-    )(spot, row, last, edge_a, edge_b, stats, gain_down[None], shift_down[None], cache_hidden, kernel_mix)
+    )(row, last, above, below, ends, stats, gain_down[None], shift_down[None], cache_hidden, kernel_mix)
     stats = everyone(stats)
     encoded = pl.pallas_call(
         final_kernel,

time: 78.4 us -> 76.7 us (0.978)
  blocking collectives: 38.5 us -> 31.1 us
  starting transfers between devices: 24.4 us -> 29.6 us
  Pallas kernels: 14.1 us -> 11.8 us
  waiting for transfers between devices: 0.01 us -> 1.96 us
  local copies, waits for them, and re-layouts: 0.03 us -> 1.05 us
    all_to_all x2, blocking collectives: 38.5 us -> 31.1 us  [everyone(): return lax.all_to_all(copies, HA[:-1], 0, 0)]
    ppermute x3 -> x5, starting transfers between devices: 24.4 us -> 29.6 us  [the longest x1 22.4 us: local(): rim = lax.ppermute(rim, HA, up)]
    ppermute x3 -> x5, waiting for transfers between devices: 0.01 us -> 1.96 us  [the longest x2 1.95 us: everyone(): other = lax.ppermute(message, HA, [(i, i ^ 1) for i in range(devices)])]
    pallas_call x1, Pallas kernels: 6.17 us -> 4.78 us  [local(): pl.pallas_call(mix_kernel, name='mix', out_shape=(whole((frames, 2, half,...]
    unnamed x12 -> x14, local copies, waits for them, and re-layouts: 0.03 us -> 0.98 us
    pallas_call x1 -> x3, Pallas kernels: 1.73 us -> 0.89 us  [the longest x1 0.84 us: local(): pl.pallas_call(rim_down_kernel, name='rim_down', out_shape=(line, edge, m...]
  transfers between devices with their start and end apart: 3 -> 5, of which waited for: 0 -> 2; matrix products, arithmetic and copies ran while one was open for 0% -> 0% of each run, Pallas kernels for 5% -> 6%
where the time goes in v3:
time: 76.7 us; the launch traced here: 76.4 us
  blocking collectives  31.1 us (41%)
  starting transfers between devices  29.6 us (39%)
  Pallas kernels  11.8 us (15%)
  waiting for transfers between devices  1.96 us (3%)
  local copies, waits for them, and re-layouts  1.05 us (1%)
  between operations  0.77 us (1%)
    all_to_all x2, blocking collectives, everyone(): return lax.all_to_all(copies, HA[:-1], 0, 0)  31.1 us
    ppermute x1, starting transfers between devices, local(): rim = lax.ppermute(rim, HA, up)  22.4 us
    pallas_call x1, Pallas kernels, local(): pl.pallas_call(mix_kernel, name='mix', out_shape=(whole((frames, 2, half,...  4.78 us
    pallas_call x1, Pallas kernels, local(): pl.pallas_call(down_kernel, name='down', out_shape=(line, line, whole((3,...  3.81 us
    ppermute x1, starting transfers between devices, local(): above = lax.ppermute(above, HA, down)  3.67 us
    ppermute x2, waiting for transfers between devices, everyone(): other = lax.ppermute(message, HA, [(i, i ^ 1) for i in range(devices)])  1.95 us
    ppermute x1, starting transfers between devices, local(): below = lax.ppermute(below, HA, up)  1.95 us
    ppermute x2, starting transfers between devices, everyone(): other = lax.ppermute(message, HA, [(i, i ^ 1) for i in range(devices)])  1.63 us
  transfers between devices with their start and end apart: 5, of which 2 were waited for; matrix products, arithmetic and copies ran while one was open for 0% of the time, Pallas kernels for 6%

profile of v3, /device:TPU:513, one launch (start us, length us, event | category | flops | bytes accessed | tf_op | source)
XLA Modules:
  0.0 76.4 jit_solution(8623261044891149775)
XLA Ops:
  0.6 1.0 %rim.1 = bf16[6,256,128]{2,1,0:T(8,128)(2,1)S(1)} custom-call(bf16[2,4,256,128]{3,2,1,0:T(8,128)(2,1)} %cache_ref.3, bf16[4,4,256,128]{3,2,1,0:T(8,128)(2,1)} %video_ref.3), custom_call_target="tpu_custom_call" | custom-call | tf_op jit(solution)/shard_map/rim/pallas_call | solution.py:317
  1.7 22.4 %collective-permute-start = (bf16[6,256,128]{2,1,0:T(8,128)(2,1)S(1)}, bf16[6,256,128]{2,1,0:T(8,128)(2,1)S(1)}, u32[]{:S(2)}, u32[]{:S(2)}) collective-permute-start(bf16[6,256,128]{2,1,0:T(8,128)(2,1)S(1)} %rim.1), channel_id=1, source_target_pairs={{1,0},{2,1},{3,2},{4,3},{5,4},{6,5},{7,6},{8,7},{9,8},{10,9},{11,1... | collective-permute-start | bytes 1179656 | tf_op jit(solution)/shard_map/ppermute | solution.py:326
  24.0 0.1 add_convert_fusion
  24.1 0.1 broadcast_in_dim.18.ends_ref
  24.2 0.0 copy-start.1
  24.2 0.9 %copy-done.1 = bf16[2,2,128,256]{3,2,1,0:T(8,128)(2,1)S(1)} copy-done((bf16[2,2,128,256]{3,2,1,0:T(8,128)(2,1)S(1)}, bf16[2,2,128,256]{3,2,1,0:T(8,128)(2,1)}, u32[]{:S(2)}) %copy-start.1) | copy-done | bytes 262168
  25.1 0.0 copy-start
  25.1 0.0 copy-start.2
  25.2 0.0 copy-start.5
  25.2 3.8 %down.1 = (f32[4,128,256]{2,1,0:T(8,128)S(1)}, f32[4,128,256]{2,1,0:T(8,128)S(1)}, bf16[3,3,128,256]{3,2,1,0:T(8,128)(2,1)S(1)}, f32[1,256]{1,0:T(1,128)S(1)}, f...) custom-call(bf16[2,4,256,128]{3,2,1,0:T(8,128)(2,1)} %cache_ref.3, bf16[4,4,256,128]{3,2,1,0:T(8,128)(2,1)} %video_ref.3, ...), custom_call_target="tpu_custom_call" | custom-call | flops 2000000000 | bytes 4000000 | tf_op jit(solution)/shard_map/down/pallas_call | solution.py:334
  29.0 2.0 %collective-permute-start.2 = (bf16[10,128,256]{2,1,0:T(8,128)(2,1)S(1)}, bf16[10,128,256]{2,1,0:T(8,128)(2,1)S(1)}, u32[]{:S(2)}, u32[]{:S(2)}) collective-permute-start(bf16[10,128,256]{2,1,0:T(8,128)(2,1)S(1)} %get-tuple-element.24), channel_id=1, source_target_pairs={{1,0},{2,1},{3,2},{4,3},{5,4},{6,5},{7,6},{8,7},{9,8},{10,9},{11,1... | collective-permute-start | bytes 1966088 | tf_op jit(solution)/shard_map/ppermute | solution.py:357
  30.9 0.0 collective-permute-done.rim_ref
  31.0 0.8 %rim_down.1 = (f32[4,128,256]{2,1,0:T(8,128)S(1)}, bf16[10,128,256]{2,1,0:T(8,128)(2,1)S(1)}, f32[1,128]{1,0:T(1,128)S(1)}) custom-call(bf16[6,256,128]{2,1,0:T(8,128)(2,1)S(1)} %collective-permute-done.rim_ref, bf16[3,3,128,256]{3,2,1,0:T(8,128)(2,1)S(1)} %get-tuple-element.18.third_ref, f32[4,128,256]{2,1,0:T(8,128)S(1)} %get-tuple-element.19.part_ref, ...), custom_call_target="tpu_custom_call" | custom-call | tf_op jit(solution)/shard_map/rim_down/pallas_call | solution.py:358
  31.8 0.0 copy-start.3
  31.8 0.0 copy-start.4
  31.8 3.7 %collective-permute-start.1 = (bf16[10,128,256]{2,1,0:T(8,128)(2,1)S(1)}, bf16[10,128,256]{2,1,0:T(8,128)(2,1)S(1)}, u32[]{:S(2)}, u32[]{:S(2)}) collective-permute-start(bf16[10,128,256]{2,1,0:T(8,128)(2,1)S(1)} %get-tuple-element.23), channel_id=1, source_target_pairs={{0,1},{1,2},{2,3},{3,4},{4,5},{5,6},{6,7},{7,8},{8,9},{9,10},{10,1... | collective-permute-start | bytes 1966088 | tf_op jit(solution)/shard_map/ppermute | solution.py:367
  35.5 0.1 collective-permute-start.3
  35.7 1.1 %collective-permute-done.3.other_ref = f32[1,128]{1,0:T(1,128)S(1)} collective-permute-done((f32[1,128]{1,0:T(1,128)S(1)}, f32[1,128]{1,0:T(1,128)S(1)}, u32[]{:S(2)}, u32[]{:S(2)}) %collective-permute-start.3) | collective-permute-done | bytes 544 | tf_op jit(solution)/shard_map/ppermute | solution.py:292
  36.8 15.6 %all_to_all.10.stats_ref = f32[64,1,256]{2,1,0:T(1,128)S(1)} all-to-all(f32[64,1,256]{2,1,0:T(1,128)S(1)} %both.2), channel_id=1, replica_groups=mesh['groups'=2,'ha_0'=8,'ha_1'=8,'ha_2'=2] {'ha_0','ha_1'}, dimensions={0} | all-to-all | bytes 131072 | tf_op jit(solution)/shard_map/all_to_all | solution.py:301
  52.4 0.0 collective-permute-done.2.below_ref
  52.4 0.0 collective-permute-done.1.above_ref
  52.4 0.0 copy-done
  52.4 0.0 copy-done.2
  52.4 0.0 copy-done.5
  52.4 0.0 copy-done.6
  52.4 4.8 %mix.1 = (f32[4,2,128,256]{3,2,1,0:T(8,128)S(1)}, bf16[2,2,128,256]{3,2,1,0:T(8,128)(2,1)}, f32[1,128]{1,0:T(1,128)S(1)}) custom-call(f32[4,128,256]{2,1,0:T(8,128)S(1)} %get-tuple-element.17.row_ref, f32[4,128,256]{2,1,0:T(8,128)S(1)} %get-tuple-element.22.last_ref, bf16[10,128,256]{2,1,0:T(8,128)(2,1)S(1)} %collective-permute-done.1.above_ref, ...), custom_call_target="tpu_custom_call" | custom-call | tf_op jit(solution)/shard_map/mix/pallas_call | solution.py:369
  57.2 1.5 %collective-permute-start.4 = (f32[1,128]{1,0:T(1,128)S(1)}, f32[1,128]{1,0:T(1,128)S(1)}, u32[]{:S(2)}, u32[]{:S(2)}) collective-permute-start(f32[1,128]{1,0:T(1,128)S(1)} %get-tuple-element.28.mine_ref), channel_id=1, source_target_pairs={{0,1},{1,0},{2,3},{3,2},{4,5},{5,4},{6,7},{7,6},{8,9},{9,8},{10,11... | collective-permute-start | bytes 1544 | tf_op jit(solution)/shard_map/ppermute | solution.py:292
  58.7 0.8 %collective-permute-done.4.other_ref = f32[1,128]{1,0:T(1,128)S(1)} collective-permute-done((f32[1,128]{1,0:T(1,128)S(1)}, f32[1,128]{1,0:T(1,128)S(1)}, u32[]{:S(2)}, u32[]{:S(2)}) %collective-permute-start.4) | collective-permute-done | bytes 544 | tf_op jit(solution)/shard_map/ppermute | solution.py:292
  59.6 15.5 %all_to_all.11.stats_ref = f32[64,1,256]{2,1,0:T(1,128)S(1)} all-to-all(f32[64,1,256]{2,1,0:T(1,128)S(1)} %both.3), channel_id=1, replica_groups=mesh['groups'=2,'ha_0'=8,'ha_1'=8,'ha_2'=2] {'ha_0','ha_1'}, dimensions={0} | all-to-all | bytes 131072 | tf_op jit(solution)/shard_map/all_to_all | solution.py:301
  75.1 0.0 copy-done.3
  75.1 0.0 copy-done.4
  75.1 1.3 %final.1 = bf16[4,2,128,256]{3,2,1,0:T(8,128)(2,1)} custom-call(f32[4,2,128,256]{3,2,1,0:T(8,128)S(1)} %get-tuple-element.27.second_ref, f32[64,1,256]{2,1,0:T(1,128)S(1)} %all_to_all.11.stats_ref, f32[1,256]{1,0:T(1,128)S(1)} %bitcast.6, f32[1,256]{1,0:T(1,128)S(1)} %bitcast.7), custom_call_target="tpu_custom_call" | custom-call | tf_op jit(solution)/shard_map/final/pallas_call | solution.py:382
  (3 shorter events, 0.0 us)
Async XLA Ops:
  1.7 29.3 %collective-permute-start = (bf16[6,256,128]{2,1,0:T(8,128)(2,1)S(1)}, bf16[6,256,128]{2,1,0:T(8,128)(2,1)S(1)}, u32[]{:S(2)}, u32[]{:S(2)}) collective-permute-start(bf16[6,256,128]{2,1,0:T(8,128)(2,1)S(1)} %rim.1), channel_id=1, source_target_pairs={{1,0},{2,1},{3,2},{4,3},{5,4},{6,5},{7,6},{8,7},{9,8},{10,9},{11,1... | collective-permute-start | bytes 1179656 | tf_op jit(solution)/shard_map/ppermute | solution.py:326
  24.2 1.0 %copy-start.1 = (bf16[2,2,128,256]{3,2,1,0:T(8,128)(2,1)S(1)}, bf16[2,2,128,256]{3,2,1,0:T(8,128)(2,1)}, u32[]{:S(2)}) copy-start(bf16[2,2,128,256]{3,2,1,0:T(8,128)(2,1)} %hidden_ref.2) | copy-start | bytes 786436
  25.1 27.2 %copy-start = (bf16[3,3,3,256,256]{4,3,2,1,0:T(8,128)(2,1)S(1)}, bf16[3,3,3,256,256]{4,3,2,1,0:T(8,128)(2,1)}, u32[]{:S(2)}) copy-start(bf16[3,3,3,256,256]{4,3,2,1,0:T(8,128)(2,1)} %kernel_ref.3) | copy-start | bytes 10616836
  25.1 27.3 %copy-start.2 = (bf16[2,2,128,256]{3,2,1,0:T(8,128)(2,1)S(1)}, bf16[2,2,128,256]{3,2,1,0:T(8,128)(2,1)}, u32[]{:S(2)}) copy-start(bf16[2,2,128,256]{3,2,1,0:T(8,128)(2,1)} %hidden_ref.2) | copy-start | bytes 786436
  25.2 27.3 %copy-start.5 = (f32[256]{0:T(256)S(1)}, f32[256]{0:T(256)}, u32[]{:S(2)}) copy-start(f32[256]{0:T(256)} %param.13) | copy-start | bytes 3076
  25.2 27.3 %copy-start.6 = (f32[256]{0:T(256)S(1)}, f32[256]{0:T(256)}, u32[]{:S(2)}) copy-start(f32[256]{0:T(256)} %param.14) | copy-start | bytes 3076
  29.0 23.4 %collective-permute-start.2 = (bf16[10,128,256]{2,1,0:T(8,128)(2,1)S(1)}, bf16[10,128,256]{2,1,0:T(8,128)(2,1)S(1)}, u32[]{:S(2)}, u32[]{:S(2)}) collective-permute-start(bf16[10,128,256]{2,1,0:T(8,128)(2,1)S(1)} %get-tuple-element.24), channel_id=1, source_target_pairs={{1,0},{2,1},{3,2},{4,3},{5,4},{6,5},{7,6},{8,7},{9,8},{10,9},{11,1... | collective-permute-start | bytes 1966088 | tf_op jit(solution)/shard_map/ppermute | solution.py:357
  31.8 43.3 %copy-start.3 = (f32[256]{0:T(256)S(1)}, f32[256]{0:T(256)}, u32[]{:S(2)}) copy-start(f32[256]{0:T(256)} %param.16) | copy-start | bytes 3076
  31.8 43.3 %copy-start.4 = (f32[256]{0:T(256)S(1)}, f32[256]{0:T(256)}, u32[]{:S(2)}) copy-start(f32[256]{0:T(256)} %param.17) | copy-start | bytes 3076
  31.8 20.6 %collective-permute-start.1 = (bf16[10,128,256]{2,1,0:T(8,128)(2,1)S(1)}, bf16[10,128,256]{2,1,0:T(8,128)(2,1)S(1)}, u32[]{:S(2)}, u32[]{:S(2)}) collective-permute-start(bf16[10,128,256]{2,1,0:T(8,128)(2,1)S(1)} %get-tuple-element.23), channel_id=1, source_target_pairs={{0,1},{1,2},{2,3},{3,4},{4,5},{5,6},{6,7},{7,8},{8,9},{9,10},{10,1... | collective-permute-start | bytes 1966088 | tf_op jit(solution)/shard_map/ppermute | solution.py:367
  35.5 1.3 %collective-permute-start.3 = (f32[1,128]{1,0:T(1,128)S(1)}, f32[1,128]{1,0:T(1,128)S(1)}, u32[]{:S(2)}, u32[]{:S(2)}) collective-permute-start(f32[1,128]{1,0:T(1,128)S(1)} %get-tuple-element.26.mine_ref), channel_id=1, source_target_pairs={{0,1},{1,0},{2,3},{3,2},{4,5},{5,4},{6,7},{7,6},{8,9},{9,8},{10,11... | collective-permute-start | bytes 1544 | tf_op jit(solution)/shard_map/ppermute | solution.py:292
  57.2 2.3 %collective-permute-start.4 = (f32[1,128]{1,0:T(1,128)S(1)}, f32[1,128]{1,0:T(1,128)S(1)}, u32[]{:S(2)}, u32[]{:S(2)}) collective-permute-start(f32[1,128]{1,0:T(1,128)S(1)} %get-tuple-element.28.mine_ref), channel_id=1, source_target_pairs={{0,1},{1,0},{2,3},{3,2},{4,5},{5,4},{6,7},{7,6},{8,9},{9,8},{10,11... | collective-permute-start | bytes 1544 | tf_op jit(solution)/shard_map/ppermute | solution.py:292

commit v4 on v3

--- a/solution.py
+++ b/solution.py
@@ -127,6 +127,7 @@
         pltpu.make_async_copy(video_ref, video_buf, sems.at[1]),
         pltpu.make_async_copy(kernel_ref.at[:, :2], kernel_buf, sems.at[2]),
         pltpu.make_async_copy(kernel_ref.at[:, 2], third_ref, sems.at[3]),
+        pltpu.make_async_copy(hidden_ref.at[:, 0], edge_ref.at[:cached], sems.at[4]),
     ]
     for c in loads:
         c.start()
@@ -138,8 +139,6 @@
         for r in range(rows):
             source = cache_buf.at[f, r] if f < cached else video_buf.at[f - cached, r]
             pair_up(source, pairs_ref.at[f, r], c_in)
-    for f in range(cached):
-        edge_ref[f] = hidden_ref[f, 0]
     loads[2].wait()
     loads[3].wait()
 
@@ -167,20 +166,21 @@
     center_ref[...] = center
     sums_ref[0:1] = total - center * (frames * half)
     sums_ref[1:2] = sum(column_sum((row_ref[t] - center) ** 2) for t in range(frames))
+    loads[4].wait()
 
 
 def rim_down_kernel(
     rim_ref, third_ref, part_ref, center_ref, sums_ref, hidden_ref,
     last_ref, edge_ref, message_ref,
-    pairs_ref,
+    pairs_ref, sem,
 ):
-    frames, half, c_out = part_ref.shape
+    frames, half, _ = part_ref.shape
     c_in = rim_ref.shape[-1]
     cached, rows = hidden_ref.shape[:2]
+    load = pltpu.make_async_copy(hidden_ref.at[:, rows - 1], edge_ref.at[:cached], sem)
+    load.start()
     for f in range(rim_ref.shape[0]):
         pair_up(rim_ref.at[f], pairs_ref.at[f], c_in)
-    for f in range(cached):
-        edge_ref[f] = hidden_ref[f, rows - 1]
     taps = [pairs_ref[a : a + frames].reshape(frames * half, 2 * c_in) for a in range(3)]
     both = jnp.concatenate([third_ref[a, c] for a in range(3) for c in range(2)], axis=0)
     ahead = jnp.concatenate([third_ref[a, 2] for a in range(3)], axis=0)
@@ -198,6 +198,7 @@
         sums = sums + column_sum(off)
         squares = squares + column_sum(off * off)
     message_ref[...] = moments_row(center, sums, squares, 2 * frames * half)
+    load.wait()
 
 
 def unpack(stats_ref):
@@ -208,17 +209,22 @@
 def mix_kernel(
     row_ref, last_ref, above_ref, below_ref, ends_ref, stats_ref, gain_ref, shift_ref, hidden_ref, kernel_ref,
     second_ref, next_ref, message_ref,
-    rows_ref, sem,
+    rows_ref, kernel_buf, sems,
 ):
     frames, width, channels = row_ref.shape
     cached = hidden_ref.shape[0]
     rows = 2
     count = rows * frames * width
+    load = pltpu.make_async_copy(hidden_ref, rows_ref.at[:cached, 1 : 1 + rows], sems.at[0])
+    load.start()
+    fetches = [
+        pltpu.make_async_copy(kernel_ref.at[:, :, c], kernel_buf.at[c], sems.at[2 + c]) for c in range(3)
+    ]
+    for f in fetches:
+        f.start()
     for f in range(cached):
         rows_ref[f, 0] = above_ref[f]
         rows_ref[f, rows + 1] = below_ref[f]
-        for i in range(rows):
-            rows_ref[f, 1 + i] = hidden_ref[f, i]
     center, factor = affine(unpack(stats_ref), count * (channels // GROUPS), gain_ref[...])
     offset = shift_ref[...]
     keep_above, keep_below = ends_ref[0:1], ends_ref[1:2]
@@ -231,14 +237,12 @@
         rows_ref[cached + t, 1] = silu_norm(row_ref[t], center, factor, offset).astype(BF16)
         rows_ref[cached + t, 2] = silu_norm(last_ref[t], center, factor, offset).astype(BF16)
 
-    weights = [
-        jnp.concatenate([kernel_ref[a, b, c] for a in range(3) for b in range(3)], axis=0)
-        for c in range(3)
-    ]
     step = frames // 2
     for begin in range(0, frames, step):
         for t in range(begin, begin + step):
             activate(t)
+        if begin == 0:
+            load.wait()
         taps = jnp.concatenate(
             [
                 rows_ref[begin + a : begin + a + step, b : b + rows].reshape(step * rows * width, channels)
@@ -247,7 +251,13 @@
             ],
             axis=1,
         )
-        left, here, right = (jnp.dot(taps, w, preferred_element_type=F32) for w in weights)
+        parts = []
+        for c in range(3):
+            if begin == 0:
+                fetches[c].wait()
+            weights = jnp.concatenate([kernel_buf[c, a, b] for a in range(3) for b in range(3)], axis=0)
+            parts.append(jnp.dot(taps, weights, preferred_element_type=F32))
+        left, here, right = parts
         for n in range(step * rows):
             span = slice(n * width, (n + 1) * width)
             t, i = begin + n // rows, n % rows
@@ -257,7 +267,7 @@
             total = sum(column_sum(b) for b in blocks)
             middle = group_sum(total) * (2.0 / (count * (channels // GROUPS)))
     store = pltpu.make_async_copy(
-        rows_ref.at[cached + frames - 2 : cached + frames, 1 : 1 + rows], next_ref, sem
+        rows_ref.at[cached + frames - 2 : cached + frames, 1 : 1 + rows], next_ref, sems.at[1]
     )
     store.start()
     offs = [second_ref[t, i] - middle for t in range(frames) for i in range(rows)]
@@ -306,8 +316,9 @@
     cached = cache_video.shape[0]
     c_out = kernel_down.shape[-1]
     half = width // 2
-    video, cache_video, kernel_down = (
-        pltpu.with_memory_space_constraint(x, pltpu.HBM) for x in (video, cache_video, kernel_down)
+    video, cache_video, cache_hidden, kernel_mix = (
+        pltpu.with_memory_space_constraint(x, pltpu.HBM)
+        for x in (video, cache_video, cache_hidden, kernel_mix)
     )
     devices = lax.axis_size(HA)
     place = lax.axis_index(HA)
@@ -327,7 +338,8 @@
     ends = jnp.broadcast_to(
         jnp.stack([place > 0, place < devices - 1]).astype(F32)[:, None], (2, c_out)
     )
-    cache_hidden, ends = lax.optimization_barrier((cache_hidden, ends))
+    kernel_down, ends = lax.optimization_barrier((kernel_down, ends))
+    kernel_down = pltpu.with_memory_space_constraint(kernel_down, pltpu.HBM)
     line = whole((frames, half, c_out), F32)
     edge = whole((cached + 2 * frames, half, c_out), BF16)
     message = whole((1, LANES), F32)
@@ -342,14 +354,14 @@
             whole((2, c_out), F32),
             edge,
         ),
-        in_specs=[HBM] * 3 + [AUTO],
+        in_specs=[HBM] * 4,
         out_specs=(AUTO,) * 6,
         scratch_shapes=[
             pltpu.VMEM(cache_video.shape, BF16),
             pltpu.VMEM(video.shape, BF16),
             pltpu.VMEM((3, 2, 3, c_in, c_out), BF16),
             pltpu.VMEM((cached + frames, rows, half, 2 * c_in), BF16),
-            DMA((4,)),
+            DMA((5,)),
         ],
         compiler_params=limit(24),
         cost_estimate=pl.CostEstimate(flops=2 * 10**9, bytes_accessed=4 * 10**6, transcendentals=0),
@@ -359,9 +371,9 @@
         rim_down_kernel,
         name="rim_down",
         out_shape=(line, edge, message),
-        in_specs=[AUTO] * 6,
+        in_specs=[AUTO] * 5 + [HBM],
         out_specs=(AUTO,) * 3,
-        scratch_shapes=[pltpu.VMEM((cached + frames, half, 2 * c_in), BF16)],
+        scratch_shapes=[pltpu.VMEM((cached + frames, half, 2 * c_in), BF16), DMA(())],
         compiler_params=limit(16),
     )(rim, third, part, center, sums, cache_hidden)
     above = lax.ppermute(above, HA, down)
@@ -370,11 +382,12 @@
         mix_kernel,
         name="mix",
         out_shape=(whole((frames, 2, half, c_out), F32), whole((2, 2, half, c_out), BF16), message),
-        in_specs=[AUTO] * 10,
+        in_specs=[AUTO] * 8 + [HBM] * 2,
         out_specs=(AUTO, ANY, AUTO),
         scratch_shapes=[
             pltpu.VMEM((cached + frames, 4, half, c_out), BF16),
-            DMA(()),
+            pltpu.VMEM((3, 3, 3, c_out, c_out), BF16),
+            DMA((5,)),
         ],
         compiler_params=limit(28),
     )(row, last, above, below, ends, stats, gain_down[None], shift_down[None], cache_hidden, kernel_mix)
@@ -396,6 +409,7 @@
         mesh.devices.reshape(mesh.shape["groups"], 8, 8, 2), ("groups", "ha_0", "ha_1", "ha_2")
     )
     strips = P("groups", HA, None, None)
+
     return jax.shard_map(
         local,
         mesh=split,

time: 76.7 us -> 78.6 us (1.025)
  Pallas kernels: 11.8 us -> 14.7 us
  local copies, waits for them, and re-layouts: 1.05 us -> 0.09 us
    pallas_call x1, Pallas kernels: 4.78 us -> 7.62 us  [local(): pl.pallas_call(mix_kernel, name='mix', out_shape=(whole((frames, 2, half,...]
    unnamed x14 -> x8, local copies, waits for them, and re-layouts: 0.98 us -> 0.02 us
where the time goes in v4:
time: 78.6 us; the launch traced here: 78.3 us
  blocking collectives  31.1 us (40%)
  starting transfers between devices  29.6 us (38%)
  Pallas kernels  14.7 us (19%)
  waiting for transfers between devices  1.96 us (2%)
    all_to_all x2, blocking collectives, everyone(): return lax.all_to_all(copies, HA[:-1], 0, 0)  31.1 us
    ppermute x1, starting transfers between devices, local(): rim = lax.ppermute(rim, HA, up)  22.4 us
    pallas_call x1, Pallas kernels, local(): pl.pallas_call(mix_kernel, name='mix', out_shape=(whole((frames, 2, half,...  7.62 us
    pallas_call x1, Pallas kernels, local(): pl.pallas_call(down_kernel, name='down', out_shape=(line, line, whole((3,...  3.7 us
    ppermute x1, starting transfers between devices, local(): above = lax.ppermute(above, HA, down)  3.67 us
    ppermute x2, waiting for transfers between devices, everyone(): other = lax.ppermute(message, HA, [(i, i ^ 1) for i in range(devices)])  1.95 us
    ppermute x1, starting transfers between devices, local(): below = lax.ppermute(below, HA, up)  1.95 us
    ppermute x2, starting transfers between devices, everyone(): other = lax.ppermute(message, HA, [(i, i ^ 1) for i in range(devices)])  1.64 us
  transfers between devices with their start and end apart: 5, of which 2 were waited for; matrix products, arithmetic and copies ran while one was open for 0% of the time, Pallas kernels for 6%

profile of v4, /device:TPU:513, one launch (start us, length us, event | category | flops | bytes accessed | tf_op | source)
XLA Modules:
  0.0 78.3 jit_solution(16717591821875450819)
XLA Ops:
  0.6 1.0 %rim.1 = bf16[6,256,128]{2,1,0:T(8,128)(2,1)S(1)} custom-call(bf16[2,4,256,128]{3,2,1,0:T(8,128)(2,1)} %cache_ref.3, bf16[4,4,256,128]{3,2,1,0:T(8,128)(2,1)} %video_ref.3), custom_call_target="tpu_custom_call" | custom-call | tf_op jit(solution)/shard_map/rim/pallas_call | solution.py:328
  1.7 22.4 %collective-permute-start = (bf16[6,256,128]{2,1,0:T(8,128)(2,1)S(1)}, bf16[6,256,128]{2,1,0:T(8,128)(2,1)S(1)}, u32[]{:S(2)}, u32[]{:S(2)}) collective-permute-start(bf16[6,256,128]{2,1,0:T(8,128)(2,1)S(1)} %rim.1), channel_id=1, source_target_pairs={{1,0},{2,1},{3,2},{4,3},{5,4},{6,5},{7,6},{8,7},{9,8},{10,9},{11,1... | collective-permute-start | bytes 1179656 | tf_op jit(solution)/shard_map/ppermute | solution.py:337
  24.0 0.1 add_convert_fusion
  24.1 0.1 broadcast_in_dim.18.ends_ref
  24.2 0.0 copy-start.2
  24.2 0.0 copy-start.3
  24.2 3.7 %down.1 = (f32[4,128,256]{2,1,0:T(8,128)S(1)}, f32[4,128,256]{2,1,0:T(8,128)S(1)}, bf16[3,3,128,256]{3,2,1,0:T(8,128)(2,1)S(1)}, f32[1,256]{1,0:T(1,128)S(1)}, f...) custom-call(bf16[2,4,256,128]{3,2,1,0:T(8,128)(2,1)} %cache_ref.3, bf16[4,4,256,128]{3,2,1,0:T(8,128)(2,1)} %video_ref.3, ...), custom_call_target="tpu_custom_call" | custom-call | flops 2000000000 | bytes 4000000 | tf_op jit(solution)/shard_map/down/pallas_call | solution.py:346
  27.9 2.0 %collective-permute-start.2 = (bf16[10,128,256]{2,1,0:T(8,128)(2,1)S(1)}, bf16[10,128,256]{2,1,0:T(8,128)(2,1)S(1)}, u32[]{:S(2)}, u32[]{:S(2)}) collective-permute-start(bf16[10,128,256]{2,1,0:T(8,128)(2,1)S(1)} %get-tuple-element.24), channel_id=1, source_target_pairs={{1,0},{2,1},{3,2},{4,3},{5,4},{6,5},{7,6},{8,7},{9,8},{10,9},{11,1... | collective-permute-start | bytes 1966088 | tf_op jit(solution)/shard_map/ppermute | solution.py:369
  29.9 0.0 collective-permute-done.rim_ref
  29.9 1.0 %rim_down.1 = (f32[4,128,256]{2,1,0:T(8,128)S(1)}, bf16[10,128,256]{2,1,0:T(8,128)(2,1)S(1)}, f32[1,128]{1,0:T(1,128)S(1)}) custom-call(bf16[6,256,128]{2,1,0:T(8,128)(2,1)S(1)} %collective-permute-done.rim_ref, bf16[3,3,128,256]{3,2,1,0:T(8,128)(2,1)S(1)} %get-tuple-element.18.third_ref, f32[4,128,256]{2,1,0:T(8,128)S(1)} %get-tuple-element.19.part_ref, ...), custom_call_target="tpu_custom_call" | custom-call | tf_op jit(solution)/shard_map/rim_down/pallas_call | solution.py:370
  30.8 0.0 copy-start
  30.9 0.0 copy-start.1
  30.9 3.7 %collective-permute-start.1 = (bf16[10,128,256]{2,1,0:T(8,128)(2,1)S(1)}, bf16[10,128,256]{2,1,0:T(8,128)(2,1)S(1)}, u32[]{:S(2)}, u32[]{:S(2)}) collective-permute-start(bf16[10,128,256]{2,1,0:T(8,128)(2,1)S(1)} %get-tuple-element.23), channel_id=1, source_target_pairs={{0,1},{1,2},{2,3},{3,4},{4,5},{5,6},{6,7},{7,8},{8,9},{9,10},{10,1... | collective-permute-start | bytes 1966088 | tf_op jit(solution)/shard_map/ppermute | solution.py:379
  34.5 0.1 collective-permute-start.3
  34.7 1.1 %collective-permute-done.3.other_ref = f32[1,128]{1,0:T(1,128)S(1)} collective-permute-done((f32[1,128]{1,0:T(1,128)S(1)}, f32[1,128]{1,0:T(1,128)S(1)}, u32[]{:S(2)}, u32[]{:S(2)}) %collective-permute-start.3) | collective-permute-done | bytes 544 | tf_op jit(solution)/shard_map/ppermute | solution.py:302
  35.9 15.6 %all_to_all.10.stats_ref = f32[64,1,256]{2,1,0:T(1,128)S(1)} all-to-all(f32[64,1,256]{2,1,0:T(1,128)S(1)} %both.2), channel_id=1, replica_groups=mesh['groups'=2,'ha_0'=8,'ha_1'=8,'ha_2'=2] {'ha_0','ha_1'}, dimensions={0} | all-to-all | bytes 131072 | tf_op jit(solution)/shard_map/all_to_all | solution.py:311
  51.4 0.0 collective-permute-done.2.below_ref
  51.4 0.0 collective-permute-done.1.above_ref
  51.4 0.0 copy-done.2
  51.4 0.0 copy-done.3
  51.5 7.6 %mix.1 = (f32[4,2,128,256]{3,2,1,0:T(8,128)S(1)}, bf16[2,2,128,256]{3,2,1,0:T(8,128)(2,1)}, f32[1,128]{1,0:T(1,128)S(1)}) custom-call(f32[4,128,256]{2,1,0:T(8,128)S(1)} %get-tuple-element.17.row_ref, f32[4,128,256]{2,1,0:T(8,128)S(1)} %get-tuple-element.22.last_ref, bf16[10,128,256]{2,1,0:T(8,128)(2,1)S(1)} %collective-permute-done.1.above_ref, ...), custom_call_target="tpu_custom_call" | custom-call | tf_op jit(solution)/shard_map/mix/pallas_call | solution.py:381
  59.1 1.5 %collective-permute-start.4 = (f32[1,128]{1,0:T(1,128)S(1)}, f32[1,128]{1,0:T(1,128)S(1)}, u32[]{:S(2)}, u32[]{:S(2)}) collective-permute-start(f32[1,128]{1,0:T(1,128)S(1)} %get-tuple-element.28.mine_ref), channel_id=1, source_target_pairs={{0,1},{1,0},{2,3},{3,2},{4,5},{5,4},{6,7},{7,6},{8,9},{9,8},{10,11... | collective-permute-start | bytes 1544 | tf_op jit(solution)/shard_map/ppermute | solution.py:302
  60.6 0.8 %collective-permute-done.4.other_ref = f32[1,128]{1,0:T(1,128)S(1)} collective-permute-done((f32[1,128]{1,0:T(1,128)S(1)}, f32[1,128]{1,0:T(1,128)S(1)}, u32[]{:S(2)}, u32[]{:S(2)}) %collective-permute-start.4) | collective-permute-done | bytes 544 | tf_op jit(solution)/shard_map/ppermute | solution.py:302
  61.4 15.5 %all_to_all.11.stats_ref = f32[64,1,256]{2,1,0:T(1,128)S(1)} all-to-all(f32[64,1,256]{2,1,0:T(1,128)S(1)} %both.3), channel_id=1, replica_groups=mesh['groups'=2,'ha_0'=8,'ha_1'=8,'ha_2'=2] {'ha_0','ha_1'}, dimensions={0} | all-to-all | bytes 131072 | tf_op jit(solution)/shard_map/all_to_all | solution.py:311
  77.0 0.0 copy-done
  77.0 0.0 copy-done.1
  77.0 1.3 %final.1 = bf16[4,2,128,256]{3,2,1,0:T(8,128)(2,1)} custom-call(f32[4,2,128,256]{3,2,1,0:T(8,128)S(1)} %get-tuple-element.27.second_ref, f32[64,1,256]{2,1,0:T(1,128)S(1)} %all_to_all.11.stats_ref, f32[1,256]{1,0:T(1,128)S(1)} %bitcast.6, f32[1,256]{1,0:T(1,128)S(1)} %bitcast.7), custom_call_target="tpu_custom_call" | custom-call | tf_op jit(solution)/shard_map/final/pallas_call | solution.py:395
  (2 shorter events, 0.0 us)
Async XLA Ops:
  1.7 28.2 %collective-permute-start = (bf16[6,256,128]{2,1,0:T(8,128)(2,1)S(1)}, bf16[6,256,128]{2,1,0:T(8,128)(2,1)S(1)}, u32[]{:S(2)}, u32[]{:S(2)}) collective-permute-start(bf16[6,256,128]{2,1,0:T(8,128)(2,1)S(1)} %rim.1), channel_id=1, source_target_pairs={{1,0},{2,1},{3,2},{4,3},{5,4},{6,5},{7,6},{8,7},{9,8},{10,9},{11,1... | collective-permute-start | bytes 1179656 | tf_op jit(solution)/shard_map/ppermute | solution.py:337
  24.2 27.2 %copy-start.2 = (f32[256]{0:T(256)S(1)}, f32[256]{0:T(256)}, u32[]{:S(2)}) copy-start(f32[256]{0:T(256)} %param.13) | copy-start | bytes 3076
  24.2 27.2 %copy-start.3 = (f32[256]{0:T(256)S(1)}, f32[256]{0:T(256)}, u32[]{:S(2)}) copy-start(f32[256]{0:T(256)} %param.14) | copy-start | bytes 3076
  27.9 23.5 %collective-permute-start.2 = (bf16[10,128,256]{2,1,0:T(8,128)(2,1)S(1)}, bf16[10,128,256]{2,1,0:T(8,128)(2,1)S(1)}, u32[]{:S(2)}, u32[]{:S(2)}) collective-permute-start(bf16[10,128,256]{2,1,0:T(8,128)(2,1)S(1)} %get-tuple-element.24), channel_id=1, source_target_pairs={{1,0},{2,1},{3,2},{4,3},{5,4},{6,5},{7,6},{8,7},{9,8},{10,9},{11,1... | collective-permute-start | bytes 1966088 | tf_op jit(solution)/shard_map/ppermute | solution.py:369
  30.8 46.1 %copy-start = (f32[256]{0:T(256)S(1)}, f32[256]{0:T(256)}, u32[]{:S(2)}) copy-start(f32[256]{0:T(256)} %param.16) | copy-start | bytes 3076
  30.9 46.1 %copy-start.1 = (f32[256]{0:T(256)S(1)}, f32[256]{0:T(256)}, u32[]{:S(2)}) copy-start(f32[256]{0:T(256)} %param.17) | copy-start | bytes 3076
  30.9 20.6 %collective-permute-start.1 = (bf16[10,128,256]{2,1,0:T(8,128)(2,1)S(1)}, bf16[10,128,256]{2,1,0:T(8,128)(2,1)S(1)}, u32[]{:S(2)}, u32[]{:S(2)}) collective-permute-start(bf16[10,128,256]{2,1,0:T(8,128)(2,1)S(1)} %get-tuple-element.23), channel_id=1, source_target_pairs={{0,1},{1,2},{2,3},{3,4},{4,5},{5,6},{6,7},{7,8},{8,9},{9,10},{10,1... | collective-permute-start | bytes 1966088 | tf_op jit(solution)/shard_map/ppermute | solution.py:379
  34.5 1.3 %collective-permute-start.3 = (f32[1,128]{1,0:T(1,128)S(1)}, f32[1,128]{1,0:T(1,128)S(1)}, u32[]{:S(2)}, u32[]{:S(2)}) collective-permute-start(f32[1,128]{1,0:T(1,128)S(1)} %get-tuple-element.26.mine_ref), channel_id=1, source_target_pairs={{0,1},{1,0},{2,3},{3,2},{4,5},{5,4},{6,7},{7,6},{8,9},{9,8},{10,11... | collective-permute-start | bytes 1544 | tf_op jit(solution)/shard_map/ppermute | solution.py:302
  59.1 2.3 %collective-permute-start.4 = (f32[1,128]{1,0:T(1,128)S(1)}, f32[1,128]{1,0:T(1,128)S(1)}, u32[]{:S(2)}, u32[]{:S(2)}) collective-permute-start(f32[1,128]{1,0:T(1,128)S(1)} %get-tuple-element.28.mine_ref), channel_id=1, source_target_pairs={{0,1},{1,0},{2,3},{3,2},{4,5},{5,4},{6,7},{7,6},{8,9},{9,8},{10,11... | collective-permute-start | bytes 1544 | tf_op jit(solution)/shard_map/ppermute | solution.py:302

commit v5 on v4

--- a/solution.py
+++ b/solution.py
@@ -170,7 +170,7 @@
 
 
 def rim_down_kernel(
-    rim_ref, third_ref, part_ref, center_ref, sums_ref, hidden_ref,
+    rim_ref, ends_ref, third_ref, part_ref, center_ref, sums_ref, hidden_ref,
     last_ref, edge_ref, message_ref,
     pairs_ref, sem,
 ):
@@ -187,11 +187,12 @@
     here = jnp.dot(jnp.concatenate(taps, axis=1), both, preferred_element_type=F32)
     evens = jnp.concatenate([t[:, :c_in] for t in taps], axis=1)
     after = jnp.dot(evens, ahead, preferred_element_type=F32)
+    keep = ends_ref[1:2]
     center = center_ref[...]
     sums, squares = sums_ref[0:1], sums_ref[1:2]
     for t in range(frames):
         span = slice(t * half, (t + 1) * half)
-        block = part_ref[t] + here[span] + shift_back(after[span])
+        block = part_ref[t] + jnp.where(keep > 0, here[span] + shift_back(after[span]), 0.0)
         last_ref[t] = block
         edge_ref[cached + t], edge_ref[cached + frames + t] = split_in_two(block)
         off = block - center
@@ -209,7 +210,7 @@
 def mix_kernel(
     row_ref, last_ref, above_ref, below_ref, ends_ref, stats_ref, gain_ref, shift_ref, hidden_ref, kernel_ref,
     second_ref, next_ref, message_ref,
-    rows_ref, kernel_buf, sems,
+    rows_ref, sems,
 ):
     frames, width, channels = row_ref.shape
     cached = hidden_ref.shape[0]
@@ -217,17 +218,12 @@
     count = rows * frames * width
     load = pltpu.make_async_copy(hidden_ref, rows_ref.at[:cached, 1 : 1 + rows], sems.at[0])
     load.start()
-    fetches = [
-        pltpu.make_async_copy(kernel_ref.at[:, :, c], kernel_buf.at[c], sems.at[2 + c]) for c in range(3)
-    ]
-    for f in fetches:
-        f.start()
+    keep_above, keep_below = ends_ref[0:1], ends_ref[1:2]
     for f in range(cached):
-        rows_ref[f, 0] = above_ref[f]
-        rows_ref[f, rows + 1] = below_ref[f]
+        rows_ref[f, 0] = jnp.where(keep_above > 0, above_ref[f].astype(F32), 0.0).astype(BF16)
+        rows_ref[f, rows + 1] = jnp.where(keep_below > 0, below_ref[f].astype(F32), 0.0).astype(BF16)
     center, factor = affine(unpack(stats_ref), count * (channels // GROUPS), gain_ref[...])
     offset = shift_ref[...]
-    keep_above, keep_below = ends_ref[0:1], ends_ref[1:2]
 
     def activate(t):
         for at, edge_ref, keep in ((0, above_ref, keep_above), (rows + 1, below_ref, keep_below)):
@@ -253,9 +249,7 @@
         )
         parts = []
         for c in range(3):
-            if begin == 0:
-                fetches[c].wait()
-            weights = jnp.concatenate([kernel_buf[c, a, b] for a in range(3) for b in range(3)], axis=0)
+            weights = jnp.concatenate([kernel_ref[a, b, c] for a in range(3) for b in range(3)], axis=0)
             parts.append(jnp.dot(taps, weights, preferred_element_type=F32))
         left, here, right = parts
         for n in range(step * rows):
@@ -316,14 +310,13 @@
     cached = cache_video.shape[0]
     c_out = kernel_down.shape[-1]
     half = width // 2
-    video, cache_video, cache_hidden, kernel_mix = (
-        pltpu.with_memory_space_constraint(x, pltpu.HBM)
-        for x in (video, cache_video, cache_hidden, kernel_mix)
+    video, cache_video, cache_hidden = (
+        pltpu.with_memory_space_constraint(x, pltpu.HBM) for x in (video, cache_video, cache_hidden)
     )
     devices = lax.axis_size(HA)
     place = lax.axis_index(HA)
-    up = [(i + 1, i) for i in range(devices - 1)]
-    down = [(i, i + 1) for i in range(devices - 1)]
+    up = [((i + 1) % devices, i) for i in range(devices)]
+    down = [(i, (i + 1) % devices) for i in range(devices)]
     whole = jax.ShapeDtypeStruct
     rim = pl.pallas_call(
         rim_kernel,
@@ -371,23 +364,22 @@
         rim_down_kernel,
         name="rim_down",
         out_shape=(line, edge, message),
-        in_specs=[AUTO] * 5 + [HBM],
+        in_specs=[AUTO] * 6 + [HBM],
         out_specs=(AUTO,) * 3,
         scratch_shapes=[pltpu.VMEM((cached + frames, half, 2 * c_in), BF16), DMA(())],
         compiler_params=limit(16),
-    )(rim, third, part, center, sums, cache_hidden)
+    )(rim, ends, third, part, center, sums, cache_hidden)
     above = lax.ppermute(above, HA, down)
     stats = everyone(stats)
     second, next_cache, stats = pl.pallas_call(
         mix_kernel,
         name="mix",
         out_shape=(whole((frames, 2, half, c_out), F32), whole((2, 2, half, c_out), BF16), message),
-        in_specs=[AUTO] * 8 + [HBM] * 2,
+        in_specs=[AUTO] * 8 + [HBM, AUTO],
         out_specs=(AUTO, ANY, AUTO),
         scratch_shapes=[
             pltpu.VMEM((cached + frames, 4, half, c_out), BF16),
-            pltpu.VMEM((3, 3, 3, c_out, c_out), BF16),
-            DMA((5,)),
+            DMA((2,)),
         ],
         compiler_params=limit(28),
     )(row, last, above, below, ends, stats, gain_down[None], shift_down[None], cache_hidden, kernel_mix)

time: 78.6 us -> 74.7 us (0.950)
  starting transfers between devices: 29.6 us -> 24.2 us
  blocking collectives: 31.1 us -> 34.4 us
  Pallas kernels: 14.7 us -> 13 us
    all_to_all x2, blocking collectives: 31.1 us -> 34.4 us  [everyone(): return lax.all_to_all(copies, HA[:-1], 0, 0)]
    pallas_call x1, Pallas kernels: 7.62 us -> 5.66 us  [local(): pl.pallas_call(mix_kernel, name='mix', out_shape=(whole((frames, 2, half,...]
    ppermute x1, starting transfers between devices: 3.67 us -> 1.82 us  [local(): above = lax.ppermute(above, HA, down)]
    ppermute x1, starting transfers between devices: 22.4 us -> 20.5 us  [local(): rim = lax.ppermute(rim, HA, up)]
    ppermute x1, starting transfers between devices: 1.95 us -> 0.15 us  [local(): below = lax.ppermute(below, HA, up)]
  transfers between devices with their start and end apart: 5 -> 5, of which waited for: 2 -> 2; matrix products, arithmetic and copies ran while one was open for 0% -> 0% of each run, Pallas kernels for 6% -> 7%
where the time goes in v5:
time: 74.7 us; the launch traced here: 74.4 us
  blocking collectives  34.4 us (46%)
  starting transfers between devices  24.2 us (32%)
  Pallas kernels  13 us (17%)
  waiting for transfers between devices  1.99 us (3%)
    all_to_all x2, blocking collectives, everyone(): return lax.all_to_all(copies, HA[:-1], 0, 0)  34.4 us
    ppermute x1, starting transfers between devices, local(): rim = lax.ppermute(rim, HA, up)  20.5 us
    pallas_call x1, Pallas kernels, local(): pl.pallas_call(mix_kernel, name='mix', out_shape=(whole((frames, 2, half,...  5.66 us
    pallas_call x1, Pallas kernels, local(): pl.pallas_call(down_kernel, name='down', out_shape=(line, line, whole((3,...  3.82 us
    ppermute x2, waiting for transfers between devices, everyone(): other = lax.ppermute(message, HA, [(i, i ^ 1) for i in range(devices)])  1.98 us
    ppermute x1, starting transfers between devices, local(): above = lax.ppermute(above, HA, down)  1.82 us
    ppermute x2, starting transfers between devices, everyone(): other = lax.ppermute(message, HA, [(i, i ^ 1) for i in range(devices)])  1.69 us
  transfers between devices with their start and end apart: 5, of which 2 were waited for; matrix products, arithmetic and copies ran while one was open for 0% of the time, Pallas kernels for 7%

profile of v5, /device:TPU:513, one launch (start us, length us, event | category | flops | bytes accessed | tf_op | source)
XLA Modules:
  0.0 74.4 jit_solution(4356740620835155928)
XLA Ops:
  0.6 1.0 %rim.1 = bf16[6,256,128]{2,1,0:T(8,128)(2,1)S(1)} custom-call(bf16[2,4,256,128]{3,2,1,0:T(8,128)(2,1)} %cache_ref.3, bf16[4,4,256,128]{3,2,1,0:T(8,128)(2,1)} %video_ref.3), custom_call_target="tpu_custom_call" | custom-call | tf_op jit(solution)/shard_map/rim/pallas_call | solution.py:321
  1.7 20.5 %collective-permute-start = (bf16[6,256,128]{2,1,0:T(8,128)(2,1)S(1)}, bf16[6,256,128]{2,1,0:T(8,128)(2,1)S(1)}, u32[]{:S(2)}, u32[]{:S(2)}) collective-permute-start(bf16[6,256,128]{2,1,0:T(8,128)(2,1)S(1)} %rim.1), channel_id=1, source_target_pairs={{1,0},{2,1},{3,2},{4,3},{5,4},{6,5},{7,6},{8,7},{9,8},{10,9},{11,1... | collective-permute-start | bytes 1179656 | tf_op jit(solution)/shard_map/ppermute | solution.py:330
  22.2 0.1 add_convert_fusion
  22.3 0.1 broadcast_in_dim.18.ends_ref
  22.4 0.0 copy-start
  22.4 0.0 copy-start.3
  22.4 0.0 copy-start.4
  22.4 3.8 %down.1 = (f32[4,128,256]{2,1,0:T(8,128)S(1)}, f32[4,128,256]{2,1,0:T(8,128)S(1)}, bf16[3,3,128,256]{3,2,1,0:T(8,128)(2,1)S(1)}, f32[1,256]{1,0:T(1,128)S(1)}, f...) custom-call(bf16[2,4,256,128]{3,2,1,0:T(8,128)(2,1)} %cache_ref.3, bf16[4,4,256,128]{3,2,1,0:T(8,128)(2,1)} %video_ref.3, ...), custom_call_target="tpu_custom_call" | custom-call | flops 2000000000 | bytes 4000000 | tf_op jit(solution)/shard_map/down/pallas_call | solution.py:339
  26.2 0.2 collective-permute-start.2
  26.3 0.0 collective-permute-done.rim_ref
  26.3 1.1 %rim_down.1 = (f32[4,128,256]{2,1,0:T(8,128)S(1)}, bf16[10,128,256]{2,1,0:T(8,128)(2,1)S(1)}, f32[1,128]{1,0:T(1,128)S(1)}) custom-call(bf16[6,256,128]{2,1,0:T(8,128)(2,1)S(1)} %collective-permute-done.rim_ref, f32[2,256]{1,0:T(2,128)S(1)} %broadcast_in_dim.18.ends_ref, bf16[3,3,128,256]{3,2,1,0:T(8,128)(2,1)S(1)} %get-tuple-element.19.third_ref, ...), custom_call_target="tpu_custom_call" | custom-call | tf_op jit(solution)/shard_map/rim_down/pallas_call | solution.py:363
  27.4 0.0 copy-start.1
  27.5 0.0 copy-start.2
  27.5 1.8 %collective-permute-start.1 = (bf16[10,128,256]{2,1,0:T(8,128)(2,1)S(1)}, bf16[10,128,256]{2,1,0:T(8,128)(2,1)S(1)}, u32[]{:S(2)}, u32[]{:S(2)}) collective-permute-start(bf16[10,128,256]{2,1,0:T(8,128)(2,1)S(1)} %get-tuple-element.24), channel_id=1, source_target_pairs={{0,1},{1,2},{2,3},{3,4},{4,5},{5,6},{6,7},{7,8},{8,9},{9,10},{10,1... | collective-permute-start | bytes 1966088 | tf_op jit(solution)/shard_map/ppermute | solution.py:372
  29.3 0.0 collective-permute-start.3
  29.3 1.2 %collective-permute-done.3.other_ref = f32[1,128]{1,0:T(1,128)S(1)} collective-permute-done((f32[1,128]{1,0:T(1,128)S(1)}, f32[1,128]{1,0:T(1,128)S(1)}, u32[]{:S(2)}, u32[]{:S(2)}) %collective-permute-start.3) | collective-permute-done | bytes 544 | tf_op jit(solution)/shard_map/ppermute | solution.py:296
  30.5 18.9 %all_to_all.10.stats_ref = f32[64,1,256]{2,1,0:T(1,128)S(1)} all-to-all(f32[64,1,256]{2,1,0:T(1,128)S(1)} %both.2), channel_id=1, replica_groups=mesh['groups'=2,'ha_0'=8,'ha_1'=8,'ha_2'=2] {'ha_0','ha_1'}, dimensions={0} | all-to-all | bytes 131072 | tf_op jit(solution)/shard_map/all_to_all | solution.py:305
  49.3 0.0 collective-permute-done.2.below_ref
  49.3 0.0 collective-permute-done.1.above_ref
  49.3 0.0 copy-done
  49.3 0.0 copy-done.3
  49.4 0.0 copy-done.4
  49.4 5.7 %mix.1 = (f32[4,2,128,256]{3,2,1,0:T(8,128)S(1)}, bf16[2,2,128,256]{3,2,1,0:T(8,128)(2,1)}, f32[1,128]{1,0:T(1,128)S(1)}) custom-call(f32[4,128,256]{2,1,0:T(8,128)S(1)} %get-tuple-element.17.row_ref, f32[4,128,256]{2,1,0:T(8,128)S(1)} %get-tuple-element.23.last_ref, bf16[10,128,256]{2,1,0:T(8,128)(2,1)S(1)} %collective-permute-done.1.above_ref, ...), custom_call_target="tpu_custom_call" | custom-call | tf_op jit(solution)/shard_map/mix/pallas_call | solution.py:374
  55.0 1.7 %collective-permute-start.4 = (f32[1,128]{1,0:T(1,128)S(1)}, f32[1,128]{1,0:T(1,128)S(1)}, u32[]{:S(2)}, u32[]{:S(2)}) collective-permute-start(f32[1,128]{1,0:T(1,128)S(1)} %get-tuple-element.28.mine_ref), channel_id=1, source_target_pairs={{0,1},{1,0},{2,3},{3,2},{4,5},{5,4},{6,7},{7,6},{8,9},{9,8},{10,11... | collective-permute-start | bytes 1544 | tf_op jit(solution)/shard_map/ppermute | solution.py:296
  56.7 0.8 %collective-permute-done.4.other_ref = f32[1,128]{1,0:T(1,128)S(1)} collective-permute-done((f32[1,128]{1,0:T(1,128)S(1)}, f32[1,128]{1,0:T(1,128)S(1)}, u32[]{:S(2)}, u32[]{:S(2)}) %collective-permute-start.4) | collective-permute-done | bytes 544 | tf_op jit(solution)/shard_map/ppermute | solution.py:296
  57.6 15.5 %all_to_all.11.stats_ref = f32[64,1,256]{2,1,0:T(1,128)S(1)} all-to-all(f32[64,1,256]{2,1,0:T(1,128)S(1)} %both.3), channel_id=1, replica_groups=mesh['groups'=2,'ha_0'=8,'ha_1'=8,'ha_2'=2] {'ha_0','ha_1'}, dimensions={0} | all-to-all | bytes 131072 | tf_op jit(solution)/shard_map/all_to_all | solution.py:305
  73.1 0.0 copy-done.1
  73.1 0.0 copy-done.2
  73.1 1.3 %final.1 = bf16[4,2,128,256]{3,2,1,0:T(8,128)(2,1)} custom-call(f32[4,2,128,256]{3,2,1,0:T(8,128)S(1)} %get-tuple-element.27.second_ref, f32[64,1,256]{2,1,0:T(1,128)S(1)} %all_to_all.11.stats_ref, f32[1,256]{1,0:T(1,128)S(1)} %bitcast.6, f32[1,256]{1,0:T(1,128)S(1)} %bitcast.7), custom_call_target="tpu_custom_call" | custom-call | tf_op jit(solution)/shard_map/final/pallas_call | solution.py:387
  (2 shorter events, 0.0 us)
Async XLA Ops:
  1.7 24.7 %collective-permute-start = (bf16[6,256,128]{2,1,0:T(8,128)(2,1)S(1)}, bf16[6,256,128]{2,1,0:T(8,128)(2,1)S(1)}, u32[]{:S(2)}, u32[]{:S(2)}) collective-permute-start(bf16[6,256,128]{2,1,0:T(8,128)(2,1)S(1)} %rim.1), channel_id=1, source_target_pairs={{1,0},{2,1},{3,2},{4,3},{5,4},{6,5},{7,6},{8,7},{9,8},{10,9},{11,1... | collective-permute-start | bytes 1179656 | tf_op jit(solution)/shard_map/ppermute | solution.py:330
  22.4 27.0 %copy-start = (bf16[3,3,3,256,256]{4,3,2,1,0:T(8,128)(2,1)S(1)}, bf16[3,3,3,256,256]{4,3,2,1,0:T(8,128)(2,1)}, u32[]{:S(2)}) copy-start(bf16[3,3,3,256,256]{4,3,2,1,0:T(8,128)(2,1)} %kernel_ref.2) | copy-start | bytes 10616836
  22.4 27.0 %copy-start.3 = (f32[256]{0:T(256)S(1)}, f32[256]{0:T(256)}, u32[]{:S(2)}) copy-start(f32[256]{0:T(256)} %param.13) | copy-start | bytes 3076
  22.4 27.0 %copy-start.4 = (f32[256]{0:T(256)S(1)}, f32[256]{0:T(256)}, u32[]{:S(2)}) copy-start(f32[256]{0:T(256)} %param.14) | copy-start | bytes 3076
  26.2 23.1 %collective-permute-start.2 = (bf16[10,128,256]{2,1,0:T(8,128)(2,1)S(1)}, bf16[10,128,256]{2,1,0:T(8,128)(2,1)S(1)}, u32[]{:S(2)}, u32[]{:S(2)}) collective-permute-start(bf16[10,128,256]{2,1,0:T(8,128)(2,1)S(1)} %get-tuple-element.25), channel_id=1, source_target_pairs={{1,0},{2,1},{3,2},{4,3},{5,4},{6,5},{7,6},{8,7},{9,8},{10,9},{11,1... | collective-permute-start | bytes 1966088 | tf_op jit(solution)/shard_map/ppermute | solution.py:362
  27.4 45.7 %copy-start.1 = (f32[256]{0:T(256)S(1)}, f32[256]{0:T(256)}, u32[]{:S(2)}) copy-start(f32[256]{0:T(256)} %param.16) | copy-start | bytes 3076
  27.5 45.7 %copy-start.2 = (f32[256]{0:T(256)S(1)}, f32[256]{0:T(256)}, u32[]{:S(2)}) copy-start(f32[256]{0:T(256)} %param.17) | copy-start | bytes 3076
  27.5 21.9 %collective-permute-start.1 = (bf16[10,128,256]{2,1,0:T(8,128)(2,1)S(1)}, bf16[10,128,256]{2,1,0:T(8,128)(2,1)S(1)}, u32[]{:S(2)}, u32[]{:S(2)}) collective-permute-start(bf16[10,128,256]{2,1,0:T(8,128)(2,1)S(1)} %get-tuple-element.24), channel_id=1, source_target_pairs={{0,1},{1,2},{2,3},{3,4},{4,5},{5,6},{6,7},{7,8},{8,9},{9,10},{10,1... | collective-permute-start | bytes 1966088 | tf_op jit(solution)/shard_map/ppermute | solution.py:372
  29.3 1.2 %collective-permute-start.3 = (f32[1,128]{1,0:T(1,128)S(1)}, f32[1,128]{1,0:T(1,128)S(1)}, u32[]{:S(2)}, u32[]{:S(2)}) collective-permute-start(f32[1,128]{1,0:T(1,128)S(1)} %get-tuple-element.26.mine_ref), channel_id=1, source_target_pairs={{0,1},{1,0},{2,3},{3,2},{4,5},{5,4},{6,7},{7,6},{8,9},{9,8},{10,11... | collective-permute-start | bytes 1544 | tf_op jit(solution)/shard_map/ppermute | solution.py:296
  55.0 2.5 %collective-permute-start.4 = (f32[1,128]{1,0:T(1,128)S(1)}, f32[1,128]{1,0:T(1,128)S(1)}, u32[]{:S(2)}, u32[]{:S(2)}) collective-permute-start(f32[1,128]{1,0:T(1,128)S(1)} %get-tuple-element.28.mine_ref), channel_id=1, source_target_pairs={{0,1},{1,0},{2,3},{3,2},{4,5},{5,4},{6,7},{7,6},{8,9},{9,8},{10,11... | collective-permute-start | bytes 1544 | tf_op jit(solution)/shard_map/ppermute | solution.py:296

commit v6 on v5

--- a/solution.py
+++ b/solution.py
@@ -172,13 +172,13 @@
 def rim_down_kernel(
     rim_ref, ends_ref, third_ref, part_ref, center_ref, sums_ref, hidden_ref,
     last_ref, edge_ref, message_ref,
-    pairs_ref, sem,
+    pairs_ref,
 ):
     frames, half, _ = part_ref.shape
     c_in = rim_ref.shape[-1]
     cached, rows = hidden_ref.shape[:2]
-    load = pltpu.make_async_copy(hidden_ref.at[:, rows - 1], edge_ref.at[:cached], sem)
-    load.start()
+    for f in range(cached):
+        edge_ref[f] = hidden_ref[f, rows - 1]
     for f in range(rim_ref.shape[0]):
         pair_up(rim_ref.at[f], pairs_ref.at[f], c_in)
     taps = [pairs_ref[a : a + frames].reshape(frames * half, 2 * c_in) for a in range(3)]
@@ -199,7 +199,6 @@
         sums = sums + column_sum(off)
         squares = squares + column_sum(off * off)
     message_ref[...] = moments_row(center, sums, squares, 2 * frames * half)
-    load.wait()
 
 
 def unpack(stats_ref):
@@ -210,18 +209,19 @@
 def mix_kernel(
     row_ref, last_ref, above_ref, below_ref, ends_ref, stats_ref, gain_ref, shift_ref, hidden_ref, kernel_ref,
     second_ref, next_ref, message_ref,
-    rows_ref, sems,
+    rows_ref, sem,
 ):
     frames, width, channels = row_ref.shape
     cached = hidden_ref.shape[0]
     rows = 2
     count = rows * frames * width
-    load = pltpu.make_async_copy(hidden_ref, rows_ref.at[:cached, 1 : 1 + rows], sems.at[0])
-    load.start()
+    for f in range(cached):
+        for i in range(rows):
+            rows_ref[f, 1 + i] = hidden_ref[f, i]
     keep_above, keep_below = ends_ref[0:1], ends_ref[1:2]
     for f in range(cached):
-        rows_ref[f, 0] = jnp.where(keep_above > 0, above_ref[f].astype(F32), 0.0).astype(BF16)
-        rows_ref[f, rows + 1] = jnp.where(keep_below > 0, below_ref[f].astype(F32), 0.0).astype(BF16)
+        rows_ref[f, 0] = above_ref[f] * keep_above.astype(BF16)
+        rows_ref[f, rows + 1] = below_ref[f] * keep_below.astype(BF16)
     center, factor = affine(unpack(stats_ref), count * (channels // GROUPS), gain_ref[...])
     offset = shift_ref[...]
 
@@ -237,8 +237,6 @@
     for begin in range(0, frames, step):
         for t in range(begin, begin + step):
             activate(t)
-        if begin == 0:
-            load.wait()
         taps = jnp.concatenate(
             [
                 rows_ref[begin + a : begin + a + step, b : b + rows].reshape(step * rows * width, channels)
@@ -261,7 +259,7 @@
             total = sum(column_sum(b) for b in blocks)
             middle = group_sum(total) * (2.0 / (count * (channels // GROUPS)))
     store = pltpu.make_async_copy(
-        rows_ref.at[cached + frames - 2 : cached + frames, 1 : 1 + rows], next_ref, sems.at[1]
+        rows_ref.at[cached + frames - 2 : cached + frames, 1 : 1 + rows], next_ref, sem
     )
     store.start()
     offs = [second_ref[t, i] - middle for t in range(frames) for i in range(rows)]
@@ -305,12 +303,31 @@
     return lax.all_to_all(copies, HA[:-1], 0, 0)
 
 
+def run_mix(row, last, above, below, ends, stats, gain, shift, hidden, kernel):
+    frames, half, c_out = row.shape
+    cached = hidden.shape[0]
+    whole = jax.ShapeDtypeStruct
+    return pl.pallas_call(
+        mix_kernel,
+        name="mix",
+        out_shape=(
+            whole((frames, 2, half, c_out), F32),
+            whole((2, 2, half, c_out), BF16),
+            whole((1, LANES), F32),
+        ),
+        in_specs=[AUTO] * 10,
+        out_specs=(AUTO, ANY, AUTO),
+        scratch_shapes=[pltpu.VMEM((cached + frames, 4, half, c_out), BF16), DMA(())],
+        compiler_params=limit(28),
+    )(row, last, above, below, ends, stats, gain, shift, hidden, kernel)
+
+
 def local(video, cache_video, cache_hidden, kernel_down, gain_down, shift_down, kernel_mix, gain_mix, shift_mix):
     frames, rows, width, c_in = video.shape
     cached = cache_video.shape[0]
     c_out = kernel_down.shape[-1]
     half = width // 2
-    video, cache_video, cache_hidden = (
+    video, cache_video, stored_hidden = (
         pltpu.with_memory_space_constraint(x, pltpu.HBM) for x in (video, cache_video, cache_hidden)
     )
     devices = lax.axis_size(HA)
@@ -358,31 +375,22 @@
         ],
         compiler_params=limit(24),
         cost_estimate=pl.CostEstimate(flops=2 * 10**9, bytes_accessed=4 * 10**6, transcendentals=0),
-    )(cache_video, video, kernel_down, cache_hidden)
+    )(cache_video, video, kernel_down, stored_hidden)
     below = lax.ppermute(below, HA, up)
     last, above, stats = pl.pallas_call(
         rim_down_kernel,
         name="rim_down",
         out_shape=(line, edge, message),
-        in_specs=[AUTO] * 6 + [HBM],
+        in_specs=[AUTO] * 7,
         out_specs=(AUTO,) * 3,
-        scratch_shapes=[pltpu.VMEM((cached + frames, half, 2 * c_in), BF16), DMA(())],
+        scratch_shapes=[pltpu.VMEM((cached + frames, half, 2 * c_in), BF16)],
         compiler_params=limit(16),
     )(rim, ends, third, part, center, sums, cache_hidden)
     above = lax.ppermute(above, HA, down)
     stats = everyone(stats)
-    second, next_cache, stats = pl.pallas_call(
-        mix_kernel,
-        name="mix",
-        out_shape=(whole((frames, 2, half, c_out), F32), whole((2, 2, half, c_out), BF16), message),
-        in_specs=[AUTO] * 8 + [HBM, AUTO],
-        out_specs=(AUTO, ANY, AUTO),
-        scratch_shapes=[
-            pltpu.VMEM((cached + frames, 4, half, c_out), BF16),
-            DMA((2,)),
-        ],
-        compiler_params=limit(28),
-    )(row, last, above, below, ends, stats, gain_down[None], shift_down[None], cache_hidden, kernel_mix)
+    second, next_cache, stats = run_mix(
+        row, last, above, below, ends, stats, gain_down[None], shift_down[None], cache_hidden, kernel_mix
+    )
     stats = everyone(stats)
     encoded = pl.pallas_call(
         final_kernel,

time: 74.7 us -> 73.6 us (0.985)
  Pallas kernels: 13 us -> 11.9 us
    pallas_call x1, Pallas kernels: 5.66 us -> 4.8 us  [run_mix(): pl.pallas_call(mix_kernel, name='mix', out_shape=(whole((frames, 2, half,...]
  transfers between devices with their start and end apart: 5 -> 5, of which waited for: 2 -> 2; matrix products, arithmetic and copies ran while one was open for 0% -> 0% of each run, Pallas kernels for 7% -> 6%
where the time goes in v6:
time: 73.6 us; the launch traced here: 73.4 us
  blocking collectives  34.4 us (47%)
  starting transfers between devices  24.2 us (33%)
  Pallas kernels  11.9 us (16%)
  waiting for transfers between devices  1.99 us (3%)
    all_to_all x2, blocking collectives, everyone(): return lax.all_to_all(copies, HA[:-1], 0, 0)  34.4 us
    ppermute x1, starting transfers between devices, local(): rim = lax.ppermute(rim, HA, up)  20.5 us
    pallas_call x1, Pallas kernels, run_mix(): pl.pallas_call(mix_kernel, name='mix', out_shape=(whole((frames, 2, half,...  4.8 us
    pallas_call x1, Pallas kernels, local(): pl.pallas_call(down_kernel, name='down', out_shape=(line, line, whole((3,...  3.84 us
    ppermute x2, waiting for transfers between devices, everyone(): other = lax.ppermute(message, HA, [(i, i ^ 1) for i in range(devices)])  1.98 us
    ppermute x1, starting transfers between devices, local(): above = lax.ppermute(above, HA, down)  1.81 us
    ppermute x2, starting transfers between devices, everyone(): other = lax.ppermute(message, HA, [(i, i ^ 1) for i in range(devices)])  1.69 us
  transfers between devices with their start and end apart: 5, of which 2 were waited for; matrix products, arithmetic and copies ran while one was open for 0% of the time, Pallas kernels for 6%

profile of v6, /device:TPU:513, one launch (start us, length us, event | category | flops | bytes accessed | tf_op | source)
XLA Modules:
  0.0 73.4 jit_solution(7646558780460584110)
XLA Ops:
  0.6 1.0 %rim.1 = bf16[6,256,128]{2,1,0:T(8,128)(2,1)S(1)} custom-call(bf16[2,4,256,128]{3,2,1,0:T(8,128)(2,1)} %cache_ref.3, bf16[4,4,256,128]{3,2,1,0:T(8,128)(2,1)} %video_ref.3), custom_call_target="tpu_custom_call" | custom-call | tf_op jit(solution)/shard_map/rim/pallas_call | solution.py:338
  1.7 20.5 %collective-permute-start = (bf16[6,256,128]{2,1,0:T(8,128)(2,1)S(1)}, bf16[6,256,128]{2,1,0:T(8,128)(2,1)S(1)}, u32[]{:S(2)}, u32[]{:S(2)}) collective-permute-start(bf16[6,256,128]{2,1,0:T(8,128)(2,1)S(1)} %rim.1), channel_id=1, source_target_pairs={{1,0},{2,1},{3,2},{4,3},{5,4},{6,5},{7,6},{8,7},{9,8},{10,9},{11,1... | collective-permute-start | bytes 1179656 | tf_op jit(solution)/shard_map/ppermute | solution.py:347
  22.2 0.1 add_convert_fusion
  22.3 0.1 broadcast_in_dim.18.ends_ref
  22.4 0.0 copy-start.1
  22.4 0.0 copy-start
  22.4 0.0 copy-start.4
  22.4 0.0 copy-start.5
  22.4 3.8 %down.1 = (f32[4,128,256]{2,1,0:T(8,128)S(1)}, f32[4,128,256]{2,1,0:T(8,128)S(1)}, bf16[3,3,128,256]{3,2,1,0:T(8,128)(2,1)S(1)}, f32[1,256]{1,0:T(1,128)S(1)}, f...) custom-call(bf16[2,4,256,128]{3,2,1,0:T(8,128)(2,1)} %cache_ref.3, bf16[4,4,256,128]{3,2,1,0:T(8,128)(2,1)} %video_ref.3, ...), custom_call_target="tpu_custom_call" | custom-call | flops 2000000000 | bytes 4000000 | tf_op jit(solution)/shard_map/down/pallas_call | solution.py:356
  26.2 0.2 collective-permute-start.2
  26.4 0.0 collective-permute-done.rim_ref
  26.4 0.0 copy-done.1
  26.4 0.9 %rim_down.1 = (f32[4,128,256]{2,1,0:T(8,128)S(1)}, bf16[10,128,256]{2,1,0:T(8,128)(2,1)S(1)}, f32[1,128]{1,0:T(1,128)S(1)}) custom-call(bf16[6,256,128]{2,1,0:T(8,128)(2,1)S(1)} %collective-permute-done.rim_ref, f32[2,256]{1,0:T(2,128)S(1)} %broadcast_in_dim.18.ends_ref, bf16[3,3,128,256]{3,2,1,0:T(8,128)(2,1)S(1)} %get-tuple-element.19.third_ref, ...), custom_call_target="tpu_custom_call" | custom-call | tf_op jit(solution)/shard_map/rim_down/pallas_call | solution.py:380
  27.2 0.0 copy-start.2
  27.2 0.0 copy-start.3
  27.3 1.8 %collective-permute-start.1 = (bf16[10,128,256]{2,1,0:T(8,128)(2,1)S(1)}, bf16[10,128,256]{2,1,0:T(8,128)(2,1)S(1)}, u32[]{:S(2)}, u32[]{:S(2)}) collective-permute-start(bf16[10,128,256]{2,1,0:T(8,128)(2,1)S(1)} %get-tuple-element.24), channel_id=1, source_target_pairs={{0,1},{1,2},{2,3},{3,4},{4,5},{5,6},{6,7},{7,8},{8,9},{9,10},{10,1... | collective-permute-start | bytes 1966088 | tf_op jit(solution)/shard_map/ppermute | solution.py:389
  29.1 0.0 collective-permute-start.3
  29.1 1.2 %collective-permute-done.3.other_ref = f32[1,128]{1,0:T(1,128)S(1)} collective-permute-done((f32[1,128]{1,0:T(1,128)S(1)}, f32[1,128]{1,0:T(1,128)S(1)}, u32[]{:S(2)}, u32[]{:S(2)}) %collective-permute-start.3) | collective-permute-done | bytes 544 | tf_op jit(solution)/shard_map/ppermute | solution.py:294
  30.3 18.8 %all_to_all.10.stats_ref = f32[64,1,256]{2,1,0:T(1,128)S(1)} all-to-all(f32[64,1,256]{2,1,0:T(1,128)S(1)} %both.2), channel_id=1, replica_groups=mesh['groups'=2,'ha_0'=8,'ha_1'=8,'ha_2'=2] {'ha_0','ha_1'}, dimensions={0} | all-to-all | bytes 131072 | tf_op jit(solution)/shard_map/all_to_all | solution.py:303
  49.1 0.0 collective-permute-done.2.below_ref
  49.1 0.0 collective-permute-done.1.above_ref
  49.1 0.0 copy-done
  49.1 0.0 copy-done.4
  49.1 0.0 copy-done.5
  49.1 4.8 %mix.1 = (f32[4,2,128,256]{3,2,1,0:T(8,128)S(1)}, bf16[2,2,128,256]{3,2,1,0:T(8,128)(2,1)}, f32[1,128]{1,0:T(1,128)S(1)}) custom-call(f32[4,128,256]{2,1,0:T(8,128)S(1)} %get-tuple-element.17.row_ref, f32[4,128,256]{2,1,0:T(8,128)S(1)} %get-tuple-element.23.last_ref, bf16[10,128,256]{2,1,0:T(8,128)(2,1)S(1)} %collective-permute-done.1.above_ref, ...), custom_call_target="tpu_custom_call" | custom-call | tf_op jit(solution)/shard_map/mix/pallas_call | solution.py:310
  54.0 1.7 %collective-permute-start.4 = (f32[1,128]{1,0:T(1,128)S(1)}, f32[1,128]{1,0:T(1,128)S(1)}, u32[]{:S(2)}, u32[]{:S(2)}) collective-permute-start(f32[1,128]{1,0:T(1,128)S(1)} %get-tuple-element.28.mine_ref), channel_id=1, source_target_pairs={{0,1},{1,0},{2,3},{3,2},{4,5},{5,4},{6,7},{7,6},{8,9},{9,8},{10,11... | collective-permute-start | bytes 1544 | tf_op jit(solution)/shard_map/ppermute | solution.py:294
  55.6 0.8 %collective-permute-done.4.other_ref = f32[1,128]{1,0:T(1,128)S(1)} collective-permute-done((f32[1,128]{1,0:T(1,128)S(1)}, f32[1,128]{1,0:T(1,128)S(1)}, u32[]{:S(2)}, u32[]{:S(2)}) %collective-permute-start.4) | collective-permute-done | bytes 544 | tf_op jit(solution)/shard_map/ppermute | solution.py:294
  56.5 15.5 %all_to_all.11.stats_ref = f32[64,1,256]{2,1,0:T(1,128)S(1)} all-to-all(f32[64,1,256]{2,1,0:T(1,128)S(1)} %both.3), channel_id=1, replica_groups=mesh['groups'=2,'ha_0'=8,'ha_1'=8,'ha_2'=2] {'ha_0','ha_1'}, dimensions={0} | all-to-all | bytes 131072 | tf_op jit(solution)/shard_map/all_to_all | solution.py:303
  72.0 0.0 copy-done.2
  72.0 0.0 copy-done.3
  72.0 1.3 %final.1 = bf16[4,2,128,256]{3,2,1,0:T(8,128)(2,1)} custom-call(f32[4,2,128,256]{3,2,1,0:T(8,128)S(1)} %get-tuple-element.27.second_ref, f32[64,1,256]{2,1,0:T(1,128)S(1)} %all_to_all.11.stats_ref, f32[1,256]{1,0:T(1,128)S(1)} %bitcast.6, f32[1,256]{1,0:T(1,128)S(1)} %bitcast.7), custom_call_target="tpu_custom_call" | custom-call | tf_op jit(solution)/shard_map/final/pallas_call | solution.py:395
  (2 shorter events, 0.0 us)
Async XLA Ops:
  1.7 24.7 %collective-permute-start = (bf16[6,256,128]{2,1,0:T(8,128)(2,1)S(1)}, bf16[6,256,128]{2,1,0:T(8,128)(2,1)S(1)}, u32[]{:S(2)}, u32[]{:S(2)}) collective-permute-start(bf16[6,256,128]{2,1,0:T(8,128)(2,1)S(1)} %rim.1), channel_id=1, source_target_pairs={{1,0},{2,1},{3,2},{4,3},{5,4},{6,5},{7,6},{8,7},{9,8},{10,9},{11,1... | collective-permute-start | bytes 1179656 | tf_op jit(solution)/shard_map/ppermute | solution.py:347
  22.4 4.0 %copy-start.1 = (bf16[2,2,128,256]{3,2,1,0:T(8,128)(2,1)S(1)}, bf16[2,2,128,256]{3,2,1,0:T(8,128)(2,1)}, u32[]{:S(2)}) copy-start(bf16[2,2,128,256]{3,2,1,0:T(8,128)(2,1)} %hidden_ref.5) | copy-start | bytes 786436
  22.4 26.8 %copy-start = (bf16[3,3,3,256,256]{4,3,2,1,0:T(8,128)(2,1)S(1)}, bf16[3,3,3,256,256]{4,3,2,1,0:T(8,128)(2,1)}, u32[]{:S(2)}) copy-start(bf16[3,3,3,256,256]{4,3,2,1,0:T(8,128)(2,1)} %kernel_ref.2) | copy-start | bytes 10616836
  22.4 26.8 %copy-start.4 = (f32[256]{0:T(256)S(1)}, f32[256]{0:T(256)}, u32[]{:S(2)}) copy-start(f32[256]{0:T(256)} %param.13) | copy-start | bytes 3076
  22.4 26.8 %copy-start.5 = (f32[256]{0:T(256)S(1)}, f32[256]{0:T(256)}, u32[]{:S(2)}) copy-start(f32[256]{0:T(256)} %param.14) | copy-start | bytes 3076
  26.2 22.9 %collective-permute-start.2 = (bf16[10,128,256]{2,1,0:T(8,128)(2,1)S(1)}, bf16[10,128,256]{2,1,0:T(8,128)(2,1)S(1)}, u32[]{:S(2)}, u32[]{:S(2)}) collective-permute-start(bf16[10,128,256]{2,1,0:T(8,128)(2,1)S(1)} %get-tuple-element.25), channel_id=1, source_target_pairs={{1,0},{2,1},{3,2},{4,3},{5,4},{6,5},{7,6},{8,7},{9,8},{10,9},{11,1... | collective-permute-start | bytes 1966088 | tf_op jit(solution)/shard_map/ppermute | solution.py:379
  27.2 44.8 %copy-start.2 = (f32[256]{0:T(256)S(1)}, f32[256]{0:T(256)}, u32[]{:S(2)}) copy-start(f32[256]{0:T(256)} %param.16) | copy-start | bytes 3076
  27.2 44.8 %copy-start.3 = (f32[256]{0:T(256)S(1)}, f32[256]{0:T(256)}, u32[]{:S(2)}) copy-start(f32[256]{0:T(256)} %param.17) | copy-start | bytes 3076
  27.3 21.9 %collective-permute-start.1 = (bf16[10,128,256]{2,1,0:T(8,128)(2,1)S(1)}, bf16[10,128,256]{2,1,0:T(8,128)(2,1)S(1)}, u32[]{:S(2)}, u32[]{:S(2)}) collective-permute-start(bf16[10,128,256]{2,1,0:T(8,128)(2,1)S(1)} %get-tuple-element.24), channel_id=1, source_target_pairs={{0,1},{1,2},{2,3},{3,4},{4,5},{5,6},{6,7},{7,8},{8,9},{9,10},{10,1... | collective-permute-start | bytes 1966088 | tf_op jit(solution)/shard_map/ppermute | solution.py:389
  29.1 1.2 %collective-permute-start.3 = (f32[1,128]{1,0:T(1,128)S(1)}, f32[1,128]{1,0:T(1,128)S(1)}, u32[]{:S(2)}, u32[]{:S(2)}) collective-permute-start(f32[1,128]{1,0:T(1,128)S(1)} %get-tuple-element.26.mine_ref), channel_id=1, source_target_pairs={{0,1},{1,0},{2,3},{3,2},{4,5},{5,4},{6,7},{7,6},{8,9},{9,8},{10,11... | collective-permute-start | bytes 1544 | tf_op jit(solution)/shard_map/ppermute | solution.py:294
  54.0 2.5 %collective-permute-start.4 = (f32[1,128]{1,0:T(1,128)S(1)}, f32[1,128]{1,0:T(1,128)S(1)}, u32[]{:S(2)}, u32[]{:S(2)}) collective-permute-start(f32[1,128]{1,0:T(1,128)S(1)} %get-tuple-element.28.mine_ref), channel_id=1, source_target_pairs={{0,1},{1,0},{2,3},{3,2},{4,5},{5,4},{6,7},{7,6},{8,9},{9,8},{10,11... | collective-permute-start | bytes 1544 | tf_op jit(solution)/shard_map/ppermute | solution.py:294

commit v7 on v6

--- a/solution.py
+++ b/solution.py
@@ -92,10 +92,10 @@
 
 def rim_kernel(cache_ref, video_ref, out_ref, sems):
     cached = cache_ref.shape[0]
-    copies = [
-        pltpu.make_async_copy(cache_ref.at[:, 0], out_ref.at[:cached], sems.at[0]),
-        pltpu.make_async_copy(video_ref.at[:, 0], out_ref.at[cached:], sems.at[1]),
-    ]
+    copies = []
+    for f in range(out_ref.shape[0]):
+        source = cache_ref.at[f, 0] if f < cached else video_ref.at[f - cached, 0]
+        copies.append(pltpu.make_async_copy(source, out_ref.at[f], sems.at[f]))
     for c in copies:
         c.start()
     for c in copies:
@@ -170,16 +170,18 @@
 
 
 def rim_down_kernel(
-    rim_ref, ends_ref, third_ref, part_ref, center_ref, sums_ref, hidden_ref,
+    near_ref, far_ref, ends_ref, third_ref, part_ref, center_ref, sums_ref, hidden_ref,
     last_ref, edge_ref, message_ref,
-    pairs_ref,
+    rim_ref, pairs_ref,
 ):
     frames, half, _ = part_ref.shape
-    c_in = rim_ref.shape[-1]
+    c_in = near_ref.shape[-1]
     cached, rows = hidden_ref.shape[:2]
     for f in range(cached):
         edge_ref[f] = hidden_ref[f, rows - 1]
+    odd = ends_ref[2:3, :c_in].astype(BF16)
     for f in range(rim_ref.shape[0]):
+        rim_ref[f] = far_ref[f] * odd + near_ref[f] * (1 - odd)
         pair_up(rim_ref.at[f], pairs_ref.at[f], c_in)
     taps = [pairs_ref[a : a + frames].reshape(frames * half, 2 * c_in) for a in range(3)]
     both = jnp.concatenate([third_ref[a, c] for a in range(3) for c in range(2)], axis=0)
@@ -235,8 +237,9 @@
 
     step = frames // 2
     for begin in range(0, frames, step):
-        for t in range(begin, begin + step):
-            activate(t)
+        if begin == 0:
+            for t in range(step):
+                activate(t)
         taps = jnp.concatenate(
             [
                 rows_ref[begin + a : begin + a + step, b : b + rows].reshape(step * rows * width, channels)
@@ -250,21 +253,30 @@
             weights = jnp.concatenate([kernel_ref[a, b, c] for a in range(3) for b in range(3)], axis=0)
             parts.append(jnp.dot(taps, weights, preferred_element_type=F32))
         left, here, right = parts
+        if begin == 0:
+            for t in range(step, frames):
+                activate(t)
+        blocks = []
         for n in range(step * rows):
             span = slice(n * width, (n + 1) * width)
             t, i = begin + n // rows, n % rows
-            second_ref[t, i] = here[span] + shift_on(left[span]) + shift_back(right[span])
+            block = here[span] + shift_on(left[span]) + shift_back(right[span])
+            second_ref[t, i] = block
+            blocks.append(block)
         if begin == 0:
+            total = sum(column_sum(b) for b in blocks)
+            middle = group_sum(total) * (1.0 / (step * rows * width * (channels // GROUPS)))
+            sums = total - middle * (step * rows * width)
             blocks = [second_ref[t, i] for t in range(step) for i in range(rows)]
-            total = sum(column_sum(b) for b in blocks)
-            middle = group_sum(total) * (2.0 / (count * (channels // GROUPS)))
+            squares = sum(column_sum((b - middle) ** 2) for b in blocks)
+        else:
+            offs = [b - middle for b in blocks]
+            sums = sums + sum(column_sum(off) for off in offs)
+            squares = squares + sum(column_sum(off * off) for off in offs)
     store = pltpu.make_async_copy(
         rows_ref.at[cached + frames - 2 : cached + frames, 1 : 1 + rows], next_ref, sem
     )
     store.start()
-    offs = [second_ref[t, i] - middle for t in range(frames) for i in range(rows)]
-    sums = sum(column_sum(off) for off in offs)
-    squares = sum(column_sum(off * off) for off in offs)
     message_ref[...] = moments_row(middle, sums, squares, count)
     store.wait()
 
@@ -278,8 +290,8 @@
     for t in range(frames):
         for i in range(rows):
             buf[t, i] = silu_norm(second_ref[t, i], center, factor, offset).astype(BF16)
-        stores.append(pltpu.make_async_copy(buf.at[t], out_ref.at[t], sems.at[t]))
-        stores[-1].start()
+            stores.append(pltpu.make_async_copy(buf.at[t, i], out_ref.at[t, i], sems.at[t * rows + i]))
+            stores[-1].start()
     for c in stores:
         c.wait()
 
@@ -341,12 +353,15 @@
         out_shape=whole((cached + frames, width, c_in), BF16),
         in_specs=[HBM] * 2,
         out_specs=AUTO,
-        scratch_shapes=[DMA((2,))],
+        scratch_shapes=[DMA((cached + frames,))],
         compiler_params=limit(4),
     )(cache_video, video)
-    rim = lax.ppermute(rim, HA, up)
+    pairs = [(i, i ^ 1) for i in range(devices)]
+    bridges = [(i, min(max(i + (1 if i % 2 else -1), 0), devices - 1)) for i in range(devices)]
+    near_rim = lax.ppermute(rim, HA, pairs)
+    far_rim = lax.ppermute(rim, HA, bridges)
     ends = jnp.broadcast_to(
-        jnp.stack([place > 0, place < devices - 1]).astype(F32)[:, None], (2, c_out)
+        jnp.stack([place > 0, place < devices - 1, place % 2 > 0]).astype(F32)[:, None], (3, c_out)
     )
     kernel_down, ends = lax.optimization_barrier((kernel_down, ends))
     kernel_down = pltpu.with_memory_space_constraint(kernel_down, pltpu.HBM)
@@ -381,11 +396,14 @@
         rim_down_kernel,
         name="rim_down",
         out_shape=(line, edge, message),
-        in_specs=[AUTO] * 7,
+        in_specs=[AUTO] * 8,
         out_specs=(AUTO,) * 3,
-        scratch_shapes=[pltpu.VMEM((cached + frames, half, 2 * c_in), BF16)],
+        scratch_shapes=[
+            pltpu.VMEM((cached + frames, width, c_in), BF16),
+            pltpu.VMEM((cached + frames, half, 2 * c_in), BF16),
+        ],
         compiler_params=limit(16),
-    )(rim, ends, third, part, center, sums, cache_hidden)
+    )(near_rim, far_rim, ends, third, part, center, sums, cache_hidden)
     above = lax.ppermute(above, HA, down)
     stats = everyone(stats)
     second, next_cache, stats = run_mix(
@@ -398,7 +416,7 @@
         out_shape=whole((frames, 2, half, c_out), BF16),
         in_specs=[AUTO] * 4,
         out_specs=ANY,
-        scratch_shapes=[pltpu.VMEM((frames, 2, half, c_out), BF16), DMA((frames,))],
+        scratch_shapes=[pltpu.VMEM((frames, 2, half, c_out), BF16), DMA((2 * frames,))],
         compiler_params=limit(8),
     )(second, stats, gain_mix[None], shift_mix[None])
     return (encoded, next_cache)

time: 73.6 us -> 72.2 us (0.981)
  blocking collectives: 34.4 us -> 32.2 us
    all_to_all x2, blocking collectives: 34.4 us -> 32.2 us  [everyone(): return lax.all_to_all(copies, HA[:-1], 0, 0)]
    ppermute x1 -> x2, starting transfers between devices: 20.5 us -> 21.2 us  [the longest x1 16.6 us: local(): near_rim = lax.ppermute(rim, HA, pairs)]
  transfers between devices with their start and end apart: 5 -> 6, of which waited for: 2 -> 2; matrix products, arithmetic and copies ran while one was open for 0% -> 0% of each run, Pallas kernels for 6% -> 7%
where the time goes in v7:
time: 72.2 us; the launch traced here: 71.9 us
  blocking collectives  32.2 us (45%)
  starting transfers between devices  24.9 us (34%)
  Pallas kernels  11.9 us (16%)
  waiting for transfers between devices  1.99 us (3%)
  between operations  0.73 us (1%)
    all_to_all x2, blocking collectives, everyone(): return lax.all_to_all(copies, HA[:-1], 0, 0)  32.2 us
    ppermute x1, starting transfers between devices, local(): near_rim = lax.ppermute(rim, HA, pairs)  16.6 us
    pallas_call x1, Pallas kernels, run_mix(): pl.pallas_call(mix_kernel, name='mix', out_shape=(whole((frames, 2, half,...  4.74 us
    ppermute x1, starting transfers between devices, local(): far_rim = lax.ppermute(rim, HA, bridges)  4.6 us
    pallas_call x1, Pallas kernels, local(): pl.pallas_call(down_kernel, name='down', out_shape=(line, line, whole((3,...  3.84 us
    ppermute x2, waiting for transfers between devices, everyone(): other = lax.ppermute(message, HA, [(i, i ^ 1) for i in range(devices)])  1.98 us
    ppermute x1, starting transfers between devices, local(): above = lax.ppermute(above, HA, down)  1.81 us
    ppermute x2, starting transfers between devices, everyone(): other = lax.ppermute(message, HA, [(i, i ^ 1) for i in range(devices)])  1.72 us
  transfers between devices with their start and end apart: 6, of which 2 were waited for; matrix products, arithmetic and copies ran while one was open for 0% of the time, Pallas kernels for 7%

profile of v7, /device:TPU:513, one launch (start us, length us, event | category | flops | bytes accessed | tf_op | source)
XLA Modules:
  0.0 71.9 jit_solution(2309480024122923544)
XLA Ops:
  0.6 1.1 %rim.1 = bf16[6,256,128]{2,1,0:T(8,128)(2,1)S(1)} custom-call(bf16[2,4,256,128]{3,2,1,0:T(8,128)(2,1)} %cache_ref.3, bf16[4,4,256,128]{3,2,1,0:T(8,128)(2,1)} %video_ref.3), custom_call_target="tpu_custom_call" | custom-call | tf_op jit(solution)/shard_map/rim/pallas_call | solution.py:350
  1.7 4.6 %collective-permute-start.1 = (bf16[6,256,128]{2,1,0:T(8,128)(2,1)S(1)}, bf16[6,256,128]{2,1,0:T(8,128)(2,1)S(1)}, u32[]{:S(2)}, u32[]{:S(2)}) collective-permute-start(bf16[6,256,128]{2,1,0:T(8,128)(2,1)S(1)} %rim.1), channel_id=1, source_target_pairs={{0,0},{1,2},{2,1},{3,4},{4,3},{5,6},{6,5},{7,8},{8,7},{9,10},{10,9... | collective-permute-start | bytes 1179656 | tf_op jit(solution)/shard_map/ppermute | solution.py:362
  6.3 16.6 %collective-permute-start = (bf16[6,256,128]{2,1,0:T(8,128)(2,1)S(1)}, bf16[6,256,128]{2,1,0:T(8,128)(2,1)S(1)}, u32[]{:S(2)}, u32[]{:S(2)}) collective-permute-start(bf16[6,256,128]{2,1,0:T(8,128)(2,1)S(1)} %rim.1), channel_id=1, source_target_pairs={{0,1},{1,0},{2,3},{3,2},{4,5},{5,4},{6,7},{7,6},{8,9},{9,8},{10,11... | collective-permute-start | bytes 1179656 | tf_op jit(solution)/shard_map/ppermute | solution.py:361
  22.9 0.1 add_convert_fusion
  23.0 0.1 broadcast_in_dim.18.ends_ref
  23.1 0.0 copy-start
  23.1 0.0 copy-start.2
  23.1 0.0 copy-start.3
  23.1 3.8 %down.1 = (f32[4,128,256]{2,1,0:T(8,128)S(1)}, f32[4,128,256]{2,1,0:T(8,128)S(1)}, bf16[3,3,128,256]{3,2,1,0:T(8,128)(2,1)S(1)}, f32[1,256]{1,0:T(1,128)S(1)}, f...) custom-call(bf16[2,4,256,128]{3,2,1,0:T(8,128)(2,1)} %cache_ref.3, bf16[4,4,256,128]{3,2,1,0:T(8,128)(2,1)} %video_ref.3, ...), custom_call_target="tpu_custom_call" | custom-call | flops 2000000000 | bytes 4000000 | tf_op jit(solution)/shard_map/down/pallas_call | solution.py:371
  26.9 0.2 collective-permute-start.3
  27.1 0.0 collective-permute-done.1.far_ref
  27.1 0.0 collective-permute-done.near_ref
  27.1 0.0 copy-done.1
  27.1 0.9 %rim_down.1 = (f32[4,128,256]{2,1,0:T(8,128)S(1)}, bf16[10,128,256]{2,1,0:T(8,128)(2,1)S(1)}, f32[1,128]{1,0:T(1,128)S(1)}) custom-call(bf16[6,256,128]{2,1,0:T(8,128)(2,1)S(1)} %collective-permute-done.near_ref, bf16[6,256,128]{2,1,0:T(8,128)(2,1)S(1)} %collective-permute-done.1.far_ref, f32[3,256]{1,0:T(4,128)S(1)} %broadcast_in_dim.18.ends_ref, ...), custom_call_target="tpu_custom_call" | custom-call | tf_op jit(solution)/shard_map/rim_down/pallas_call | solution.py:395
  28.0 0.0 copy-start.4
  28.1 0.0 copy-start.5
  28.1 1.8 %collective-permute-start.2 = (bf16[10,128,256]{2,1,0:T(8,128)(2,1)S(1)}, bf16[10,128,256]{2,1,0:T(8,128)(2,1)S(1)}, u32[]{:S(2)}, u32[]{:S(2)}) collective-permute-start(bf16[10,128,256]{2,1,0:T(8,128)(2,1)S(1)} %get-tuple-element.24), channel_id=1, source_target_pairs={{0,1},{1,2},{2,3},{3,4},{4,5},{5,6},{6,7},{7,8},{8,9},{9,10},{10,1... | collective-permute-start | bytes 1966088 | tf_op jit(solution)/shard_map/ppermute | solution.py:407
  29.9 0.0 collective-permute-start.4
  29.9 1.2 %collective-permute-done.4.other_ref = f32[1,128]{1,0:T(1,128)S(1)} collective-permute-done((f32[1,128]{1,0:T(1,128)S(1)}, f32[1,128]{1,0:T(1,128)S(1)}, u32[]{:S(2)}, u32[]{:S(2)}) %collective-permute-start.4) | collective-permute-done | bytes 544 | tf_op jit(solution)/shard_map/ppermute | solution.py:306
  31.1 16.6 %all_to_all.10.stats_ref = f32[64,1,256]{2,1,0:T(1,128)S(1)} all-to-all(f32[64,1,256]{2,1,0:T(1,128)S(1)} %both.2), channel_id=1, replica_groups=mesh['groups'=2,'ha_0'=8,'ha_1'=8,'ha_2'=2] {'ha_0','ha_1'}, dimensions={0} | all-to-all | bytes 131072 | tf_op jit(solution)/shard_map/all_to_all | solution.py:315
  47.7 0.0 collective-permute-done.3.below_ref
  47.7 0.0 collective-permute-done.2.above_ref
  47.7 0.0 copy-done
  47.7 0.0 copy-done.2
  47.7 0.0 copy-done.3
  47.7 4.7 %mix.1 = (f32[4,2,128,256]{3,2,1,0:T(8,128)S(1)}, bf16[2,2,128,256]{3,2,1,0:T(8,128)(2,1)}, f32[1,128]{1,0:T(1,128)S(1)}) custom-call(f32[4,128,256]{2,1,0:T(8,128)S(1)} %get-tuple-element.17.row_ref, f32[4,128,256]{2,1,0:T(8,128)S(1)} %get-tuple-element.23.last_ref, bf16[10,128,256]{2,1,0:T(8,128)(2,1)S(1)} %collective-permute-done.2.above_ref, ...), custom_call_target="tpu_custom_call" | custom-call | tf_op jit(solution)/shard_map/mix/pallas_call | solution.py:322
  52.5 1.7 %collective-permute-start.5 = (f32[1,128]{1,0:T(1,128)S(1)}, f32[1,128]{1,0:T(1,128)S(1)}, u32[]{:S(2)}, u32[]{:S(2)}) collective-permute-start(f32[1,128]{1,0:T(1,128)S(1)} %get-tuple-element.28.mine_ref), channel_id=1, source_target_pairs={{0,1},{1,0},{2,3},{3,2},{4,5},{5,4},{6,7},{7,6},{8,9},{9,8},{10,11... | collective-permute-start | bytes 1544 | tf_op jit(solution)/shard_map/ppermute | solution.py:306
  54.2 0.8 %collective-permute-done.5.other_ref = f32[1,128]{1,0:T(1,128)S(1)} collective-permute-done((f32[1,128]{1,0:T(1,128)S(1)}, f32[1,128]{1,0:T(1,128)S(1)}, u32[]{:S(2)}, u32[]{:S(2)}) %collective-permute-start.5) | collective-permute-done | bytes 544 | tf_op jit(solution)/shard_map/ppermute | solution.py:306
  55.0 15.5 %all_to_all.11.stats_ref = f32[64,1,256]{2,1,0:T(1,128)S(1)} all-to-all(f32[64,1,256]{2,1,0:T(1,128)S(1)} %both.3), channel_id=1, replica_groups=mesh['groups'=2,'ha_0'=8,'ha_1'=8,'ha_2'=2] {'ha_0','ha_1'}, dimensions={0} | all-to-all | bytes 131072 | tf_op jit(solution)/shard_map/all_to_all | solution.py:315
  70.6 0.0 copy-done.4
  70.6 0.0 copy-done.5
  70.6 1.3 %final.1 = bf16[4,2,128,256]{3,2,1,0:T(8,128)(2,1)} custom-call(f32[4,2,128,256]{3,2,1,0:T(8,128)S(1)} %get-tuple-element.27.second_ref, f32[64,1,256]{2,1,0:T(1,128)S(1)} %all_to_all.11.stats_ref, f32[1,256]{1,0:T(1,128)S(1)} %bitcast.9, f32[1,256]{1,0:T(1,128)S(1)} %bitcast.10), custom_call_target="tpu_custom_call" | custom-call | tf_op jit(solution)/shard_map/final/pallas_call | solution.py:413
  (3 shorter events, 0.0 us)
Async XLA Ops:
  1.7 25.4 %collective-permute-start.1 = (bf16[6,256,128]{2,1,0:T(8,128)(2,1)S(1)}, bf16[6,256,128]{2,1,0:T(8,128)(2,1)S(1)}, u32[]{:S(2)}, u32[]{:S(2)}) collective-permute-start(bf16[6,256,128]{2,1,0:T(8,128)(2,1)S(1)} %rim.1), channel_id=1, source_target_pairs={{0,0},{1,2},{2,1},{3,4},{4,3},{5,6},{6,5},{7,8},{8,7},{9,10},{10,9... | collective-permute-start | bytes 1179656 | tf_op jit(solution)/shard_map/ppermute | solution.py:362
  6.3 20.8 %collective-permute-start = (bf16[6,256,128]{2,1,0:T(8,128)(2,1)S(1)}, bf16[6,256,128]{2,1,0:T(8,128)(2,1)S(1)}, u32[]{:S(2)}, u32[]{:S(2)}) collective-permute-start(bf16[6,256,128]{2,1,0:T(8,128)(2,1)S(1)} %rim.1), channel_id=1, source_target_pairs={{0,1},{1,0},{2,3},{3,2},{4,5},{5,4},{6,7},{7,6},{8,9},{9,8},{10,11... | collective-permute-start | bytes 1179656 | tf_op jit(solution)/shard_map/ppermute | solution.py:361
  23.1 4.0 %copy-start.1 = (bf16[2,2,128,256]{3,2,1,0:T(8,128)(2,1)S(1)}, bf16[2,2,128,256]{3,2,1,0:T(8,128)(2,1)}, u32[]{:S(2)}) copy-start(bf16[2,2,128,256]{3,2,1,0:T(8,128)(2,1)} %hidden_ref.5) | copy-start | bytes 786436
  23.1 24.6 %copy-start = (bf16[3,3,3,256,256]{4,3,2,1,0:T(8,128)(2,1)S(1)}, bf16[3,3,3,256,256]{4,3,2,1,0:T(8,128)(2,1)}, u32[]{:S(2)}) copy-start(bf16[3,3,3,256,256]{4,3,2,1,0:T(8,128)(2,1)} %kernel_ref.2) | copy-start | bytes 10616836
  23.1 24.6 %copy-start.2 = (f32[256]{0:T(256)S(1)}, f32[256]{0:T(256)}, u32[]{:S(2)}) copy-start(f32[256]{0:T(256)} %param.13) | copy-start | bytes 3076
  23.1 24.7 %copy-start.3 = (f32[256]{0:T(256)S(1)}, f32[256]{0:T(256)}, u32[]{:S(2)}) copy-start(f32[256]{0:T(256)} %param.14) | copy-start | bytes 3076
  26.9 20.8 %collective-permute-start.3 = (bf16[10,128,256]{2,1,0:T(8,128)(2,1)S(1)}, bf16[10,128,256]{2,1,0:T(8,128)(2,1)S(1)}, u32[]{:S(2)}, u32[]{:S(2)}) collective-permute-start(bf16[10,128,256]{2,1,0:T(8,128)(2,1)S(1)} %get-tuple-element.25), channel_id=1, source_target_pairs={{1,0},{2,1},{3,2},{4,3},{5,4},{6,5},{7,6},{8,7},{9,8},{10,9},{11,1... | collective-permute-start | bytes 1966088 | tf_op jit(solution)/shard_map/ppermute | solution.py:394
  28.0 42.6 %copy-start.4 = (f32[256]{0:T(256)S(1)}, f32[256]{0:T(256)}, u32[]{:S(2)}) copy-start(f32[256]{0:T(256)} %param.16) | copy-start | bytes 3076
  28.1 42.5 %copy-start.5 = (f32[256]{0:T(256)S(1)}, f32[256]{0:T(256)}, u32[]{:S(2)}) copy-start(f32[256]{0:T(256)} %param.17) | copy-start | bytes 3076
  28.1 19.6 %collective-permute-start.2 = (bf16[10,128,256]{2,1,0:T(8,128)(2,1)S(1)}, bf16[10,128,256]{2,1,0:T(8,128)(2,1)S(1)}, u32[]{:S(2)}, u32[]{:S(2)}) collective-permute-start(bf16[10,128,256]{2,1,0:T(8,128)(2,1)S(1)} %get-tuple-element.24), channel_id=1, source_target_pairs={{0,1},{1,2},{2,3},{3,4},{4,5},{5,6},{6,7},{7,8},{8,9},{9,10},{10,1... | collective-permute-start | bytes 1966088 | tf_op jit(solution)/shard_map/ppermute | solution.py:407
  29.9 1.2 %collective-permute-start.4 = (f32[1,128]{1,0:T(1,128)S(1)}, f32[1,128]{1,0:T(1,128)S(1)}, u32[]{:S(2)}, u32[]{:S(2)}) collective-permute-start(f32[1,128]{1,0:T(1,128)S(1)} %get-tuple-element.26.mine_ref), channel_id=1, source_target_pairs={{0,1},{1,0},{2,3},{3,2},{4,5},{5,4},{6,7},{7,6},{8,9},{9,8},{10,11... | collective-permute-start | bytes 1544 | tf_op jit(solution)/shard_map/ppermute | solution.py:306
  52.5 2.5 %collective-permute-start.5 = (f32[1,128]{1,0:T(1,128)S(1)}, f32[1,128]{1,0:T(1,128)S(1)}, u32[]{:S(2)}, u32[]{:S(2)}) collective-permute-start(f32[1,128]{1,0:T(1,128)S(1)} %get-tuple-element.28.mine_ref), channel_id=1, source_target_pairs={{0,1},{1,0},{2,3},{3,2},{4,5},{5,4},{6,7},{7,6},{8,9},{9,8},{10,11... | collective-permute-start | bytes 1544 | tf_op jit(solution)/shard_map/ppermute | solution.py:306

commit v8 on v7

--- a/solution.py
+++ b/solution.py
@@ -113,9 +113,20 @@
     return coarse, (value - coarse.astype(F32)).astype(BF16)
 
 
+def third_row(pairs, third_ref, frames, half, c_in):
+    taps = [pairs[a : a + frames].reshape(frames * half, 2 * c_in) for a in range(3)]
+    both = jnp.concatenate([third_ref[a, c] for a in range(3) for c in range(2)], axis=0)
+    ahead = jnp.concatenate([third_ref[a, 2] for a in range(3)], axis=0)
+    here = jnp.dot(jnp.concatenate(taps, axis=1), both, preferred_element_type=F32)
+    evens = jnp.concatenate([t[:, :c_in] for t in taps], axis=1)
+    after = jnp.dot(evens, ahead, preferred_element_type=F32)
+    spans = [slice(t * half, (t + 1) * half) for t in range(frames)]
+    return [here[span] + shift_back(after[span]) for span in spans]
+
+
 def down_kernel(
     cache_ref, video_ref, kernel_ref, hidden_ref,
-    row_ref, part_ref, third_ref, center_ref, sums_ref, edge_ref,
+    row_ref, part_ref, share_ref, third_ref, center_ref, sums_ref, upper_ref, lower_ref,
     cache_buf, video_buf, kernel_buf, pairs_ref, sems,
 ):
     frames, rows, width, c_in = video_ref.shape
@@ -127,7 +138,8 @@
         pltpu.make_async_copy(video_ref, video_buf, sems.at[1]),
         pltpu.make_async_copy(kernel_ref.at[:, :2], kernel_buf, sems.at[2]),
         pltpu.make_async_copy(kernel_ref.at[:, 2], third_ref, sems.at[3]),
-        pltpu.make_async_copy(hidden_ref.at[:, 0], edge_ref.at[:cached], sems.at[4]),
+        pltpu.make_async_copy(hidden_ref.at[:, 0], upper_ref.at[:cached], sems.at[4]),
+        pltpu.make_async_copy(hidden_ref.at[:, rows // 2 - 1], lower_ref.at[:cached], sems.at[5]),
     ]
     for c in loads:
         c.start()
@@ -156,47 +168,39 @@
         for t in range(frames):
             span = slice(t * half, (t + 1) * half)
             block = here[span] + shift_back(after[span])
-            if i == 0:
-                row_ref[t] = block
-                edge_ref[cached + t], edge_ref[cached + frames + t] = split_in_two(block)
-            else:
-                part_ref[t] = block
+            target, edge_ref = (row_ref, upper_ref) if i == 0 else (part_ref, lower_ref)
+            target[t] = block
+            edge_ref[cached + t], edge_ref[cached + frames + t] = split_in_two(block)
+    shares = third_row(pairs_ref[:, 0], third_ref, frames, half, c_in)
+    for t in range(frames):
+        share_ref[t] = shares[t]
     total = sum(column_sum(row_ref[t]) for t in range(frames))
     center = group_sum(total) * (1.0 / (frames * half * (c_out // GROUPS)))
     center_ref[...] = center
     sums_ref[0:1] = total - center * (frames * half)
     sums_ref[1:2] = sum(column_sum((row_ref[t] - center) ** 2) for t in range(frames))
     loads[4].wait()
+    loads[5].wait()
 
 
 def rim_down_kernel(
-    near_ref, far_ref, ends_ref, third_ref, part_ref, center_ref, sums_ref, hidden_ref,
-    last_ref, edge_ref, message_ref,
+    near_ref, far_ref, ends_ref, third_ref, part_ref, center_ref, sums_ref,
+    last_ref, message_ref,
     rim_ref, pairs_ref,
 ):
     frames, half, _ = part_ref.shape
     c_in = near_ref.shape[-1]
-    cached, rows = hidden_ref.shape[:2]
-    for f in range(cached):
-        edge_ref[f] = hidden_ref[f, rows - 1]
     odd = ends_ref[2:3, :c_in].astype(BF16)
     for f in range(rim_ref.shape[0]):
         rim_ref[f] = far_ref[f] * odd + near_ref[f] * (1 - odd)
         pair_up(rim_ref.at[f], pairs_ref.at[f], c_in)
-    taps = [pairs_ref[a : a + frames].reshape(frames * half, 2 * c_in) for a in range(3)]
-    both = jnp.concatenate([third_ref[a, c] for a in range(3) for c in range(2)], axis=0)
-    ahead = jnp.concatenate([third_ref[a, 2] for a in range(3)], axis=0)
-    here = jnp.dot(jnp.concatenate(taps, axis=1), both, preferred_element_type=F32)
-    evens = jnp.concatenate([t[:, :c_in] for t in taps], axis=1)
-    after = jnp.dot(evens, ahead, preferred_element_type=F32)
     keep = ends_ref[1:2]
     center = center_ref[...]
     sums, squares = sums_ref[0:1], sums_ref[1:2]
+    shares = third_row(pairs_ref[...], third_ref, frames, half, c_in)
     for t in range(frames):
-        span = slice(t * half, (t + 1) * half)
-        block = part_ref[t] + jnp.where(keep > 0, here[span] + shift_back(after[span]), 0.0)
+        block = part_ref[t] + jnp.where(keep > 0, shares[t], 0.0)
         last_ref[t] = block
-        edge_ref[cached + t], edge_ref[cached + frames + t] = split_in_two(block)
         off = block - center
         sums = sums + column_sum(off)
         squares = squares + column_sum(off * off)
@@ -209,7 +213,7 @@
 
 
 def mix_kernel(
-    row_ref, last_ref, above_ref, below_ref, ends_ref, stats_ref, gain_ref, shift_ref, hidden_ref, kernel_ref,
+    row_ref, last_ref, share_ref, above_ref, below_ref, ends_ref, stats_ref, gain_ref, shift_ref, hidden_ref, kernel_ref,
     second_ref, next_ref, message_ref,
     rows_ref, sem,
 ):
@@ -230,6 +234,8 @@
     def activate(t):
         for at, edge_ref, keep in ((0, above_ref, keep_above), (rows + 1, below_ref, keep_below)):
             value = edge_ref[cached + t].astype(F32) + edge_ref[cached + frames + t].astype(F32)
+            if at == 0:
+                value = value + share_ref[t]
             hidden = silu_norm(value, center, factor, offset)
             rows_ref[cached + t, at] = jnp.where(keep > 0, hidden, 0.0).astype(BF16)
         rows_ref[cached + t, 1] = silu_norm(row_ref[t], center, factor, offset).astype(BF16)
@@ -315,7 +321,7 @@
     return lax.all_to_all(copies, HA[:-1], 0, 0)
 
 
-def run_mix(row, last, above, below, ends, stats, gain, shift, hidden, kernel):
+def run_mix(row, last, share, above, below, ends, stats, gain, shift, hidden, kernel):
     frames, half, c_out = row.shape
     cached = hidden.shape[0]
     whole = jax.ShapeDtypeStruct
@@ -327,11 +333,11 @@
             whole((2, 2, half, c_out), BF16),
             whole((1, LANES), F32),
         ),
-        in_specs=[AUTO] * 10,
+        in_specs=[AUTO] * 11,
         out_specs=(AUTO, ANY, AUTO),
         scratch_shapes=[pltpu.VMEM((cached + frames, 4, half, c_out), BF16), DMA(())],
         compiler_params=limit(28),
-    )(row, last, above, below, ends, stats, gain, shift, hidden, kernel)
+    )(row, last, share, above, below, ends, stats, gain, shift, hidden, kernel)
 
 
 def local(video, cache_video, cache_hidden, kernel_down, gain_down, shift_down, kernel_mix, gain_mix, shift_mix):
@@ -368,46 +374,48 @@
     line = whole((frames, half, c_out), F32)
     edge = whole((cached + 2 * frames, half, c_out), BF16)
     message = whole((1, LANES), F32)
-    row, part, third, center, sums, below = pl.pallas_call(
+    row, part, share, third, center, sums, below, above = pl.pallas_call(
         down_kernel,
         name="down",
         out_shape=(
+            line,
             line,
             line,
             whole((3, 3, c_in, c_out), BF16),
             whole((1, c_out), F32),
             whole((2, c_out), F32),
             edge,
+            edge,
         ),
         in_specs=[HBM] * 4,
-        out_specs=(AUTO,) * 6,
+        out_specs=(AUTO,) * 8,
         scratch_shapes=[
             pltpu.VMEM(cache_video.shape, BF16),
             pltpu.VMEM(video.shape, BF16),
             pltpu.VMEM((3, 2, 3, c_in, c_out), BF16),
             pltpu.VMEM((cached + frames, rows, half, 2 * c_in), BF16),
-            DMA((5,)),
+            DMA((6,)),
         ],
         compiler_params=limit(24),
         cost_estimate=pl.CostEstimate(flops=2 * 10**9, bytes_accessed=4 * 10**6, transcendentals=0),
     )(cache_video, video, kernel_down, stored_hidden)
     below = lax.ppermute(below, HA, up)
-    last, above, stats = pl.pallas_call(
+    above = lax.ppermute(above, HA, down)
+    last, stats = pl.pallas_call(
         rim_down_kernel,
         name="rim_down",
-        out_shape=(line, edge, message),
-        in_specs=[AUTO] * 8,
-        out_specs=(AUTO,) * 3,
+        out_shape=(line, message),
+        in_specs=[AUTO] * 7,
+        out_specs=(AUTO,) * 2,
         scratch_shapes=[
             pltpu.VMEM((cached + frames, width, c_in), BF16),
             pltpu.VMEM((cached + frames, half, 2 * c_in), BF16),
         ],
         compiler_params=limit(16),
-    )(near_rim, far_rim, ends, third, part, center, sums, cache_hidden)
-    above = lax.ppermute(above, HA, down)
+    )(near_rim, far_rim, ends, third, part, center, sums)
     stats = everyone(stats)
     second, next_cache, stats = run_mix(
-        row, last, above, below, ends, stats, gain_down[None], shift_down[None], cache_hidden, kernel_mix
+        row, last, share, above, below, ends, stats, gain_down[None], shift_down[None], cache_hidden, kernel_mix
     )
     stats = everyone(stats)
     encoded = pl.pallas_call(

time: 72.2 us -> 79.5 us (1.10)
  waiting for transfers between devices: 1.99 us -> 5.64 us
  starting transfers between devices: 24.9 us -> 28.3 us
    ppermute x1, starting transfers between devices: 0.16 us -> 17.9 us  [local(): below = lax.ppermute(below, HA, up)]
    ppermute x1, starting transfers between devices: 16.6 us -> 3.78 us  [local(): near_rim = lax.ppermute(rim, HA, pairs)]
    ppermute x1, waiting for transfers between devices: 0.01 us -> 3.68 us  [local(): far_rim = lax.ppermute(rim, HA, bridges)]
    ppermute x1, starting transfers between devices: 4.6 us -> 1.95 us  [local(): far_rim = lax.ppermute(rim, HA, bridges)]
    ppermute x1, starting transfers between devices: 1.81 us -> 2.77 us  [local(): above = lax.ppermute(above, HA, down)]
  transfers between devices with their start and end apart: 6 -> 6, of which waited for: 2 -> 3; matrix products, arithmetic and copies ran while one was open for 0% -> 0% of each run, Pallas kernels for 7% -> 2%
where the time goes in v8:
time: 79.5 us; the launch traced here: 79.2 us
  blocking collectives  32.2 us (41%)
  starting transfers between devices  28.3 us (36%)
  Pallas kernels  12.1 us (15%)
  waiting for transfers between devices  5.64 us (7%)
    all_to_all x2, blocking collectives, everyone(): return lax.all_to_all(copies, HA[:-1], 0, 0)  32.2 us
    ppermute x1, starting transfers between devices, local(): below = lax.ppermute(below, HA, up)  17.9 us
    pallas_call x1, Pallas kernels, run_mix(): pl.pallas_call(mix_kernel, name='mix', out_shape=(whole((frames, 2, half,...  4.74 us
    pallas_call x1, Pallas kernels, local(): pl.pallas_call(down_kernel, name='down', out_shape=(line, line, line, who...  4.03 us
    ppermute x1, starting transfers between devices, local(): near_rim = lax.ppermute(rim, HA, pairs)  3.78 us
    ppermute x1, waiting for transfers between devices, local(): far_rim = lax.ppermute(rim, HA, bridges)  3.68 us
    ppermute x1, starting transfers between devices, local(): above = lax.ppermute(above, HA, down)  2.77 us
    ppermute x2, waiting for transfers between devices, everyone(): other = lax.ppermute(message, HA, [(i, i ^ 1) for i in range(devices)])  1.95 us
  transfers between devices with their start and end apart: 6, of which 3 were waited for; matrix products, arithmetic and copies ran while one was open for 0% of the time, Pallas kernels for 2%

profile of v8, /device:TPU:513, one launch (start us, length us, event | category | flops | bytes accessed | tf_op | source)
XLA Modules:
  0.0 79.2 jit_solution(12548989041707202915)
XLA Ops:
  0.6 0.1 add_convert_fusion
  0.7 0.1 broadcast_in_dim.18.ends_ref
  0.8 4.0 %down.1 = (f32[4,128,256]{2,1,0:T(8,128)S(1)}, f32[4,128,256]{2,1,0:T(8,128)S(1)}, f32[4,128,256]{2,1,0:T(8,128)S(1)}, bf16[3,3,128,256]{3,2,1,0:T(8,128)(2,1)S(...) custom-call(bf16[2,4,256,128]{3,2,1,0:T(8,128)(2,1)} %cache_ref.3, ...), custom_call_target="tpu_custom_call" | custom-call | flops 2000000000 | bytes 4000000 | tf_op jit(solution)/shard_map/down/pallas_call | solution.py:377
  4.8 0.0 copy-start
  4.8 0.0 copy-start.1
  4.9 0.0 copy-start.4
  4.9 0.0 copy-start.5
  4.9 2.8 %collective-permute-start.2 = (bf16[10,128,256]{2,1,0:T(8,128)(2,1)S(1)}, bf16[10,128,256]{2,1,0:T(8,128)(2,1)S(1)}, u32[]{:S(2)}, u32[]{:S(2)}) collective-permute-start(bf16[10,128,256]{2,1,0:T(8,128)(2,1)S(1)} %get-tuple-element.26), channel_id=1, source_target_pairs={{0,1},{1,2},{2,3},{3,4},{4,5},{5,6},{6,7},{7,8},{8,9},{9,10},{10,1... | collective-permute-start | bytes 1966088 | tf_op jit(solution)/shard_map/ppermute | solution.py:403
  7.7 17.9 %collective-permute-start.3 = (bf16[10,128,256]{2,1,0:T(8,128)(2,1)S(1)}, bf16[10,128,256]{2,1,0:T(8,128)(2,1)S(1)}, u32[]{:S(2)}, u32[]{:S(2)}) collective-permute-start(bf16[10,128,256]{2,1,0:T(8,128)(2,1)S(1)} %get-tuple-element.27), channel_id=1, source_target_pairs={{1,0},{2,1},{3,2},{4,3},{5,4},{6,5},{7,6},{8,7},{9,8},{10,9},{11,1... | collective-permute-start | bytes 1966088 | tf_op jit(solution)/shard_map/ppermute | solution.py:402
  25.6 1.0 %rim.1 = bf16[6,256,128]{2,1,0:T(8,128)(2,1)S(1)} custom-call(bf16[2,4,256,128]{3,2,1,0:T(8,128)(2,1)} %cache_ref.3, bf16[4,4,256,128]{3,2,1,0:T(8,128)(2,1)} %video_ref.3), custom_call_target="tpu_custom_call" | custom-call | tf_op jit(solution)/shard_map/rim/pallas_call | solution.py:356
  26.6 2.0 %collective-permute-start.1 = (bf16[6,256,128]{2,1,0:T(8,128)(2,1)S(1)}, bf16[6,256,128]{2,1,0:T(8,128)(2,1)S(1)}, u32[]{:S(2)}, u32[]{:S(2)}) collective-permute-start(bf16[6,256,128]{2,1,0:T(8,128)(2,1)S(1)} %rim.1), channel_id=1, source_target_pairs={{0,0},{1,2},{2,1},{3,4},{4,3},{5,6},{6,5},{7,8},{8,7},{9,10},{10,9... | collective-permute-start | bytes 1179656 | tf_op jit(solution)/shard_map/ppermute | solution.py:368
  28.6 3.8 %collective-permute-start = (bf16[6,256,128]{2,1,0:T(8,128)(2,1)S(1)}, bf16[6,256,128]{2,1,0:T(8,128)(2,1)S(1)}, u32[]{:S(2)}, u32[]{:S(2)}) collective-permute-start(bf16[6,256,128]{2,1,0:T(8,128)(2,1)S(1)} %rim.1), channel_id=1, source_target_pairs={{0,1},{1,0},{2,3},{3,2},{4,5},{5,4},{6,7},{7,6},{8,9},{9,8},{10,11... | collective-permute-start | bytes 1179656 | tf_op jit(solution)/shard_map/ppermute | solution.py:367
  32.4 3.7 %collective-permute-done.1.far_ref = bf16[6,256,128]{2,1,0:T(8,128)(2,1)S(1)} collective-permute-done((bf16[6,256,128]{2,1,0:T(8,128)(2,1)S(1)}, bf16[6,256,128]{2,1,0:T(8,128)(2,1)S(1)}, u32[]{:S(2)}, u32[]{:S(2)}) %collective-permute-start.1) | collective-permute-done | bytes 393248 | tf_op jit(solution)/shard_map/ppermute | solution.py:368
  36.0 0.0 collective-permute-done.near_ref
  36.0 0.9 %rim_down.1 = (f32[4,128,256]{2,1,0:T(8,128)S(1)}, f32[1,128]{1,0:T(1,128)S(1)}) custom-call(bf16[6,256,128]{2,1,0:T(8,128)(2,1)S(1)} %collective-permute-done.near_ref, bf16[6,256,128]{2,1,0:T(8,128)(2,1)S(1)} %collective-permute-done.1.far_ref, f32[3,256]{1,0:T(4,128)S(1)} %broadcast_in_dim.18.ends_ref, ...), custom_call_target="tpu_custom_call" | custom-call | tf_op jit(solution)/shard_map/rim_down/pallas_call | solution.py:404
  36.9 0.1 collective-permute-start.4
  37.1 1.1 %collective-permute-done.4.other_ref = f32[1,128]{1,0:T(1,128)S(1)} collective-permute-done((f32[1,128]{1,0:T(1,128)S(1)}, f32[1,128]{1,0:T(1,128)S(1)}, u32[]{:S(2)}, u32[]{:S(2)}) %collective-permute-start.4) | collective-permute-done | bytes 544 | tf_op jit(solution)/shard_map/ppermute | solution.py:312
  38.2 0.0 copy-start.2
  38.2 0.0 copy-start.3
  38.3 16.7 %all_to_all.10.stats_ref = f32[64,1,256]{2,1,0:T(1,128)S(1)} all-to-all(f32[64,1,256]{2,1,0:T(1,128)S(1)} %both.2), channel_id=1, replica_groups=mesh['groups'=2,'ha_0'=8,'ha_1'=8,'ha_2'=2] {'ha_0','ha_1'}, dimensions={0} | all-to-all | bytes 131072 | tf_op jit(solution)/shard_map/all_to_all | solution.py:321
  54.9 0.0 collective-permute-done.2.above_ref
  54.9 0.0 collective-permute-done.3.below_ref
  54.9 0.0 copy-done
  54.9 0.0 copy-done.1
  55.0 0.0 copy-done.4
  55.0 0.0 copy-done.5
  55.0 4.7 %mix.1 = (f32[4,2,128,256]{3,2,1,0:T(8,128)S(1)}, bf16[2,2,128,256]{3,2,1,0:T(8,128)(2,1)}, f32[1,128]{1,0:T(1,128)S(1)}) custom-call(f32[4,128,256]{2,1,0:T(8,128)S(1)} %get-tuple-element.18.row_ref, f32[4,128,256]{2,1,0:T(8,128)S(1)} %get-tuple-element.24.last_ref, f32[4,128,256]{2,1,0:T(8,128)S(1)} %get-tuple-element.25.share_ref, ...), custom_call_target="tpu_custom_call" | custom-call | tf_op jit(solution)/shard_map/mix/pallas_call | solution.py:328
  59.7 1.7 %collective-permute-start.5 = (f32[1,128]{1,0:T(1,128)S(1)}, f32[1,128]{1,0:T(1,128)S(1)}, u32[]{:S(2)}, u32[]{:S(2)}) collective-permute-start(f32[1,128]{1,0:T(1,128)S(1)} %get-tuple-element.30.mine_ref), channel_id=1, source_target_pairs={{0,1},{1,0},{2,3},{3,2},{4,5},{5,4},{6,7},{7,6},{8,9},{9,8},{10,11... | collective-permute-start | bytes 1544 | tf_op jit(solution)/shard_map/ppermute | solution.py:312
  61.4 0.8 %collective-permute-done.5.other_ref = f32[1,128]{1,0:T(1,128)S(1)} collective-permute-done((f32[1,128]{1,0:T(1,128)S(1)}, f32[1,128]{1,0:T(1,128)S(1)}, u32[]{:S(2)}, u32[]{:S(2)}) %collective-permute-start.5) | collective-permute-done | bytes 544 | tf_op jit(solution)/shard_map/ppermute | solution.py:312
  62.3 15.5 %all_to_all.11.stats_ref = f32[64,1,256]{2,1,0:T(1,128)S(1)} all-to-all(f32[64,1,256]{2,1,0:T(1,128)S(1)} %both.3), channel_id=1, replica_groups=mesh['groups'=2,'ha_0'=8,'ha_1'=8,'ha_2'=2] {'ha_0','ha_1'}, dimensions={0} | all-to-all | bytes 131072 | tf_op jit(solution)/shard_map/all_to_all | solution.py:321
  77.8 0.0 copy-done.3
  77.8 1.3 %final.1 = bf16[4,2,128,256]{3,2,1,0:T(8,128)(2,1)} custom-call(f32[4,2,128,256]{3,2,1,0:T(8,128)S(1)} %get-tuple-element.29.second_ref, f32[64,1,256]{2,1,0:T(1,128)S(1)} %all_to_all.11.stats_ref, f32[1,256]{1,0:T(1,128)S(1)} %bitcast.7, f32[1,256]{1,0:T(1,128)S(1)} %bitcast.8), custom_call_target="tpu_custom_call" | custom-call | tf_op jit(solution)/shard_map/final/pallas_call | solution.py:421
  (3 shorter events, 0.0 us)
Async XLA Ops:
  4.8 50.1 %copy-start = (bf16[3,3,3,256,256]{4,3,2,1,0:T(8,128)(2,1)S(1)}, bf16[3,3,3,256,256]{4,3,2,1,0:T(8,128)(2,1)}, u32[]{:S(2)}) copy-start(bf16[3,3,3,256,256]{4,3,2,1,0:T(8,128)(2,1)} %kernel_ref.2) | copy-start | bytes 10616836
  4.8 50.1 %copy-start.1 = (bf16[2,2,128,256]{3,2,1,0:T(8,128)(2,1)S(1)}, bf16[2,2,128,256]{3,2,1,0:T(8,128)(2,1)}, u32[]{:S(2)}) copy-start(bf16[2,2,128,256]{3,2,1,0:T(8,128)(2,1)} %hidden_ref.3) | copy-start | bytes 786436
  4.9 50.1 %copy-start.4 = (f32[256]{0:T(256)S(1)}, f32[256]{0:T(256)}, u32[]{:S(2)}) copy-start(f32[256]{0:T(256)} %param.13) | copy-start | bytes 3076
  4.9 50.1 %copy-start.5 = (f32[256]{0:T(256)S(1)}, f32[256]{0:T(256)}, u32[]{:S(2)}) copy-start(f32[256]{0:T(256)} %param.14) | copy-start | bytes 3076
  4.9 50.1 %collective-permute-start.2 = (bf16[10,128,256]{2,1,0:T(8,128)(2,1)S(1)}, bf16[10,128,256]{2,1,0:T(8,128)(2,1)S(1)}, u32[]{:S(2)}, u32[]{:S(2)}) collective-permute-start(bf16[10,128,256]{2,1,0:T(8,128)(2,1)S(1)} %get-tuple-element.26), channel_id=1, source_target_pairs={{0,1},{1,2},{2,3},{3,4},{4,5},{5,6},{6,7},{7,8},{8,9},{9,10},{10,1... | collective-permute-start | bytes 1966088 | tf_op jit(solution)/shard_map/ppermute | solution.py:403
  7.7 47.3 %collective-permute-start.3 = (bf16[10,128,256]{2,1,0:T(8,128)(2,1)S(1)}, bf16[10,128,256]{2,1,0:T(8,128)(2,1)S(1)}, u32[]{:S(2)}, u32[]{:S(2)}) collective-permute-start(bf16[10,128,256]{2,1,0:T(8,128)(2,1)S(1)} %get-tuple-element.27), channel_id=1, source_target_pairs={{1,0},{2,1},{3,2},{4,3},{5,4},{6,5},{7,6},{8,7},{9,8},{10,9},{11,1... | collective-permute-start | bytes 1966088 | tf_op jit(solution)/shard_map/ppermute | solution.py:402
  26.6 9.4 %collective-permute-start.1 = (bf16[6,256,128]{2,1,0:T(8,128)(2,1)S(1)}, bf16[6,256,128]{2,1,0:T(8,128)(2,1)S(1)}, u32[]{:S(2)}, u32[]{:S(2)}) collective-permute-start(bf16[6,256,128]{2,1,0:T(8,128)(2,1)S(1)} %rim.1), channel_id=1, source_target_pairs={{0,0},{1,2},{2,1},{3,4},{4,3},{5,6},{6,5},{7,8},{8,7},{9,10},{10,9... | collective-permute-start | bytes 1179656 | tf_op jit(solution)/shard_map/ppermute | solution.py:368
  28.6 7.5 %collective-permute-start = (bf16[6,256,128]{2,1,0:T(8,128)(2,1)S(1)}, bf16[6,256,128]{2,1,0:T(8,128)(2,1)S(1)}, u32[]{:S(2)}, u32[]{:S(2)}) collective-permute-start(bf16[6,256,128]{2,1,0:T(8,128)(2,1)S(1)} %rim.1), channel_id=1, source_target_pairs={{0,1},{1,0},{2,3},{3,2},{4,5},{5,4},{6,7},{7,6},{8,9},{9,8},{10,11... | collective-permute-start | bytes 1179656 | tf_op jit(solution)/shard_map/ppermute | solution.py:367
  36.9 1.3 %collective-permute-start.4 = (f32[1,128]{1,0:T(1,128)S(1)}, f32[1,128]{1,0:T(1,128)S(1)}, u32[]{:S(2)}, u32[]{:S(2)}) collective-permute-start(f32[1,128]{1,0:T(1,128)S(1)} %get-tuple-element.28.mine_ref), channel_id=1, source_target_pairs={{0,1},{1,0},{2,3},{3,2},{4,5},{5,4},{6,7},{7,6},{8,9},{9,8},{10,11... | collective-permute-start | bytes 1544 | tf_op jit(solution)/shard_map/ppermute | solution.py:312
  38.2 39.6 %copy-start.2 = (f32[256]{0:T(256)S(1)}, f32[256]{0:T(256)}, u32[]{:S(2)}) copy-start(f32[256]{0:T(256)} %param.16) | copy-start | bytes 3076
  38.2 39.6 %copy-start.3 = (f32[256]{0:T(256)S(1)}, f32[256]{0:T(256)}, u32[]{:S(2)}) copy-start(f32[256]{0:T(256)} %param.17) | copy-start | bytes 3076
  59.7 2.5 %collective-permute-start.5 = (f32[1,128]{1,0:T(1,128)S(1)}, f32[1,128]{1,0:T(1,128)S(1)}, u32[]{:S(2)}, u32[]{:S(2)}) collective-permute-start(f32[1,128]{1,0:T(1,128)S(1)} %get-tuple-element.30.mine_ref), channel_id=1, source_target_pairs={{0,1},{1,0},{2,3},{3,2},{4,5},{5,4},{6,7},{7,6},{8,9},{9,8},{10,11... | collective-permute-start | bytes 1544 | tf_op jit(solution)/shard_map/ppermute | solution.py:312

commit v9 on v8

--- a/solution.py
+++ b/solution.py
@@ -125,9 +125,9 @@
 
 
 def down_kernel(
-    cache_ref, video_ref, kernel_ref, hidden_ref,
-    row_ref, part_ref, share_ref, third_ref, center_ref, sums_ref, upper_ref, lower_ref,
-    cache_buf, video_buf, kernel_buf, pairs_ref, sems,
+    ends_ref, cache_ref, video_ref, kernel_ref, hidden_ref,
+    row_ref, part_ref, share_ref, third_ref, center_ref, sums_ref, near_ref, far_ref,
+    hidden_buf, cache_buf, video_buf, kernel_buf, pairs_ref, sems,
 ):
     frames, rows, width, c_in = video_ref.shape
     cached = cache_ref.shape[0]
@@ -138,8 +138,7 @@
         pltpu.make_async_copy(video_ref, video_buf, sems.at[1]),
         pltpu.make_async_copy(kernel_ref.at[:, :2], kernel_buf, sems.at[2]),
         pltpu.make_async_copy(kernel_ref.at[:, 2], third_ref, sems.at[3]),
-        pltpu.make_async_copy(hidden_ref.at[:, 0], upper_ref.at[:cached], sems.at[4]),
-        pltpu.make_async_copy(hidden_ref.at[:, rows // 2 - 1], lower_ref.at[:cached], sems.at[5]),
+        pltpu.make_async_copy(hidden_ref, hidden_buf, sems.at[4]),
     ]
     for c in loads:
         c.start()
@@ -154,6 +153,8 @@
     loads[2].wait()
     loads[3].wait()
 
+    odd = ends_ref[2:3]
+
     def tap(a, b, c):
         return third_ref[a, c] if b == 2 else kernel_buf[a, b, c]
 
@@ -168,9 +169,16 @@
         for t in range(frames):
             span = slice(t * half, (t + 1) * half)
             block = here[span] + shift_back(after[span])
-            target, edge_ref = (row_ref, upper_ref) if i == 0 else (part_ref, lower_ref)
-            target[t] = block
-            edge_ref[cached + t], edge_ref[cached + frames + t] = split_in_two(block)
+            if i == 0:
+                row_ref[t] = block
+            else:
+                part_ref[t] = block
+                upper = row_ref[t]
+                for edge_ref, edge in (
+                    (near_ref, jnp.where(odd > 0, upper, block)),
+                    (far_ref, jnp.where(odd > 0, block, upper)),
+                ):
+                    edge_ref[cached + t], edge_ref[cached + frames + t] = split_in_two(edge)
     shares = third_row(pairs_ref[:, 0], third_ref, frames, half, c_in)
     for t in range(frames):
         share_ref[t] = shares[t]
@@ -180,7 +188,11 @@
     sums_ref[0:1] = total - center * (frames * half)
     sums_ref[1:2] = sum(column_sum((row_ref[t] - center) ** 2) for t in range(frames))
     loads[4].wait()
-    loads[5].wait()
+    odd_bits = odd.astype(BF16)
+    for f in range(cached):
+        upper, lower = hidden_buf[f, 0], hidden_buf[f, rows // 2 - 1]
+        near_ref[f] = upper * odd_bits + lower * (1 - odd_bits)
+        far_ref[f] = lower * odd_bits + upper * (1 - odd_bits)
 
 
 def rim_down_kernel(
@@ -213,7 +225,7 @@
 
 
 def mix_kernel(
-    row_ref, last_ref, share_ref, above_ref, below_ref, ends_ref, stats_ref, gain_ref, shift_ref, hidden_ref, kernel_ref,
+    row_ref, last_ref, share_ref, near_ref, far_ref, ends_ref, stats_ref, gain_ref, shift_ref, hidden_ref, kernel_ref,
     second_ref, next_ref, message_ref,
     rows_ref, sem,
 ):
@@ -225,17 +237,22 @@
         for i in range(rows):
             rows_ref[f, 1 + i] = hidden_ref[f, i]
     keep_above, keep_below = ends_ref[0:1], ends_ref[1:2]
-    for f in range(cached):
-        rows_ref[f, 0] = above_ref[f] * keep_above.astype(BF16)
-        rows_ref[f, rows + 1] = below_ref[f] * keep_below.astype(BF16)
+    odd = ends_ref[2:3]
+    for at, keep, is_near in ((0, keep_above, odd), (rows + 1, keep_below, 1.0 - odd)):
+        near_share = (keep * is_near).astype(BF16)
+        far_share = (keep * (1.0 - is_near)).astype(BF16)
+        for f in range(cached):
+            rows_ref[f, at] = near_ref[f] * near_share + far_ref[f] * far_share
     center, factor = affine(unpack(stats_ref), count * (channels // GROUPS), gain_ref[...])
     offset = shift_ref[...]
 
     def activate(t):
-        for at, edge_ref, keep in ((0, above_ref, keep_above), (rows + 1, below_ref, keep_below)):
-            value = edge_ref[cached + t].astype(F32) + edge_ref[cached + frames + t].astype(F32)
-            if at == 0:
-                value = value + share_ref[t]
+        near, far = (
+            ref[cached + t].astype(F32) + ref[cached + frames + t].astype(F32) for ref in (near_ref, far_ref)
+        )
+        above = jnp.where(odd > 0, near, far) + share_ref[t]
+        below = jnp.where(odd > 0, far, near)
+        for at, value, keep in ((0, above, keep_above), (rows + 1, below, keep_below)):
             hidden = silu_norm(value, center, factor, offset)
             rows_ref[cached + t, at] = jnp.where(keep > 0, hidden, 0.0).astype(BF16)
         rows_ref[cached + t, 1] = silu_norm(row_ref[t], center, factor, offset).astype(BF16)
@@ -321,7 +338,7 @@
     return lax.all_to_all(copies, HA[:-1], 0, 0)
 
 
-def run_mix(row, last, share, above, below, ends, stats, gain, shift, hidden, kernel):
+def run_mix(row, last, share, near, far, ends, stats, gain, shift, hidden, kernel):
     frames, half, c_out = row.shape
     cached = hidden.shape[0]
     whole = jax.ShapeDtypeStruct
@@ -337,7 +354,7 @@
         out_specs=(AUTO, ANY, AUTO),
         scratch_shapes=[pltpu.VMEM((cached + frames, 4, half, c_out), BF16), DMA(())],
         compiler_params=limit(28),
-    )(row, last, share, above, below, ends, stats, gain, shift, hidden, kernel)
+    )(row, last, share, near, far, ends, stats, gain, shift, hidden, kernel)
 
 
 def local(video, cache_video, cache_hidden, kernel_down, gain_down, shift_down, kernel_mix, gain_mix, shift_mix):
@@ -350,8 +367,6 @@
     )
     devices = lax.axis_size(HA)
     place = lax.axis_index(HA)
-    up = [((i + 1) % devices, i) for i in range(devices)]
-    down = [(i, (i + 1) % devices) for i in range(devices)]
     whole = jax.ShapeDtypeStruct
     rim = pl.pallas_call(
         rim_kernel,
@@ -374,7 +389,7 @@
     line = whole((frames, half, c_out), F32)
     edge = whole((cached + 2 * frames, half, c_out), BF16)
     message = whole((1, LANES), F32)
-    row, part, share, third, center, sums, below, above = pl.pallas_call(
+    row, part, share, third, center, sums, near_edge, far_edge = pl.pallas_call(
         down_kernel,
         name="down",
         out_shape=(
@@ -387,20 +402,21 @@
             edge,
             edge,
         ),
-        in_specs=[HBM] * 4,
+        in_specs=[AUTO] + [HBM] * 4,
         out_specs=(AUTO,) * 8,
         scratch_shapes=[
+            pltpu.VMEM(cache_hidden.shape, BF16),
             pltpu.VMEM(cache_video.shape, BF16),
             pltpu.VMEM(video.shape, BF16),
             pltpu.VMEM((3, 2, 3, c_in, c_out), BF16),
             pltpu.VMEM((cached + frames, rows, half, 2 * c_in), BF16),
-            DMA((6,)),
+            DMA((5,)),
         ],
         compiler_params=limit(24),
         cost_estimate=pl.CostEstimate(flops=2 * 10**9, bytes_accessed=4 * 10**6, transcendentals=0),
-    )(cache_video, video, kernel_down, stored_hidden)
-    below = lax.ppermute(below, HA, up)
-    above = lax.ppermute(above, HA, down)
+    )(ends, cache_video, video, kernel_down, stored_hidden)
+    far_edge = lax.ppermute(far_edge, HA, bridges)
+    near_edge = lax.ppermute(near_edge, HA, pairs)
     last, stats = pl.pallas_call(
         rim_down_kernel,
         name="rim_down",
@@ -415,7 +431,7 @@
     )(near_rim, far_rim, ends, third, part, center, sums)
     stats = everyone(stats)
     second, next_cache, stats = run_mix(
-        row, last, share, above, below, ends, stats, gain_down[None], shift_down[None], cache_hidden, kernel_mix
+        row, last, share, near_edge, far_edge, ends, stats, gain_down[None], shift_down[None], cache_hidden, kernel_mix
     )
     stats = everyone(stats)
     encoded = pl.pallas_call(

time: 79.5 us -> 83.8 us (1.054)
  waiting for transfers between devices: 5.64 us -> 11.3 us
  blocking collectives: 32.2 us -> 31.1 us
    ppermute x1, waiting for transfers between devices: 3.68 us -> 9.3 us  [local(): far_rim = lax.ppermute(rim, HA, bridges)]
    ppermute x1, starting transfers between devices: 3.78 us -> 0.14 us  [local(): near_rim = lax.ppermute(rim, HA, pairs)]
    ppermute x2, starting transfers between devices: 20.7 us -> 22.5 us  [the longest x1 20.5 us: local(): near_edge = lax.ppermute(near_edge, HA, pairs)]
    ppermute x1, starting transfers between devices: 1.95 us -> 3.67 us  [local(): far_rim = lax.ppermute(rim, HA, bridges)]
    all_to_all x2, blocking collectives: 32.2 us -> 31.1 us  [everyone(): return lax.all_to_all(copies, HA[:-1], 0, 0)]
where the time goes in v9:
time: 83.8 us; the launch traced here: 83.5 us
  blocking collectives  31.1 us (37%)
  starting transfers between devices  27.9 us (33%)
  Pallas kernels  12.2 us (15%)
  waiting for transfers between devices  11.3 us (13%)
    all_to_all x2, blocking collectives, everyone(): return lax.all_to_all(copies, HA[:-1], 0, 0)  31.1 us
    ppermute x1, starting transfers between devices, local(): near_edge = lax.ppermute(near_edge, HA, pairs)  20.5 us
    ppermute x1, waiting for transfers between devices, local(): far_rim = lax.ppermute(rim, HA, bridges)  9.3 us
    pallas_call x1, Pallas kernels, run_mix(): pl.pallas_call(mix_kernel, name='mix', out_shape=(whole((frames, 2, half,...  4.78 us
    pallas_call x1, Pallas kernels, local(): pl.pallas_call(down_kernel, name='down', out_shape=(line, line, line, who...  4.12 us
    ppermute x1, starting transfers between devices, local(): far_rim = lax.ppermute(rim, HA, bridges)  3.67 us
    ppermute x2, waiting for transfers between devices, everyone(): other = lax.ppermute(message, HA, [(i, i ^ 1) for i in range(devices)])  1.95 us
    ppermute x1, starting transfers between devices, local(): far_edge = lax.ppermute(far_edge, HA, bridges)  1.94 us
  transfers between devices with their start and end apart: 6, of which 3 were waited for; matrix products, arithmetic and copies ran while one was open for 0% of the time, Pallas kernels for 2%

profile of v9, /device:TPU:513, one launch (start us, length us, event | category | flops | bytes accessed | tf_op | source)
XLA Modules:
  0.0 83.5 jit_solution(3487537837709719398)
XLA Ops:
  0.6 0.1 add_convert_fusion
  0.7 0.1 broadcast_in_dim.18.ends_ref
  0.8 4.1 %down.1 = (f32[4,128,256]{2,1,0:T(8,128)S(1)}, f32[4,128,256]{2,1,0:T(8,128)S(1)}, f32[4,128,256]{2,1,0:T(8,128)S(1)}, bf16[3,3,128,256]{3,2,1,0:T(8,128)(2,1)S(...) custom-call(f32[3,256]{1,0:T(4,128)S(1)} %broadcast_in_dim.18.ends_r, ...), custom_call_target="tpu_custom_call" | custom-call | flops 2000000000 | bytes 4000000 | tf_op jit(solution)/shard_map/down/pallas_call | solution.py:392
  4.9 0.0 copy-start
  4.9 0.0 copy-start.1
  4.9 0.0 copy-start.4
  5.0 0.0 copy-start.5
  5.0 20.5 %collective-permute-start.2 = (bf16[10,128,256]{2,1,0:T(8,128)(2,1)S(1)}, bf16[10,128,256]{2,1,0:T(8,128)(2,1)S(1)}, u32[]{:S(2)}, u32[]{:S(2)}) collective-permute-start(bf16[10,128,256]{2,1,0:T(8,128)(2,1)S(1)} %get-tuple-element.26), channel_id=1, source_target_pairs={{0,1},{1,0},{2,3},{3,2},{4,5},{5,4},{6,7},{7,6},{8,9},{9,8},{10,11... | collective-permute-start | bytes 1966088 | tf_op jit(solution)/shard_map/ppermute | solution.py:419
  25.5 1.9 %collective-permute-start.3 = (bf16[10,128,256]{2,1,0:T(8,128)(2,1)S(1)}, bf16[10,128,256]{2,1,0:T(8,128)(2,1)S(1)}, u32[]{:S(2)}, u32[]{:S(2)}) collective-permute-start(bf16[10,128,256]{2,1,0:T(8,128)(2,1)S(1)} %get-tuple-element.27), channel_id=1, source_target_pairs={{0,0},{1,2},{2,1},{3,4},{4,3},{5,6},{6,5},{7,8},{8,7},{9,10},{10,9... | collective-permute-start | bytes 1966088 | tf_op jit(solution)/shard_map/ppermute | solution.py:418
  27.5 1.1 %rim.1 = bf16[6,256,128]{2,1,0:T(8,128)(2,1)S(1)} custom-call(bf16[2,4,256,128]{3,2,1,0:T(8,128)(2,1)} %cache_ref.3, bf16[4,4,256,128]{3,2,1,0:T(8,128)(2,1)} %video_ref.3), custom_call_target="tpu_custom_call" | custom-call | tf_op jit(solution)/shard_map/rim/pallas_call | solution.py:371
  28.5 3.7 %collective-permute-start.1 = (bf16[6,256,128]{2,1,0:T(8,128)(2,1)S(1)}, bf16[6,256,128]{2,1,0:T(8,128)(2,1)S(1)}, u32[]{:S(2)}, u32[]{:S(2)}) collective-permute-start(bf16[6,256,128]{2,1,0:T(8,128)(2,1)S(1)} %rim.1), channel_id=1, source_target_pairs={{0,0},{1,2},{2,1},{3,4},{4,3},{5,6},{6,5},{7,8},{8,7},{9,10},{10,9... | collective-permute-start | bytes 1179656 | tf_op jit(solution)/shard_map/ppermute | solution.py:383
  32.2 0.1 collective-permute-start
  32.3 9.3 %collective-permute-done.1.far_ref = bf16[6,256,128]{2,1,0:T(8,128)(2,1)S(1)} collective-permute-done((bf16[6,256,128]{2,1,0:T(8,128)(2,1)S(1)}, bf16[6,256,128]{2,1,0:T(8,128)(2,1)S(1)}, u32[]{:S(2)}, u32[]{:S(2)}) %collective-permute-start.1) | collective-permute-done | bytes 393248 | tf_op jit(solution)/shard_map/ppermute | solution.py:383
  41.6 0.0 collective-permute-done.near_ref
  41.6 0.9 %rim_down.1 = (f32[4,128,256]{2,1,0:T(8,128)S(1)}, f32[1,128]{1,0:T(1,128)S(1)}) custom-call(bf16[6,256,128]{2,1,0:T(8,128)(2,1)S(1)} %collective-permute-done.near_ref, bf16[6,256,128]{2,1,0:T(8,128)(2,1)S(1)} %collective-permute-done.1.far_ref, f32[3,256]{1,0:T(4,128)S(1)} %broadcast_in_dim.18.ends_ref, ...), custom_call_target="tpu_custom_call" | custom-call | tf_op jit(solution)/shard_map/rim_down/pallas_call | solution.py:420
  42.5 0.1 collective-permute-start.4
  42.7 1.1 %collective-permute-done.4.other_ref = f32[1,128]{1,0:T(1,128)S(1)} collective-permute-done((f32[1,128]{1,0:T(1,128)S(1)}, f32[1,128]{1,0:T(1,128)S(1)}, u32[]{:S(2)}, u32[]{:S(2)}) %collective-permute-start.4) | collective-permute-done | bytes 544 | tf_op jit(solution)/shard_map/ppermute | solution.py:329
  43.9 0.0 copy-start.2
  43.9 0.0 copy-start.3
  43.9 15.6 %all_to_all.10.stats_ref = f32[64,1,256]{2,1,0:T(1,128)S(1)} all-to-all(f32[64,1,256]{2,1,0:T(1,128)S(1)} %both.2), channel_id=1, replica_groups=mesh['groups'=2,'ha_0'=8,'ha_1'=8,'ha_2'=2] {'ha_0','ha_1'}, dimensions={0} | all-to-all | bytes 131072 | tf_op jit(solution)/shard_map/all_to_all | solution.py:338
  59.5 0.0 collective-permute-done.2.near_ref
  59.5 0.0 collective-permute-done.3.far_ref
  59.5 0.0 copy-done
  59.5 0.0 copy-done.1
  59.5 0.0 copy-done.4
  59.5 0.0 copy-done.5
  59.5 4.8 %mix.1 = (f32[4,2,128,256]{3,2,1,0:T(8,128)S(1)}, bf16[2,2,128,256]{3,2,1,0:T(8,128)(2,1)}, f32[1,128]{1,0:T(1,128)S(1)}) custom-call(f32[4,128,256]{2,1,0:T(8,128)S(1)} %get-tuple-element.19.row_ref, f32[4,128,256]{2,1,0:T(8,128)S(1)} %get-tuple-element.24.last_ref, f32[4,128,256]{2,1,0:T(8,128)S(1)} %get-tuple-element.25.share_ref, ...), custom_call_target="tpu_custom_call" | custom-call | tf_op jit(solution)/shard_map/mix/pallas_call | solution.py:345
  64.3 1.5 %collective-permute-start.5 = (f32[1,128]{1,0:T(1,128)S(1)}, f32[1,128]{1,0:T(1,128)S(1)}, u32[]{:S(2)}, u32[]{:S(2)}) collective-permute-start(f32[1,128]{1,0:T(1,128)S(1)} %get-tuple-element.30.mine_ref), channel_id=1, source_target_pairs={{0,1},{1,0},{2,3},{3,2},{4,5},{5,4},{6,7},{7,6},{8,9},{9,8},{10,11... | collective-permute-start | bytes 1544 | tf_op jit(solution)/shard_map/ppermute | solution.py:329
  65.8 0.8 collective-permute-done.5.other_ref
  66.6 15.5 %all_to_all.11.stats_ref = f32[64,1,256]{2,1,0:T(1,128)S(1)} all-to-all(f32[64,1,256]{2,1,0:T(1,128)S(1)} %both.3), channel_id=1, replica_groups=mesh['groups'=2,'ha_0'=8,'ha_1'=8,'ha_2'=2] {'ha_0','ha_1'}, dimensions={0} | all-to-all | bytes 131072 | tf_op jit(solution)/shard_map/all_to_all | solution.py:338
  82.2 0.0 copy-done.2
  82.2 1.3 %final.1 = bf16[4,2,128,256]{3,2,1,0:T(8,128)(2,1)} custom-call(f32[4,2,128,256]{3,2,1,0:T(8,128)S(1)} %get-tuple-element.29.second_ref, f32[64,1,256]{2,1,0:T(1,128)S(1)} %all_to_all.11.stats_ref, f32[1,256]{1,0:T(1,128)S(1)} %bitcast.7, f32[1,256]{1,0:T(1,128)S(1)} %bitcast.8), custom_call_target="tpu_custom_call" | custom-call | tf_op jit(solution)/shard_map/final/pallas_call | solution.py:437
  (3 shorter events, 0.0 us)
Async XLA Ops:
  4.9 54.5 %copy-start = (bf16[3,3,3,256,256]{4,3,2,1,0:T(8,128)(2,1)S(1)}, bf16[3,3,3,256,256]{4,3,2,1,0:T(8,128)(2,1)}, u32[]{:S(2)}) copy-start(bf16[3,3,3,256,256]{4,3,2,1,0:T(8,128)(2,1)} %kernel_ref.2) | copy-start | bytes 10616836
  4.9 54.5 %copy-start.1 = (bf16[2,2,128,256]{3,2,1,0:T(8,128)(2,1)S(1)}, bf16[2,2,128,256]{3,2,1,0:T(8,128)(2,1)}, u32[]{:S(2)}) copy-start(bf16[2,2,128,256]{3,2,1,0:T(8,128)(2,1)} %hidden_ref.3) | copy-start | bytes 786436
  4.9 54.5 %copy-start.4 = (f32[256]{0:T(256)S(1)}, f32[256]{0:T(256)}, u32[]{:S(2)}) copy-start(f32[256]{0:T(256)} %param.13) | copy-start | bytes 3076
  5.0 54.5 %copy-start.5 = (f32[256]{0:T(256)S(1)}, f32[256]{0:T(256)}, u32[]{:S(2)}) copy-start(f32[256]{0:T(256)} %param.14) | copy-start | bytes 3076
  5.0 54.5 %collective-permute-start.2 = (bf16[10,128,256]{2,1,0:T(8,128)(2,1)S(1)}, bf16[10,128,256]{2,1,0:T(8,128)(2,1)S(1)}, u32[]{:S(2)}, u32[]{:S(2)}) collective-permute-start(bf16[10,128,256]{2,1,0:T(8,128)(2,1)S(1)} %get-tuple-element.26), channel_id=1, source_target_pairs={{0,1},{1,0},{2,3},{3,2},{4,5},{5,4},{6,7},{7,6},{8,9},{9,8},{10,11... | collective-permute-start | bytes 1966088 | tf_op jit(solution)/shard_map/ppermute | solution.py:419
  25.5 34.0 %collective-permute-start.3 = (bf16[10,128,256]{2,1,0:T(8,128)(2,1)S(1)}, bf16[10,128,256]{2,1,0:T(8,128)(2,1)S(1)}, u32[]{:S(2)}, u32[]{:S(2)}) collective-permute-start(bf16[10,128,256]{2,1,0:T(8,128)(2,1)S(1)} %get-tuple-element.27), channel_id=1, source_target_pairs={{0,0},{1,2},{2,1},{3,4},{4,3},{5,6},{6,5},{7,8},{8,7},{9,10},{10,9... | collective-permute-start | bytes 1966088 | tf_op jit(solution)/shard_map/ppermute | solution.py:418
  28.5 13.1 %collective-permute-start.1 = (bf16[6,256,128]{2,1,0:T(8,128)(2,1)S(1)}, bf16[6,256,128]{2,1,0:T(8,128)(2,1)S(1)}, u32[]{:S(2)}, u32[]{:S(2)}) collective-permute-start(bf16[6,256,128]{2,1,0:T(8,128)(2,1)S(1)} %rim.1), channel_id=1, source_target_pairs={{0,0},{1,2},{2,1},{3,4},{4,3},{5,6},{6,5},{7,8},{8,7},{9,10},{10,9... | collective-permute-start | bytes 1179656 | tf_op jit(solution)/shard_map/ppermute | solution.py:383
  32.2 9.5 %collective-permute-start = (bf16[6,256,128]{2,1,0:T(8,128)(2,1)S(1)}, bf16[6,256,128]{2,1,0:T(8,128)(2,1)S(1)}, u32[]{:S(2)}, u32[]{:S(2)}) collective-permute-start(bf16[6,256,128]{2,1,0:T(8,128)(2,1)S(1)} %rim.1), channel_id=1, source_target_pairs={{0,1},{1,0},{2,3},{3,2},{4,5},{5,4},{6,7},{7,6},{8,9},{9,8},{10,11... | collective-permute-start | bytes 1179656 | tf_op jit(solution)/shard_map/ppermute | solution.py:382
  42.5 1.3 %collective-permute-start.4 = (f32[1,128]{1,0:T(1,128)S(1)}, f32[1,128]{1,0:T(1,128)S(1)}, u32[]{:S(2)}, u32[]{:S(2)}) collective-permute-start(f32[1,128]{1,0:T(1,128)S(1)} %get-tuple-element.28.mine_ref), channel_id=1, source_target_pairs={{0,1},{1,0},{2,3},{3,2},{4,5},{5,4},{6,7},{7,6},{8,9},{9,8},{10,11... | collective-permute-start | bytes 1544 | tf_op jit(solution)/shard_map/ppermute | solution.py:329
  43.9 38.3 %copy-start.2 = (f32[256]{0:T(256)S(1)}, f32[256]{0:T(256)}, u32[]{:S(2)}) copy-start(f32[256]{0:T(256)} %param.16) | copy-start | bytes 3076
  43.9 38.3 %copy-start.3 = (f32[256]{0:T(256)S(1)}, f32[256]{0:T(256)}, u32[]{:S(2)}) copy-start(f32[256]{0:T(256)} %param.17) | copy-start | bytes 3076
  64.3 2.3 %collective-permute-start.5 = (f32[1,128]{1,0:T(1,128)S(1)}, f32[1,128]{1,0:T(1,128)S(1)}, u32[]{:S(2)}, u32[]{:S(2)}) collective-permute-start(f32[1,128]{1,0:T(1,128)S(1)} %get-tuple-element.30.mine_ref), channel_id=1, source_target_pairs={{0,1},{1,0},{2,3},{3,2},{4,5},{5,4},{6,7},{7,6},{8,9},{9,8},{10,11... | collective-permute-start | bytes 1544 | tf_op jit(solution)/shard_map/ppermute | solution.py:329

commit v10 on v7

--- a/solution.py
+++ b/solution.py
@@ -90,7 +90,7 @@
     return jnp.where(place == 0, 0.0, pltpu.roll(x, 1, 0))
 
 
-def rim_kernel(cache_ref, video_ref, out_ref, sems):
+def rim_kernel(cache_ref, video_ref, out_ref, ends_ref, sems):
     cached = cache_ref.shape[0]
     copies = []
     for f in range(out_ref.shape[0]):
@@ -98,6 +98,10 @@
         copies.append(pltpu.make_async_copy(source, out_ref.at[f], sems.at[f]))
     for c in copies:
         c.start()
+    place = lax.axis_index(HA)
+    flags = (place > 0, place < lax.axis_size(HA) - 1, place % 2 > 0)
+    for n, flag in enumerate(flags):
+        ends_ref[n : n + 1] = jnp.full((1, ends_ref.shape[1]), jnp.where(flag, 1.0, 0.0), F32)
     for c in copies:
         c.wait()
 
@@ -129,11 +133,13 @@
         pltpu.make_async_copy(kernel_ref.at[:, 2], third_ref, sems.at[3]),
         pltpu.make_async_copy(hidden_ref.at[:, 0], edge_ref.at[:cached], sems.at[4]),
     ]
-    for c in loads:
-        c.start()
+    loads[0].start()
+    loads[1].start()
     for f in range(cached + frames):
         if f == 0:
             loads[0].wait()
+            for c in loads[2:]:
+                c.start()
         if f == cached:
             loads[1].wait()
         for r in range(rows):
@@ -343,16 +349,15 @@
         pltpu.with_memory_space_constraint(x, pltpu.HBM) for x in (video, cache_video, cache_hidden)
     )
     devices = lax.axis_size(HA)
-    place = lax.axis_index(HA)
     up = [((i + 1) % devices, i) for i in range(devices)]
     down = [(i, (i + 1) % devices) for i in range(devices)]
     whole = jax.ShapeDtypeStruct
-    rim = pl.pallas_call(
+    rim, ends = pl.pallas_call(
         rim_kernel,
         name="rim",
-        out_shape=whole((cached + frames, width, c_in), BF16),
+        out_shape=(whole((cached + frames, width, c_in), BF16), whole((3, c_out), F32)),
         in_specs=[HBM] * 2,
-        out_specs=AUTO,
+        out_specs=(AUTO,) * 2,
         scratch_shapes=[DMA((cached + frames,))],
         compiler_params=limit(4),
     )(cache_video, video)
@@ -360,10 +365,6 @@
     bridges = [(i, min(max(i + (1 if i % 2 else -1), 0), devices - 1)) for i in range(devices)]
     near_rim = lax.ppermute(rim, HA, pairs)
     far_rim = lax.ppermute(rim, HA, bridges)
-    ends = jnp.broadcast_to(
-        jnp.stack([place > 0, place < devices - 1, place % 2 > 0]).astype(F32)[:, None], (3, c_out)
-    )
-    kernel_down, ends = lax.optimization_barrier((kernel_down, ends))
     kernel_down = pltpu.with_memory_space_constraint(kernel_down, pltpu.HBM)
     line = whole((frames, half, c_out), F32)
     edge = whole((cached + 2 * frames, half, c_out), BF16)
@@ -389,7 +390,6 @@
             DMA((5,)),
         ],
         compiler_params=limit(24),
-        cost_estimate=pl.CostEstimate(flops=2 * 10**9, bytes_accessed=4 * 10**6, transcendentals=0),
     )(cache_video, video, kernel_down, stored_hidden)
     below = lax.ppermute(below, HA, up)
     last, above, stats = pl.pallas_call(

time: 72.2 us -> 72.8 us (level)
  no operation moved by 1% of the time
where the time goes in v10:
time: 72.8 us; the launch traced here: 72.6 us
  blocking collectives  32.2 us (44%)
  starting transfers between devices  25 us (34%)
  Pallas kernels  12.6 us (17%)
  waiting for transfers between devices  1.99 us (3%)
  between operations  0.77 us (1%)
    all_to_all x2, blocking collectives, everyone(): return lax.all_to_all(copies, HA[:-1], 0, 0)  32.2 us
    ppermute x1, starting transfers between devices, local(): near_rim = lax.ppermute(rim, HA, pairs)  16.6 us
    pallas_call x1, Pallas kernels, run_mix(): pl.pallas_call(mix_kernel, name='mix', out_shape=(whole((frames, 2, half,...  4.74 us
    ppermute x1, starting transfers between devices, local(): far_rim = lax.ppermute(rim, HA, bridges)  4.73 us
    pallas_call x1, Pallas kernels, local(): pl.pallas_call(down_kernel, name='down', out_shape=(line, line, whole((3,...  4.33 us
    ppermute x2, waiting for transfers between devices, everyone(): other = lax.ppermute(message, HA, [(i, i ^ 1) for i in range(devices)])  1.98 us
    ppermute x1, starting transfers between devices, local(): above = lax.ppermute(above, HA, down)  1.81 us
    ppermute x2, starting transfers between devices, everyone(): other = lax.ppermute(message, HA, [(i, i ^ 1) for i in range(devices)])  1.72 us
  transfers between devices with their start and end apart: 6, of which 2 were waited for; matrix products, arithmetic and copies ran while one was open for 0% of the time, Pallas kernels for 7%

profile of v10, /device:TPU:513, one launch (start us, length us, event | category | flops | bytes accessed | tf_op | source)
XLA Modules:
  0.0 72.6 jit_solution(14426875678832228788)
XLA Ops:
  0.6 0.0 copy-start.1
  0.6 0.0 copy-start
  0.7 0.0 copy-start.3
  0.7 0.0 copy-start.2
  0.7 1.2 %rim.1 = (bf16[6,256,128]{2,1,0:T(8,128)(2,1)S(1)}, f32[3,256]{1,0:T(4,128)S(1)}) custom-call(bf16[2,4,256,128]{3,2,1,0:T(8,128)(2,1)} %cache_ref.3, bf16[4,4,256,128]{3,2,1,0:T(8,128)(2,1)} %video_ref.3), custom_call_target="tpu_custom_call" | custom-call | tf_op jit(solution)/shard_map/rim/pallas_call | solution.py:355
  1.9 4.7 %collective-permute-start.1 = (bf16[6,256,128]{2,1,0:T(8,128)(2,1)S(1)}, bf16[6,256,128]{2,1,0:T(8,128)(2,1)S(1)}, u32[]{:S(2)}, u32[]{:S(2)}) collective-permute-start(bf16[6,256,128]{2,1,0:T(8,128)(2,1)S(1)} %get-tuple-element.17), channel_id=1, source_target_pairs={{0,0},{1,2},{2,1},{3,4},{4,3},{5,6},{6,5},{7,8},{8,7},{9,10},{10,9... | collective-permute-start | bytes 1179656 | tf_op jit(solution)/shard_map/ppermute | solution.py:367
  6.6 16.6 %collective-permute-start = (bf16[6,256,128]{2,1,0:T(8,128)(2,1)S(1)}, bf16[6,256,128]{2,1,0:T(8,128)(2,1)S(1)}, u32[]{:S(2)}, u32[]{:S(2)}) collective-permute-start(bf16[6,256,128]{2,1,0:T(8,128)(2,1)S(1)} %get-tuple-element.17), channel_id=1, source_target_pairs={{0,1},{1,0},{2,3},{3,2},{4,5},{5,4},{6,7},{7,6},{8,9},{9,8},{10,11... | collective-permute-start | bytes 1179656 | tf_op jit(solution)/shard_map/ppermute | solution.py:366
  23.2 4.3 %down.1 = (f32[4,128,256]{2,1,0:T(8,128)S(1)}, f32[4,128,256]{2,1,0:T(8,128)S(1)}, bf16[3,3,128,256]{3,2,1,0:T(8,128)(2,1)S(1)}, f32[1,256]{1,0:T(1,128)S(1)}, f...) custom-call(bf16[2,4,256,128]{3,2,1,0:T(8,128)(2,1)} %cache_ref.3, bf16[4,4,256,128]{3,2,1,0:T(8,128)(2,1)} %video_ref.3, ...), custom_call_target="tpu_custom_call" | custom-call | tf_op jit(solution)/shard_map/down/pallas_call | solution.py:372
  27.6 0.1 collective-permute-start.3
  27.7 0.0 collective-permute-done.1.far_ref
  27.7 0.0 collective-permute-done.near_ref
  27.7 0.0 copy-done.1
  27.8 0.9 %rim_down.1 = (f32[4,128,256]{2,1,0:T(8,128)S(1)}, bf16[10,128,256]{2,1,0:T(8,128)(2,1)S(1)}, f32[1,128]{1,0:T(1,128)S(1)}) custom-call(bf16[6,256,128]{2,1,0:T(8,128)(2,1)S(1)} %collective-permute-done.near_ref, bf16[6,256,128]{2,1,0:T(8,128)(2,1)S(1)} %collective-permute-done.1.far_ref, f32[3,256]{1,0:T(4,128)S(1)} %get-tuple-element.18.ends_ref, ...), custom_call_target="tpu_custom_call" | custom-call | tf_op jit(solution)/shard_map/rim_down/pallas_call | solution.py:395
  28.7 0.0 copy-start.4
  28.7 0.0 copy-start.5
  28.7 1.8 %collective-permute-start.2 = (bf16[10,128,256]{2,1,0:T(8,128)(2,1)S(1)}, bf16[10,128,256]{2,1,0:T(8,128)(2,1)S(1)}, u32[]{:S(2)}, u32[]{:S(2)}) collective-permute-start(bf16[10,128,256]{2,1,0:T(8,128)(2,1)S(1)} %get-tuple-element.24), channel_id=1, source_target_pairs={{0,1},{1,2},{2,3},{3,4},{4,5},{5,6},{6,7},{7,8},{8,9},{9,10},{10,1... | collective-permute-start | bytes 1966088 | tf_op jit(solution)/shard_map/ppermute | solution.py:407
  30.5 0.0 collective-permute-start.4
  30.5 1.2 %collective-permute-done.4.other_ref = f32[1,128]{1,0:T(1,128)S(1)} collective-permute-done((f32[1,128]{1,0:T(1,128)S(1)}, f32[1,128]{1,0:T(1,128)S(1)}, u32[]{:S(2)}, u32[]{:S(2)}) %collective-permute-start.4) | collective-permute-done | bytes 544 | tf_op jit(solution)/shard_map/ppermute | solution.py:312
  31.7 16.6 %all_to_all.10.stats_ref = f32[64,1,256]{2,1,0:T(1,128)S(1)} all-to-all(f32[64,1,256]{2,1,0:T(1,128)S(1)} %both.2), channel_id=1, replica_groups=mesh['groups'=2,'ha_0'=8,'ha_1'=8,'ha_2'=2] {'ha_0','ha_1'}, dimensions={0} | all-to-all | bytes 131072 | tf_op jit(solution)/shard_map/all_to_all | solution.py:321
  48.3 0.0 collective-permute-done.3.below_ref
  48.4 0.0 collective-permute-done.2.above_ref
  48.4 0.0 copy-done
  48.4 0.0 copy-done.3
  48.4 0.0 copy-done.2
  48.4 4.7 %mix.1 = (f32[4,2,128,256]{3,2,1,0:T(8,128)S(1)}, bf16[2,2,128,256]{3,2,1,0:T(8,128)(2,1)}, f32[1,128]{1,0:T(1,128)S(1)}) custom-call(f32[4,128,256]{2,1,0:T(8,128)S(1)} %get-tuple-element.16.row_ref, f32[4,128,256]{2,1,0:T(8,128)S(1)} %get-tuple-element.23.last_ref, bf16[10,128,256]{2,1,0:T(8,128)(2,1)S(1)} %collective-permute-done.2.above_ref, ...), custom_call_target="tpu_custom_call" | custom-call | tf_op jit(solution)/shard_map/mix/pallas_call | solution.py:328
  53.1 1.7 %collective-permute-start.5 = (f32[1,128]{1,0:T(1,128)S(1)}, f32[1,128]{1,0:T(1,128)S(1)}, u32[]{:S(2)}, u32[]{:S(2)}) collective-permute-start(f32[1,128]{1,0:T(1,128)S(1)} %get-tuple-element.28.mine_ref), channel_id=1, source_target_pairs={{0,1},{1,0},{2,3},{3,2},{4,5},{5,4},{6,7},{7,6},{8,9},{9,8},{10,11... | collective-permute-start | bytes 1544 | tf_op jit(solution)/shard_map/ppermute | solution.py:312
  54.8 0.8 %collective-permute-done.5.other_ref = f32[1,128]{1,0:T(1,128)S(1)} collective-permute-done((f32[1,128]{1,0:T(1,128)S(1)}, f32[1,128]{1,0:T(1,128)S(1)}, u32[]{:S(2)}, u32[]{:S(2)}) %collective-permute-start.5) | collective-permute-done | bytes 544 | tf_op jit(solution)/shard_map/ppermute | solution.py:312
  55.7 15.5 %all_to_all.11.stats_ref = f32[64,1,256]{2,1,0:T(1,128)S(1)} all-to-all(f32[64,1,256]{2,1,0:T(1,128)S(1)} %both.3), channel_id=1, replica_groups=mesh['groups'=2,'ha_0'=8,'ha_1'=8,'ha_2'=2] {'ha_0','ha_1'}, dimensions={0} | all-to-all | bytes 131072 | tf_op jit(solution)/shard_map/all_to_all | solution.py:321
  71.2 0.0 copy-done.4
  71.2 0.0 copy-done.5
  71.2 1.3 %final.1 = bf16[4,2,128,256]{3,2,1,0:T(8,128)(2,1)} custom-call(f32[4,2,128,256]{3,2,1,0:T(8,128)S(1)} %get-tuple-element.27.second_ref, f32[64,1,256]{2,1,0:T(1,128)S(1)} %all_to_all.11.stats_ref, f32[1,256]{1,0:T(1,128)S(1)} %bitcast.6, f32[1,256]{1,0:T(1,128)S(1)} %bitcast.7), custom_call_target="tpu_custom_call" | custom-call | tf_op jit(solution)/shard_map/final/pallas_call | solution.py:413
  (2 shorter events, 0.0 us)
Async XLA Ops:
  0.6 27.1 %copy-start.1 = (bf16[2,2,128,256]{3,2,1,0:T(8,128)(2,1)S(1)}, bf16[2,2,128,256]{3,2,1,0:T(8,128)(2,1)}, u32[]{:S(2)}) copy-start(bf16[2,2,128,256]{3,2,1,0:T(8,128)(2,1)} %hidden_ref.5) | copy-start | bytes 786436
  0.6 47.7 %copy-start = (bf16[3,3,3,256,256]{4,3,2,1,0:T(8,128)(2,1)S(1)}, bf16[3,3,3,256,256]{4,3,2,1,0:T(8,128)(2,1)}, u32[]{:S(2)}) copy-start(bf16[3,3,3,256,256]{4,3,2,1,0:T(8,128)(2,1)} %kernel_ref.3) | copy-start | bytes 10616836
  0.7 47.7 %copy-start.3 = (f32[256]{0:T(256)S(1)}, f32[256]{0:T(256)}, u32[]{:S(2)}) copy-start(f32[256]{0:T(256)} %param.14) | copy-start | bytes 3076
  0.7 47.7 %copy-start.2 = (f32[256]{0:T(256)S(1)}, f32[256]{0:T(256)}, u32[]{:S(2)}) copy-start(f32[256]{0:T(256)} %param.13) | copy-start | bytes 3076
  1.9 25.9 %collective-permute-start.1 = (bf16[6,256,128]{2,1,0:T(8,128)(2,1)S(1)}, bf16[6,256,128]{2,1,0:T(8,128)(2,1)S(1)}, u32[]{:S(2)}, u32[]{:S(2)}) collective-permute-start(bf16[6,256,128]{2,1,0:T(8,128)(2,1)S(1)} %get-tuple-element.17), channel_id=1, source_target_pairs={{0,0},{1,2},{2,1},{3,4},{4,3},{5,6},{6,5},{7,8},{8,7},{9,10},{10,9... | collective-permute-start | bytes 1179656 | tf_op jit(solution)/shard_map/ppermute | solution.py:367
  6.6 21.1 %collective-permute-start = (bf16[6,256,128]{2,1,0:T(8,128)(2,1)S(1)}, bf16[6,256,128]{2,1,0:T(8,128)(2,1)S(1)}, u32[]{:S(2)}, u32[]{:S(2)}) collective-permute-start(bf16[6,256,128]{2,1,0:T(8,128)(2,1)S(1)} %get-tuple-element.17), channel_id=1, source_target_pairs={{0,1},{1,0},{2,3},{3,2},{4,5},{5,4},{6,7},{7,6},{8,9},{9,8},{10,11... | collective-permute-start | bytes 1179656 | tf_op jit(solution)/shard_map/ppermute | solution.py:366
  27.6 20.8 %collective-permute-start.3 = (bf16[10,128,256]{2,1,0:T(8,128)(2,1)S(1)}, bf16[10,128,256]{2,1,0:T(8,128)(2,1)S(1)}, u32[]{:S(2)}, u32[]{:S(2)}) collective-permute-start(bf16[10,128,256]{2,1,0:T(8,128)(2,1)S(1)} %get-tuple-element.25), channel_id=1, source_target_pairs={{1,0},{2,1},{3,2},{4,3},{5,4},{6,5},{7,6},{8,7},{9,8},{10,9},{11,1... | collective-permute-start | bytes 1966088 | tf_op jit(solution)/shard_map/ppermute | solution.py:394
  28.7 42.5 %copy-start.4 = (f32[256]{0:T(256)S(1)}, f32[256]{0:T(256)}, u32[]{:S(2)}) copy-start(f32[256]{0:T(256)} %param.16) | copy-start | bytes 3076
  28.7 42.5 %copy-start.5 = (f32[256]{0:T(256)S(1)}, f32[256]{0:T(256)}, u32[]{:S(2)}) copy-start(f32[256]{0:T(256)} %param.17) | copy-start | bytes 3076
  28.7 19.6 %collective-permute-start.2 = (bf16[10,128,256]{2,1,0:T(8,128)(2,1)S(1)}, bf16[10,128,256]{2,1,0:T(8,128)(2,1)S(1)}, u32[]{:S(2)}, u32[]{:S(2)}) collective-permute-start(bf16[10,128,256]{2,1,0:T(8,128)(2,1)S(1)} %get-tuple-element.24), channel_id=1, source_target_pairs={{0,1},{1,2},{2,3},{3,4},{4,5},{5,6},{6,7},{7,8},{8,9},{9,10},{10,1... | collective-permute-start | bytes 1966088 | tf_op jit(solution)/shard_map/ppermute | solution.py:407
  30.5 1.2 %collective-permute-start.4 = (f32[1,128]{1,0:T(1,128)S(1)}, f32[1,128]{1,0:T(1,128)S(1)}, u32[]{:S(2)}, u32[]{:S(2)}) collective-permute-start(f32[1,128]{1,0:T(1,128)S(1)} %get-tuple-element.26.mine_ref), channel_id=1, source_target_pairs={{0,1},{1,0},{2,3},{3,2},{4,5},{5,4},{6,7},{7,6},{8,9},{9,8},{10,11... | collective-permute-start | bytes 1544 | tf_op jit(solution)/shard_map/ppermute | solution.py:312
  53.1 2.5 %collective-permute-start.5 = (f32[1,128]{1,0:T(1,128)S(1)}, f32[1,128]{1,0:T(1,128)S(1)}, u32[]{:S(2)}, u32[]{:S(2)}) collective-permute-start(f32[1,128]{1,0:T(1,128)S(1)} %get-tuple-element.28.mine_ref), channel_id=1, source_target_pairs={{0,1},{1,0},{2,3},{3,2},{4,5},{5,4},{6,7},{7,6},{8,9},{9,8},{10,11... | collective-permute-start | bytes 1544 | tf_op jit(solution)/shard_map/ppermute | solution.py:312
